TPU v7x, 32 devices: a whole 2x2x4 slice. The times are simulated.
32 devices in a mesh: dom: 32 (over z, y, x, core).
Axes of the slice: x: 2, y: 2, z: 4, core: 2. Of those that a mesh axis runs over, the one named last changes fastest.
Arguments:
- tracer: float32 [40, 32768], P(None, 'dom'), may hold values from -6 to 6
- bottom_levels: int32 [32768], P('dom'), may hold values from 1 to 40
- neighbours: int32 [6, 32768], P(None, 'dom'), may hold values from 0 to 2048, as said below
- edge_weight: float32 [6, 32768], P(None, 'dom'), may hold values from 0.05 to 0.5
- ssh: float32 [32768], P('dom'), may hold values from -6 to 6
- velocity: float32 [32768], P('dom'), may hold values from -3 to 3
- send_blocks: int32 [32, 4, 2], P('dom'), may hold values from -1 to 7
- thickness: float32 [40], replicated, may hold values from 0.5 to 4
- profile: float32 [40], replicated, may hold values from -4 to 4
Outputs:
- tracer_out: float32 [40, 32768], P(None, 'dom')
- ssh_out: float32 [32768], P('dom')
- velocity_out: float32 [32768], P('dom')
Inputs may be any that keep to these rules, and one draw needn't show every extreme that they name: `neighbours`: entries 0 to 1023 are the partition's own cells, the next 1024 its received halo cells in the order of ext, and 2048 is land. `send_blocks`: -1 marks an empty slot; other entries are block numbers within the sending partition.
All inputs are finite; a program needn't handle non-finite values.
Results may differ from a plain program's by a relative error of at most 0.0003.
Values sent between devices are 32-bit elements; how exact they have to be, the bound alone decides.
No kernel may reach another device: no remote copies, remote signals or barrier semaphores. Data moves between devices by JAX's collectives and lax.ppermute only.
A program may use at most 64 MiB of HBM per device.

v0:
```python
import jax
import jax.numpy as jnp
from jax import lax
from jax.sharding import PartitionSpec as P

BLOCK = 128
SUBSTEPS = 6


OFFSETS = (1, -1, 2, -2)
horizontal_rate = 0.5
vertical_rate = 0.5
tracer_step = 0.2
barotropic_step = 0.5
friction = 0.05


def from_behind(value, axis, by):
    peers = lax.axis_size(axis)
    pairs = [(i, i + by) for i in range(peers) if 0 <= i + by < peers]
    return lax.ppermute(value, axis, pairs)


def outgoing(field, picked_row, filled_row):
    blocks = field.reshape(field.shape[:-1] + (-1, BLOCK))
    chosen = jnp.take(blocks, picked_row, axis=-2) * filled_row[:, None]
    return chosen.reshape(field.shape[:-1] + (-1,))


def assemble(field, received):
    padding = jnp.zeros(field.shape[:-1] + (BLOCK,), field.dtype)
    return jnp.concatenate([field] + received + [padding], axis=-1)


def tracer_halo(tracer, levels, picked, filled):
    sending = [
        (
            outgoing(tracer, picked[number], filled[number]),
            outgoing(levels, picked[number], filled[number]),
        )
        for number in range(4)
    ]
    arrived = [
        from_behind((sending[number][0], sending[number][1]), "dom", OFFSETS[number])
        for number in range(4)
    ]
    ext_tracer = assemble(tracer, [arrived[number][0] for number in range(4)])
    ext_levels = assemble(levels, [arrived[number][1] for number in range(4)])
    return (ext_tracer, ext_levels)


def ssh_halo(height, picked, filled):
    sending = [outgoing(height, picked[number], filled[number]) for number in range(4)]
    arrived = [from_behind(sending[number], "dom", OFFSETS[number]) for number in range(4)]
    return assemble(height, arrived)


def shards(
    tracer, bottom_levels, neighbours, edge_weight, ssh, velocity, send_blocks, thickness, profile
):
    level_count = tracer.shape[0]
    slots = send_blocks[0]
    picked = jnp.maximum(slots, 0)
    filled = (slots >= 0).astype(jnp.float32)
    levels_f = bottom_levels.astype(jnp.float32)
    ext_tracer, ext_levels = tracer_halo(tracer, levels_f, picked, filled)
    level_index = jnp.arange(level_count).astype(jnp.float32)[:, None]
    active = (level_index < levels_f[None, :]).astype(jnp.float32)
    horizontal = jnp.zeros_like(tracer)
    for column in range(6):
        index = neighbours[column]
        near_levels = jnp.take(ext_levels, index)
        near_active = (level_index < near_levels[None, :]).astype(jnp.float32)
        near_tracer = jnp.take(ext_tracer, index, axis=1)
        horizontal = horizontal + edge_weight[column][None, :] * near_active * (
            near_tracer - tracer
        )
    horizontal = horizontal * active
    zero_level = jnp.zeros((1, tracer.shape[1]), tracer.dtype)
    below = jnp.concatenate([active[1:] * (tracer[1:] - tracer[:-1]), zero_level], axis=0)
    above = jnp.concatenate([zero_level, active[:-1] * (tracer[:-1] - tracer[1:])], axis=0)
    vertical = active * (below + above)
    tendency = horizontal_rate * horizontal + vertical_rate * vertical
    layers = active * thickness[:, None]
    forcing = jnp.sum(layers * tracer, axis=0) / jnp.sum(layers, axis=0)

    def substep(counter, carry):
        height, speed, summed = carry
        extended = ssh_halo(height, picked, filled)
        laplace = jnp.zeros_like(height)
        for column in range(6):
            laplace = laplace + edge_weight[column] * (
                jnp.take(extended, neighbours[column]) - height
            )
        speed = (1.0 - friction) * speed + barotropic_step * (laplace + forcing)
        height = height + barotropic_step * speed
        return (height, speed, summed + speed)

    height, speed, summed = lax.fori_loop(
        0, SUBSTEPS, substep, (ssh, velocity, jnp.zeros_like(velocity))
    )
    tracer_out = (
        tracer + tracer_step * tendency + active * profile[:, None] * (summed / SUBSTEPS)[None, :]
    )
    return (tracer_out, height, speed)


def solution(mesh):
    placed = (
        P(None, "dom"),
        P("dom"),
        P(None, "dom"),
        P(None, "dom"),
        P("dom"),
        P("dom"),
        P("dom", None, None),
        P(),
        P(),
    )
    return jax.shard_map(
        shards,
        mesh=mesh,
        in_specs=placed,
        out_specs=(P(None, "dom"), P("dom"), P("dom")),
        check_vma=False,
    )
```

profile of v0, /device:TPU:9, one launch (start us, length us, event | category | flops | bytes accessed | tf_op | source)
XLA Modules:
  0.0 438.3 jit_solution(390666301282849767)
XLA Ops:
  3.9 3.7 collective-permute-start.4
  10.7 332.0 %while.15 = (s32[]{:T(128)}, f32[1024]{0:T(1024)S(1)}, f32[1024]{0:T(1024)S(1)}, f32[1024]{0:T(1024)S(1)}, f32[6,1024]{1,0:T(8,128)S(1)}, /*index=5*/s32[4,2]{1,...) while((s32[]{:T(128)}, f32[1024]{0:T(1024)S(1)}, ...), condition=%wide.region_3.8_spmd.clone, body=%wide.region_2.0_spmd.clone.sunk | while | flops 99379 | bytes 398343 | solution.py:99
  20.8 4.0 collective-permute-start.3
  25.5 6.1 %gather_fusion.4 = f32[1024]{0:T(1024)S(1)} fusion(f32[2176]{0:T(1024)S(1)} %constant_dynamic-update-slice_fusion.29, s32[1024]{0:T(1024)S(1)} %fusion.87), kind=kCustom, calls=%fused_computation.15.clone.clone.1 | custom fusion | bytes 12288 | tf_op jit(solution)/shard_map/while/body/eval_jaxpr/jit(_take)/gather | solution.py:93
  31.6 6.2 %gather_fusion.5 = f32[1024]{0:T(1024)S(1)} fusion(f32[2176]{0:T(1024)S(1)} %constant_dynamic-update-slice_fusion.29, s32[1024]{0:T(1024)S(1)} %fusion.88), kind=kCustom, calls=%fused_computation.14.clone.clone.1 | custom fusion | bytes 12288 | tf_op jit(solution)/shard_map/while/body/eval_jaxpr/jit(_take)/gather | solution.py:93
  37.8 6.2 %gather_fusion.6 = f32[1024]{0:T(1024)S(1)} fusion(f32[2176]{0:T(1024)S(1)} %constant_dynamic-update-slice_fusion.29, s32[1024]{0:T(1024)S(1)} %fusion.89), kind=kCustom, calls=%fused_computation.13.clone.clone.1 | custom fusion | bytes 12288 | tf_op jit(solution)/shard_map/while/body/eval_jaxpr/jit(_take)/gather | solution.py:93
  43.9 6.2 %gather_fusion.7 = f32[1024]{0:T(1024)S(1)} fusion(f32[2176]{0:T(1024)S(1)} %constant_dynamic-update-slice_fusion.29, s32[1024]{0:T(1024)S(1)} %fusion.90), kind=kCustom, calls=%fused_computation.12.clone.clone.1 | custom fusion | bytes 12288 | tf_op jit(solution)/shard_map/while/body/eval_jaxpr/jit(_take)/gather | solution.py:93
  50.1 6.2 %gather_fusion.8 = f32[1024]{0:T(1024)S(1)} fusion(f32[2176]{0:T(1024)S(1)} %constant_dynamic-update-slice_fusion.29, s32[1024]{0:T(1024)S(1)} %fusion.91), kind=kCustom, calls=%fused_computation.11.clone.clone.1 | custom fusion | bytes 12288 | tf_op jit(solution)/shard_map/while/body/eval_jaxpr/jit(_take)/gather | solution.py:93
  56.3 6.2 %gather_fusion.9 = f32[1024]{0:T(1024)S(1)} fusion(f32[2176]{0:T(1024)S(1)} %constant_dynamic-update-slice_fusion.29, s32[1024]{0:T(1024)S(1)} %fusion.92), kind=kCustom, calls=%fused_computation.1.clone.clone.1 | custom fusion | bytes 12288 | tf_op jit(solution)/shard_map/while/body/eval_jaxpr/jit(_take)/gather | solution.py:93
  63.2 6.0 %collective-permute-start = (f32[256]{0:T(256)S(1)}, f32[256]{0:T(256)S(1)}, u32[]{:S(2)}, u32[]{:S(2)}) collective-permute-start(f32[256]{0:T(256)S(1)} %fusion.82), channel_id=1, source_target_pairs={{0,1},{1,2},{2,3},{3,4},{4,5},{5,6},{6,7},{7,8},{8,9},{9,10},{10,1... | collective-permute-start | bytes 3080 | tf_op jit(solution)/shard_map/while/body/eval_jaxpr/ppermute | solution.py:21
  75.6 4.5 %collective-permute-start.3 = (f32[256]{0:T(256)S(1)}, f32[256]{0:T(256)S(1)}, u32[]{:S(2)}, u32[]{:S(2)}) collective-permute-start(f32[256]{0:T(256)S(1)} %fusion.85), channel_id=1, source_target_pairs={{2,0},{3,1},{4,2},{5,3},{6,4},{7,5},{8,6},{9,7},{10,8},{11,9},{12,... | collective-permute-start | bytes 3080 | tf_op jit(solution)/shard_map/while/body/eval_jaxpr/ppermute | solution.py:21
  82.0 6.1 %gather_fusion.4 = f32[1024]{0:T(1024)S(1)} fusion(f32[2176]{0:T(1024)S(1)} %constant_dynamic-update-slice_fusion.29, s32[1024]{0:T(1024)S(1)} %fusion.87), kind=kCustom, calls=%fused_computation.15.clone.clone.1 | custom fusion | bytes 12288 | tf_op jit(solution)/shard_map/while/body/eval_jaxpr/jit(_take)/gather | solution.py:93
  88.2 6.2 %gather_fusion.5 = f32[1024]{0:T(1024)S(1)} fusion(f32[2176]{0:T(1024)S(1)} %constant_dynamic-update-slice_fusion.29, s32[1024]{0:T(1024)S(1)} %fusion.88), kind=kCustom, calls=%fused_computation.14.clone.clone.1 | custom fusion | bytes 12288 | tf_op jit(solution)/shard_map/while/body/eval_jaxpr/jit(_take)/gather | solution.py:93
  94.4 6.2 %gather_fusion.6 = f32[1024]{0:T(1024)S(1)} fusion(f32[2176]{0:T(1024)S(1)} %constant_dynamic-update-slice_fusion.29, s32[1024]{0:T(1024)S(1)} %fusion.89), kind=kCustom, calls=%fused_computation.13.clone.clone.1 | custom fusion | bytes 12288 | tf_op jit(solution)/shard_map/while/body/eval_jaxpr/jit(_take)/gather | solution.py:93
  100.5 6.2 %gather_fusion.7 = f32[1024]{0:T(1024)S(1)} fusion(f32[2176]{0:T(1024)S(1)} %constant_dynamic-update-slice_fusion.29, s32[1024]{0:T(1024)S(1)} %fusion.90), kind=kCustom, calls=%fused_computation.12.clone.clone.1 | custom fusion | bytes 12288 | tf_op jit(solution)/shard_map/while/body/eval_jaxpr/jit(_take)/gather | solution.py:93
  106.7 6.2 %gather_fusion.8 = f32[1024]{0:T(1024)S(1)} fusion(f32[2176]{0:T(1024)S(1)} %constant_dynamic-update-slice_fusion.29, s32[1024]{0:T(1024)S(1)} %fusion.91), kind=kCustom, calls=%fused_computation.11.clone.clone.1 | custom fusion | bytes 12288 | tf_op jit(solution)/shard_map/while/body/eval_jaxpr/jit(_take)/gather | solution.py:93
  112.8 6.2 %gather_fusion.9 = f32[1024]{0:T(1024)S(1)} fusion(f32[2176]{0:T(1024)S(1)} %constant_dynamic-update-slice_fusion.29, s32[1024]{0:T(1024)S(1)} %fusion.92), kind=kCustom, calls=%fused_computation.1.clone.clone.1 | custom fusion | bytes 12288 | tf_op jit(solution)/shard_map/while/body/eval_jaxpr/jit(_take)/gather | solution.py:93
  119.7 4.8 %collective-permute-start = (f32[256]{0:T(256)S(1)}, f32[256]{0:T(256)S(1)}, u32[]{:S(2)}, u32[]{:S(2)}) collective-permute-start(f32[256]{0:T(256)S(1)} %fusion.82), channel_id=1, source_target_pairs={{0,1},{1,2},{2,3},{3,4},{4,5},{5,6},{6,7},{7,8},{8,9},{9,10},{10,1... | collective-permute-start | bytes 3080 | tf_op jit(solution)/shard_map/while/body/eval_jaxpr/ppermute | solution.py:21
  127.7 3.6 collective-permute-start.2
  138.0 6.1 %gather_fusion.4 = f32[1024]{0:T(1024)S(1)} fusion(f32[2176]{0:T(1024)S(1)} %constant_dynamic-update-slice_fusion.29, s32[1024]{0:T(1024)S(1)} %fusion.87), kind=kCustom, calls=%fused_computation.15.clone.clone.1 | custom fusion | bytes 12288 | tf_op jit(solution)/shard_map/while/body/eval_jaxpr/jit(_take)/gather | solution.py:93
  144.1 6.2 %gather_fusion.5 = f32[1024]{0:T(1024)S(1)} fusion(f32[2176]{0:T(1024)S(1)} %constant_dynamic-update-slice_fusion.29, s32[1024]{0:T(1024)S(1)} %fusion.88), kind=kCustom, calls=%fused_computation.14.clone.clone.1 | custom fusion | bytes 12288 | tf_op jit(solution)/shard_map/while/body/eval_jaxpr/jit(_take)/gather | solution.py:93
  150.3 6.2 %gather_fusion.6 = f32[1024]{0:T(1024)S(1)} fusion(f32[2176]{0:T(1024)S(1)} %constant_dynamic-update-slice_fusion.29, s32[1024]{0:T(1024)S(1)} %fusion.89), kind=kCustom, calls=%fused_computation.13.clone.clone.1 | custom fusion | bytes 12288 | tf_op jit(solution)/shard_map/while/body/eval_jaxpr/jit(_take)/gather | solution.py:93
  156.4 6.2 %gather_fusion.7 = f32[1024]{0:T(1024)S(1)} fusion(f32[2176]{0:T(1024)S(1)} %constant_dynamic-update-slice_fusion.29, s32[1024]{0:T(1024)S(1)} %fusion.90), kind=kCustom, calls=%fused_computation.12.clone.clone.1 | custom fusion | bytes 12288 | tf_op jit(solution)/shard_map/while/body/eval_jaxpr/jit(_take)/gather | solution.py:93
  162.6 6.2 %gather_fusion.8 = f32[1024]{0:T(1024)S(1)} fusion(f32[2176]{0:T(1024)S(1)} %constant_dynamic-update-slice_fusion.29, s32[1024]{0:T(1024)S(1)} %fusion.91), kind=kCustom, calls=%fused_computation.11.clone.clone.1 | custom fusion | bytes 12288 | tf_op jit(solution)/shard_map/while/body/eval_jaxpr/jit(_take)/gather | solution.py:93
  168.8 6.2 %gather_fusion.9 = f32[1024]{0:T(1024)S(1)} fusion(f32[2176]{0:T(1024)S(1)} %constant_dynamic-update-slice_fusion.29, s32[1024]{0:T(1024)S(1)} %fusion.92), kind=kCustom, calls=%fused_computation.1.clone.clone.1 | custom fusion | bytes 12288 | tf_op jit(solution)/shard_map/while/body/eval_jaxpr/jit(_take)/gather | solution.py:93
  175.6 5.2 %collective-permute-start = (f32[256]{0:T(256)S(1)}, f32[256]{0:T(256)S(1)}, u32[]{:S(2)}, u32[]{:S(2)}) collective-permute-start(f32[256]{0:T(256)S(1)} %fusion.82), channel_id=1, source_target_pairs={{0,1},{1,2},{2,3},{3,4},{4,5},{5,6},{6,7},{7,8},{8,9},{9,10},{10,1... | collective-permute-start | bytes 3080 | tf_op jit(solution)/shard_map/while/body/eval_jaxpr/ppermute | solution.py:21
  187.9 3.9 collective-permute-start.3
  193.9 6.1 %gather_fusion.4 = f32[1024]{0:T(1024)S(1)} fusion(f32[2176]{0:T(1024)S(1)} %constant_dynamic-update-slice_fusion.29, s32[1024]{0:T(1024)S(1)} %fusion.87), kind=kCustom, calls=%fused_computation.15.clone.clone.1 | custom fusion | bytes 12288 | tf_op jit(solution)/shard_map/while/body/eval_jaxpr/jit(_take)/gather | solution.py:93
  200.0 6.2 %gather_fusion.5 = f32[1024]{0:T(1024)S(1)} fusion(f32[2176]{0:T(1024)S(1)} %constant_dynamic-update-slice_fusion.29, s32[1024]{0:T(1024)S(1)} %fusion.88), kind=kCustom, calls=%fused_computation.14.clone.clone.1 | custom fusion | bytes 12288 | tf_op jit(solution)/shard_map/while/body/eval_jaxpr/jit(_take)/gather | solution.py:93
  206.2 6.2 %gather_fusion.6 = f32[1024]{0:T(1024)S(1)} fusion(f32[2176]{0:T(1024)S(1)} %constant_dynamic-update-slice_fusion.29, s32[1024]{0:T(1024)S(1)} %fusion.89), kind=kCustom, calls=%fused_computation.13.clone.clone.1 | custom fusion | bytes 12288 | tf_op jit(solution)/shard_map/while/body/eval_jaxpr/jit(_take)/gather | solution.py:93
  212.3 6.2 %gather_fusion.7 = f32[1024]{0:T(1024)S(1)} fusion(f32[2176]{0:T(1024)S(1)} %constant_dynamic-update-slice_fusion.29, s32[1024]{0:T(1024)S(1)} %fusion.90), kind=kCustom, calls=%fused_computation.12.clone.clone.1 | custom fusion | bytes 12288 | tf_op jit(solution)/shard_map/while/body/eval_jaxpr/jit(_take)/gather | solution.py:93
  218.5 6.2 %gather_fusion.8 = f32[1024]{0:T(1024)S(1)} fusion(f32[2176]{0:T(1024)S(1)} %constant_dynamic-update-slice_fusion.29, s32[1024]{0:T(1024)S(1)} %fusion.91), kind=kCustom, calls=%fused_computation.11.clone.clone.1 | custom fusion | bytes 12288 | tf_op jit(solution)/shard_map/while/body/eval_jaxpr/jit(_take)/gather | solution.py:93
  224.7 6.2 %gather_fusion.9 = f32[1024]{0:T(1024)S(1)} fusion(f32[2176]{0:T(1024)S(1)} %constant_dynamic-update-slice_fusion.29, s32[1024]{0:T(1024)S(1)} %fusion.92), kind=kCustom, calls=%fused_computation.1.clone.clone.1 | custom fusion | bytes 12288 | tf_op jit(solution)/shard_map/while/body/eval_jaxpr/jit(_take)/gather | solution.py:93
  231.6 5.2 %collective-permute-start = (f32[256]{0:T(256)S(1)}, f32[256]{0:T(256)S(1)}, u32[]{:S(2)}, u32[]{:S(2)}) collective-permute-start(f32[256]{0:T(256)S(1)} %fusion.82), channel_id=1, source_target_pairs={{0,1},{1,2},{2,3},{3,4},{4,5},{5,6},{6,7},{7,8},{8,9},{9,10},{10,1... | collective-permute-start | bytes 3080 | tf_op jit(solution)/shard_map/while/body/eval_jaxpr/ppermute | solution.py:21
  243.9 3.9 collective-permute-start.3
  249.8 6.1 %gather_fusion.4 = f32[1024]{0:T(1024)S(1)} fusion(f32[2176]{0:T(1024)S(1)} %constant_dynamic-update-slice_fusion.29, s32[1024]{0:T(1024)S(1)} %fusion.87), kind=kCustom, calls=%fused_computation.15.clone.clone.1 | custom fusion | bytes 12288 | tf_op jit(solution)/shard_map/while/body/eval_jaxpr/jit(_take)/gather | solution.py:93
  255.9 6.2 %gather_fusion.5 = f32[1024]{0:T(1024)S(1)} fusion(f32[2176]{0:T(1024)S(1)} %constant_dynamic-update-slice_fusion.29, s32[1024]{0:T(1024)S(1)} %fusion.88), kind=kCustom, calls=%fused_computation.14.clone.clone.1 | custom fusion | bytes 12288 | tf_op jit(solution)/shard_map/while/body/eval_jaxpr/jit(_take)/gather | solution.py:93
  262.1 6.2 %gather_fusion.6 = f32[1024]{0:T(1024)S(1)} fusion(f32[2176]{0:T(1024)S(1)} %constant_dynamic-update-slice_fusion.29, s32[1024]{0:T(1024)S(1)} %fusion.89), kind=kCustom, calls=%fused_computation.13.clone.clone.1 | custom fusion | bytes 12288 | tf_op jit(solution)/shard_map/while/body/eval_jaxpr/jit(_take)/gather | solution.py:93
  268.3 6.2 %gather_fusion.7 = f32[1024]{0:T(1024)S(1)} fusion(f32[2176]{0:T(1024)S(1)} %constant_dynamic-update-slice_fusion.29, s32[1024]{0:T(1024)S(1)} %fusion.90), kind=kCustom, calls=%fused_computation.12.clone.clone.1 | custom fusion | bytes 12288 | tf_op jit(solution)/shard_map/while/body/eval_jaxpr/jit(_take)/gather | solution.py:93
  274.4 6.2 %gather_fusion.8 = f32[1024]{0:T(1024)S(1)} fusion(f32[2176]{0:T(1024)S(1)} %constant_dynamic-update-slice_fusion.29, s32[1024]{0:T(1024)S(1)} %fusion.91), kind=kCustom, calls=%fused_computation.11.clone.clone.1 | custom fusion | bytes 12288 | tf_op jit(solution)/shard_map/while/body/eval_jaxpr/jit(_take)/gather | solution.py:93
  280.6 6.2 %gather_fusion.9 = f32[1024]{0:T(1024)S(1)} fusion(f32[2176]{0:T(1024)S(1)} %constant_dynamic-update-slice_fusion.29, s32[1024]{0:T(1024)S(1)} %fusion.92), kind=kCustom, calls=%fused_computation.1.clone.clone.1 | custom fusion | bytes 12288 | tf_op jit(solution)/shard_map/while/body/eval_jaxpr/jit(_take)/gather | solution.py:93
  287.5 5.2 %collective-permute-start = (f32[256]{0:T(256)S(1)}, f32[256]{0:T(256)S(1)}, u32[]{:S(2)}, u32[]{:S(2)}) collective-permute-start(f32[256]{0:T(256)S(1)} %fusion.82), channel_id=1, source_target_pairs={{0,1},{1,2},{2,3},{3,4},{4,5},{5,6},{6,7},{7,8},{8,9},{9,10},{10,1... | collective-permute-start | bytes 3080 | tf_op jit(solution)/shard_map/while/body/eval_jaxpr/ppermute | solution.py:21
  299.8 3.9 collective-permute-start.3
  305.7 6.1 %gather_fusion.4 = f32[1024]{0:T(1024)S(1)} fusion(f32[2176]{0:T(1024)S(1)} %constant_dynamic-update-slice_fusion.29, s32[1024]{0:T(1024)S(1)} %fusion.87), kind=kCustom, calls=%fused_computation.15.clone.clone.1 | custom fusion | bytes 12288 | tf_op jit(solution)/shard_map/while/body/eval_jaxpr/jit(_take)/gather | solution.py:93
  311.8 6.2 %gather_fusion.5 = f32[1024]{0:T(1024)S(1)} fusion(f32[2176]{0:T(1024)S(1)} %constant_dynamic-update-slice_fusion.29, s32[1024]{0:T(1024)S(1)} %fusion.88), kind=kCustom, calls=%fused_computation.14.clone.clone.1 | custom fusion | bytes 12288 | tf_op jit(solution)/shard_map/while/body/eval_jaxpr/jit(_take)/gather | solution.py:93
  318.0 6.2 %gather_fusion.6 = f32[1024]{0:T(1024)S(1)} fusion(f32[2176]{0:T(1024)S(1)} %constant_dynamic-update-slice_fusion.29, s32[1024]{0:T(1024)S(1)} %fusion.89), kind=kCustom, calls=%fused_computation.13.clone.clone.1 | custom fusion | bytes 12288 | tf_op jit(solution)/shard_map/while/body/eval_jaxpr/jit(_take)/gather | solution.py:93
  324.2 6.2 %gather_fusion.7 = f32[1024]{0:T(1024)S(1)} fusion(f32[2176]{0:T(1024)S(1)} %constant_dynamic-update-slice_fusion.29, s32[1024]{0:T(1024)S(1)} %fusion.90), kind=kCustom, calls=%fused_computation.12.clone.clone.1 | custom fusion | bytes 12288 | tf_op jit(solution)/shard_map/while/body/eval_jaxpr/jit(_take)/gather | solution.py:93
  330.3 6.2 %gather_fusion.8 = f32[1024]{0:T(1024)S(1)} fusion(f32[2176]{0:T(1024)S(1)} %constant_dynamic-update-slice_fusion.29, s32[1024]{0:T(1024)S(1)} %fusion.91), kind=kCustom, calls=%fused_computation.11.clone.clone.1 | custom fusion | bytes 12288 | tf_op jit(solution)/shard_map/while/body/eval_jaxpr/jit(_take)/gather | solution.py:93
  336.5 6.2 %gather_fusion.9 = f32[1024]{0:T(1024)S(1)} fusion(f32[2176]{0:T(1024)S(1)} %constant_dynamic-update-slice_fusion.29, s32[1024]{0:T(1024)S(1)} %fusion.92), kind=kCustom, calls=%fused_computation.1.clone.clone.1 | custom fusion | bytes 12288 | tf_op jit(solution)/shard_map/while/body/eval_jaxpr/jit(_take)/gather | solution.py:93
  342.7 4.3 collective-permute-start.5
  351.3 4.7 %collective-permute-start.7 = (f32[256]{0:T(256)S(1)}, f32[256]{0:T(256)S(1)}, u32[]{:S(2)}, u32[]{:S(2)}) collective-permute-start(f32[256]{0:T(256)S(1)} %fusion.53), channel_id=1, source_target_pairs={{2,0},{3,1},{4,2},{5,3},{6,4},{7,5},{8,6},{9,7},{10,8},{11,9},{12,... | collective-permute-start | bytes 3080 | tf_op jit(solution)/shard_map/ppermute | solution.py:21
  366.9 3.9 collective-permute-start.11
  370.9 6.2 %gather_fusion.14 = f32[1024]{0:T(1024)S(1)} fusion(f32[2176]{0:T(1024)S(1)} %constant_dynamic-update-slice_fusion.13, s32[1024]{0:T(1024)S(1)} %get-tuple-element.233), kind=kCustom, calls=%fused_computation.16.clone | custom fusion | bytes 12288 | tf_op jit(solution)/shard_map/jit(_take)/gather | solution.py:72
  377.0 6.2 %gather_fusion.20 = f32[1024]{0:T(1024)S(1)} fusion(f32[2176]{0:T(1024)S(1)} %constant_dynamic-update-slice_fusion.13, s32[1024]{0:T(1024)S(1)} %get-tuple-element.234), kind=kCustom, calls=%fused_computation.17.clone | custom fusion | bytes 12288 | tf_op jit(solution)/shard_map/jit(_take)/gather | solution.py:72
  383.2 6.2 %gather_fusion.22 = f32[1024]{0:T(1024)S(1)} fusion(f32[2176]{0:T(1024)S(1)} %constant_dynamic-update-slice_fusion.13, s32[1024]{0:T(1024)S(1)} %get-tuple-element.235), kind=kCustom, calls=%fused_computation.18.clone | custom fusion | bytes 12288 | tf_op jit(solution)/shard_map/jit(_take)/gather | solution.py:72
  389.4 6.2 %gather_fusion.24 = f32[1024]{0:T(1024)S(1)} fusion(f32[2176]{0:T(1024)S(1)} %constant_dynamic-update-slice_fusion.13, s32[1024]{0:T(1024)S(1)} %get-tuple-element.236), kind=kCustom, calls=%fused_computation.19.clone | custom fusion | bytes 12288 | tf_op jit(solution)/shard_map/jit(_take)/gather | solution.py:72
  395.6 6.2 %gather_fusion.26 = f32[1024]{0:T(1024)S(1)} fusion(f32[2176]{0:T(1024)S(1)} %constant_dynamic-update-slice_fusion.13, s32[1024]{0:T(1024)S(1)} %get-tuple-element.237), kind=kCustom, calls=%fused_computation.20.clone | custom fusion | bytes 12288 | tf_op jit(solution)/shard_map/jit(_take)/gather | solution.py:72
  401.7 6.2 %gather_fusion.28 = f32[1024]{0:T(1024)S(1)} fusion(f32[2176]{0:T(1024)S(1)} %constant_dynamic-update-slice_fusion.13, s32[1024]{0:T(1024)S(1)} %get-tuple-element.238), kind=kCustom, calls=%fused_computation.21.clone | custom fusion | bytes 12288 | tf_op jit(solution)/shard_map/jit(_take)/gather | solution.py:72
  411.2 4.0 gather_fusion.21
  415.2 4.0 gather_fusion.23
  419.2 4.0 gather_fusion.25
  423.2 4.0 gather_fusion.27
  427.2 4.0 gather_fusion.29
  431.2 6.2 %fusion.30 = f32[40,1024]{0,1:T(8,128)S(1)} fusion(f32[40,1024]{0,1:T(8,128)S(1)} %copy.88, f32[1024,40]{1,0:T(8,128)} %gather_fusion.29, f32[1024,40]{1,0:T(8,128)} %gather_fusion.27, f32[1024,40]{1,0:T(8,128)} %gather_fusion.25, f32[1024,40]{1,0:T(8,128)} %gather_fusion.23, f32[1024,40]{1,0:T(8,128)} %gather_fusion.21, f32[1024,40]{1,0:T(8,128)S(1)} %gather_fusion.19, ...), kind=kLoop, calls=%fused_computation.105 | loop fusion | flops 1843200 | bytes 1694016 | tf_op jit(solution)/shard_map/add | solution.py:103
  (315 shorter events, 83.9 us)
Async XLA Ops:
  0.6 10.0 %copy-start.3 = (s32[6,1024]{1,0:T(8,128)S(1)}, s32[6,1024]{1,0:T(8,128)}, u32[]{:S(2)}) copy-start(s32[6,1024]{1,0:T(8,128)} %param.21) | copy-start | bytes 73732
  0.6 10.0 %copy-start.4 = (f32[6,1024]{1,0:T(8,128)S(1)}, f32[6,1024]{1,0:T(8,128)}, u32[]{:S(2)}) copy-start(f32[6,1024]{1,0:T(8,128)} %param.22) | copy-start | bytes 73732
  0.7 10.0 %copy-start.1 = (f32[1024]{0:T(1024)S(1)}, f32[1024]{0:T(1024)}, u32[]{:S(2)}) copy-start(f32[1024]{0:T(1024)} %param.23) | copy-start | bytes 12292
  0.7 10.0 %copy-start.6 = (f32[1024]{0:T(1024)S(1)}, f32[1024]{0:T(1024)}, u32[]{:S(2)}) copy-start(f32[1024]{0:T(1024)} %param.24) | copy-start | bytes 12292
  3.9 357.4 %collective-permute-start.4 = (f32[256]{0:T(256)S(1)}, f32[256]{0:T(256)S(1)}, u32[]{:S(2)}, u32[]{:S(2)}) collective-permute-start(f32[256]{0:T(256)S(1)} %fusion.56), channel_id=1, source_target_pairs={{0,1},{1,2},{2,3},{3,4},{4,5},{5,6},{6,7},{7,8},{8,9},{9,10},{10,1... | collective-permute-start | bytes 3080 | tf_op jit(solution)/shard_map/ppermute | solution.py:21
  10.7 345.3 %copy-start.7 = (s32[1024]{0:T(1024)S(1)}, s32[1024]{0:T(1024)}, u32[]{:S(2)}) copy-start(s32[1024]{0:T(1024)} %param.20) | copy-start | bytes 12292
  10.7 345.4 %copy-start.2 = (f32[40,1024]{1,0:T(8,128)S(1)}, f32[40,1024]{1,0:T(8,128)}, u32[]{:S(2)}) copy-start(f32[40,1024]{1,0:T(8,128)} %param.19) | copy-start | bytes 491524
  11.4 13.5 %collective-permute-start = (f32[256]{0:T(256)S(1)}, f32[256]{0:T(256)S(1)}, u32[]{:S(2)}, u32[]{:S(2)}) collective-permute-start(f32[256]{0:T(256)S(1)} %fusion.82), channel_id=1, source_target_pairs={{0,1},{1,2},{2,3},{3,4},{4,5},{5,6},{6,7},{7,8},{8,9},{9,10},{10,1... | collective-permute-start | bytes 3080 | tf_op jit(solution)/shard_map/while/body/eval_jaxpr/ppermute | solution.py:21
  14.0 11.0 %collective-permute-start.1 = (f32[256]{0:T(256)S(1)}, f32[256]{0:T(256)S(1)}, u32[]{:S(2)}, u32[]{:S(2)}) collective-permute-start(f32[256]{0:T(256)S(1)} %fusion.83), channel_id=1, source_target_pairs={{1,0},{2,1},{3,2},{4,3},{5,4},{6,5},{7,6},{8,7},{9,8},{10,9},{11,1... | collective-permute-start | bytes 3080 | tf_op jit(solution)/shard_map/while/body/eval_jaxpr/ppermute | solution.py:21
  17.0 7.9 %collective-permute-start.2 = (f32[256]{0:T(256)S(1)}, f32[256]{0:T(256)S(1)}, u32[]{:S(2)}, u32[]{:S(2)}) collective-permute-start(f32[256]{0:T(256)S(1)} %fusion.84), channel_id=1, source_target_pairs={{0,2},{1,3},{2,4},{3,5},{4,6},{5,7},{6,8},{7,9},{8,10},{9,11},{10,... | collective-permute-start | bytes 3080 | tf_op jit(solution)/shard_map/while/body/eval_jaxpr/ppermute | solution.py:21
  20.8 4.7 %collective-permute-start.3 = (f32[256]{0:T(256)S(1)}, f32[256]{0:T(256)S(1)}, u32[]{:S(2)}, u32[]{:S(2)}) collective-permute-start(f32[256]{0:T(256)S(1)} %fusion.85), channel_id=1, source_target_pairs={{2,0},{3,1},{4,2},{5,3},{6,4},{7,5},{8,6},{9,7},{10,8},{11,9},{12,... | collective-permute-start | bytes 3080 | tf_op jit(solution)/shard_map/while/body/eval_jaxpr/ppermute | solution.py:21
  63.2 17.1 %collective-permute-start = (f32[256]{0:T(256)S(1)}, f32[256]{0:T(256)S(1)}, u32[]{:S(2)}, u32[]{:S(2)}) collective-permute-start(f32[256]{0:T(256)S(1)} %fusion.82), channel_id=1, source_target_pairs={{0,1},{1,2},{2,3},{3,4},{4,5},{5,6},{6,7},{7,8},{8,9},{9,10},{10,1... | collective-permute-start | bytes 3080 | tf_op jit(solution)/shard_map/while/body/eval_jaxpr/ppermute | solution.py:21
  69.8 10.5 %collective-permute-start.1 = (f32[256]{0:T(256)S(1)}, f32[256]{0:T(256)S(1)}, u32[]{:S(2)}, u32[]{:S(2)}) collective-permute-start(f32[256]{0:T(256)S(1)} %fusion.83), channel_id=1, source_target_pairs={{1,0},{2,1},{3,2},{4,3},{5,4},{6,5},{7,6},{8,7},{9,8},{10,9},{11,1... | collective-permute-start | bytes 3080 | tf_op jit(solution)/shard_map/while/body/eval_jaxpr/ppermute | solution.py:21
  72.4 7.9 %collective-permute-start.2 = (f32[256]{0:T(256)S(1)}, f32[256]{0:T(256)S(1)}, u32[]{:S(2)}, u32[]{:S(2)}) collective-permute-start(f32[256]{0:T(256)S(1)} %fusion.84), channel_id=1, source_target_pairs={{0,2},{1,3},{2,4},{3,5},{4,6},{5,7},{6,8},{7,9},{8,10},{9,11},{10,... | collective-permute-start | bytes 3080 | tf_op jit(solution)/shard_map/while/body/eval_jaxpr/ppermute | solution.py:21
  75.6 6.4 %collective-permute-start.3 = (f32[256]{0:T(256)S(1)}, f32[256]{0:T(256)S(1)}, u32[]{:S(2)}, u32[]{:S(2)}) collective-permute-start(f32[256]{0:T(256)S(1)} %fusion.85), channel_id=1, source_target_pairs={{2,0},{3,1},{4,2},{5,3},{6,4},{7,5},{8,6},{9,7},{10,8},{11,9},{12,... | collective-permute-start | bytes 3080 | tf_op jit(solution)/shard_map/while/body/eval_jaxpr/ppermute | solution.py:21
  119.7 16.0 %collective-permute-start = (f32[256]{0:T(256)S(1)}, f32[256]{0:T(256)S(1)}, u32[]{:S(2)}, u32[]{:S(2)}) collective-permute-start(f32[256]{0:T(256)S(1)} %fusion.82), channel_id=1, source_target_pairs={{0,1},{1,2},{2,3},{3,4},{4,5},{5,6},{6,7},{7,8},{8,9},{9,10},{10,1... | collective-permute-start | bytes 3080 | tf_op jit(solution)/shard_map/while/body/eval_jaxpr/ppermute | solution.py:21
  125.2 10.6 %collective-permute-start.1 = (f32[256]{0:T(256)S(1)}, f32[256]{0:T(256)S(1)}, u32[]{:S(2)}, u32[]{:S(2)}) collective-permute-start(f32[256]{0:T(256)S(1)} %fusion.83), channel_id=1, source_target_pairs={{1,0},{2,1},{3,2},{4,3},{5,4},{6,5},{7,6},{8,7},{9,8},{10,9},{11,1... | collective-permute-start | bytes 3080 | tf_op jit(solution)/shard_map/while/body/eval_jaxpr/ppermute | solution.py:21
  127.7 8.0 %collective-permute-start.2 = (f32[256]{0:T(256)S(1)}, f32[256]{0:T(256)S(1)}, u32[]{:S(2)}, u32[]{:S(2)}) collective-permute-start(f32[256]{0:T(256)S(1)} %fusion.84), channel_id=1, source_target_pairs={{0,2},{1,3},{2,4},{3,5},{4,6},{5,7},{6,8},{7,9},{8,10},{9,11},{10,... | collective-permute-start | bytes 3080 | tf_op jit(solution)/shard_map/while/body/eval_jaxpr/ppermute | solution.py:21
  132.0 5.9 %collective-permute-start.3 = (f32[256]{0:T(256)S(1)}, f32[256]{0:T(256)S(1)}, u32[]{:S(2)}, u32[]{:S(2)}) collective-permute-start(f32[256]{0:T(256)S(1)} %fusion.85), channel_id=1, source_target_pairs={{2,0},{3,1},{4,2},{5,3},{6,4},{7,5},{8,6},{9,7},{10,8},{11,9},{12,... | collective-permute-start | bytes 3080 | tf_op jit(solution)/shard_map/while/body/eval_jaxpr/ppermute | solution.py:21
  175.6 16.3 %collective-permute-start = (f32[256]{0:T(256)S(1)}, f32[256]{0:T(256)S(1)}, u32[]{:S(2)}, u32[]{:S(2)}) collective-permute-start(f32[256]{0:T(256)S(1)} %fusion.82), channel_id=1, source_target_pairs={{0,1},{1,2},{2,3},{3,4},{4,5},{5,6},{6,7},{7,8},{8,9},{9,10},{10,1... | collective-permute-start | bytes 3080 | tf_op jit(solution)/shard_map/while/body/eval_jaxpr/ppermute | solution.py:21
  181.6 10.5 %collective-permute-start.1 = (f32[256]{0:T(256)S(1)}, f32[256]{0:T(256)S(1)}, u32[]{:S(2)}, u32[]{:S(2)}) collective-permute-start(f32[256]{0:T(256)S(1)} %fusion.83), channel_id=1, source_target_pairs={{1,0},{2,1},{3,2},{4,3},{5,4},{6,5},{7,6},{8,7},{9,8},{10,9},{11,1... | collective-permute-start | bytes 3080 | tf_op jit(solution)/shard_map/while/body/eval_jaxpr/ppermute | solution.py:21
  184.1 7.9 %collective-permute-start.2 = (f32[256]{0:T(256)S(1)}, f32[256]{0:T(256)S(1)}, u32[]{:S(2)}, u32[]{:S(2)}) collective-permute-start(f32[256]{0:T(256)S(1)} %fusion.84), channel_id=1, source_target_pairs={{0,2},{1,3},{2,4},{3,5},{4,6},{5,7},{6,8},{7,9},{8,10},{9,11},{10,... | collective-permute-start | bytes 3080 | tf_op jit(solution)/shard_map/while/body/eval_jaxpr/ppermute | solution.py:21
  187.9 5.9 %collective-permute-start.3 = (f32[256]{0:T(256)S(1)}, f32[256]{0:T(256)S(1)}, u32[]{:S(2)}, u32[]{:S(2)}) collective-permute-start(f32[256]{0:T(256)S(1)} %fusion.85), channel_id=1, source_target_pairs={{2,0},{3,1},{4,2},{5,3},{6,4},{7,5},{8,6},{9,7},{10,8},{11,9},{12,... | collective-permute-start | bytes 3080 | tf_op jit(solution)/shard_map/while/body/eval_jaxpr/ppermute | solution.py:21
  231.6 16.3 %collective-permute-start = (f32[256]{0:T(256)S(1)}, f32[256]{0:T(256)S(1)}, u32[]{:S(2)}, u32[]{:S(2)}) collective-permute-start(f32[256]{0:T(256)S(1)} %fusion.82), channel_id=1, source_target_pairs={{0,1},{1,2},{2,3},{3,4},{4,5},{5,6},{6,7},{7,8},{8,9},{9,10},{10,1... | collective-permute-start | bytes 3080 | tf_op jit(solution)/shard_map/while/body/eval_jaxpr/ppermute | solution.py:21
  237.5 10.5 %collective-permute-start.1 = (f32[256]{0:T(256)S(1)}, f32[256]{0:T(256)S(1)}, u32[]{:S(2)}, u32[]{:S(2)}) collective-permute-start(f32[256]{0:T(256)S(1)} %fusion.83), channel_id=1, source_target_pairs={{1,0},{2,1},{3,2},{4,3},{5,4},{6,5},{7,6},{8,7},{9,8},{10,9},{11,1... | collective-permute-start | bytes 3080 | tf_op jit(solution)/shard_map/while/body/eval_jaxpr/ppermute | solution.py:21
  240.0 7.9 %collective-permute-start.2 = (f32[256]{0:T(256)S(1)}, f32[256]{0:T(256)S(1)}, u32[]{:S(2)}, u32[]{:S(2)}) collective-permute-start(f32[256]{0:T(256)S(1)} %fusion.84), channel_id=1, source_target_pairs={{0,2},{1,3},{2,4},{3,5},{4,6},{5,7},{6,8},{7,9},{8,10},{9,11},{10,... | collective-permute-start | bytes 3080 | tf_op jit(solution)/shard_map/while/body/eval_jaxpr/ppermute | solution.py:21
  243.9 5.9 %collective-permute-start.3 = (f32[256]{0:T(256)S(1)}, f32[256]{0:T(256)S(1)}, u32[]{:S(2)}, u32[]{:S(2)}) collective-permute-start(f32[256]{0:T(256)S(1)} %fusion.85), channel_id=1, source_target_pairs={{2,0},{3,1},{4,2},{5,3},{6,4},{7,5},{8,6},{9,7},{10,8},{11,9},{12,... | collective-permute-start | bytes 3080 | tf_op jit(solution)/shard_map/while/body/eval_jaxpr/ppermute | solution.py:21
  287.5 16.3 %collective-permute-start = (f32[256]{0:T(256)S(1)}, f32[256]{0:T(256)S(1)}, u32[]{:S(2)}, u32[]{:S(2)}) collective-permute-start(f32[256]{0:T(256)S(1)} %fusion.82), channel_id=1, source_target_pairs={{0,1},{1,2},{2,3},{3,4},{4,5},{5,6},{6,7},{7,8},{8,9},{9,10},{10,1... | collective-permute-start | bytes 3080 | tf_op jit(solution)/shard_map/while/body/eval_jaxpr/ppermute | solution.py:21
  293.4 10.5 %collective-permute-start.1 = (f32[256]{0:T(256)S(1)}, f32[256]{0:T(256)S(1)}, u32[]{:S(2)}, u32[]{:S(2)}) collective-permute-start(f32[256]{0:T(256)S(1)} %fusion.83), channel_id=1, source_target_pairs={{1,0},{2,1},{3,2},{4,3},{5,4},{6,5},{7,6},{8,7},{9,8},{10,9},{11,1... | collective-permute-start | bytes 3080 | tf_op jit(solution)/shard_map/while/body/eval_jaxpr/ppermute | solution.py:21
  295.9 7.9 %collective-permute-start.2 = (f32[256]{0:T(256)S(1)}, f32[256]{0:T(256)S(1)}, u32[]{:S(2)}, u32[]{:S(2)}) collective-permute-start(f32[256]{0:T(256)S(1)} %fusion.84), channel_id=1, source_target_pairs={{0,2},{1,3},{2,4},{3,5},{4,6},{5,7},{6,8},{7,9},{8,10},{9,11},{10,... | collective-permute-start | bytes 3080 | tf_op jit(solution)/shard_map/while/body/eval_jaxpr/ppermute | solution.py:21
  299.8 5.9 %collective-permute-start.3 = (f32[256]{0:T(256)S(1)}, f32[256]{0:T(256)S(1)}, u32[]{:S(2)}, u32[]{:S(2)}) collective-permute-start(f32[256]{0:T(256)S(1)} %fusion.85), channel_id=1, source_target_pairs={{2,0},{3,1},{4,2},{5,3},{6,4},{7,5},{8,6},{9,7},{10,8},{11,9},{12,... | collective-permute-start | bytes 3080 | tf_op jit(solution)/shard_map/while/body/eval_jaxpr/ppermute | solution.py:21
  342.7 18.5 %copy-start = (f32[1024]{0:T(1024)}, f32[1024]{0:T(1024)S(1)}, u32[]{:S(2)}) copy-start(f32[1024]{0:T(1024)S(1)} %get-tuple-element.135) | copy-start | bytes 12292
  342.7 18.5 %copy-start.5 = (f32[1024]{0:T(1024)}, f32[1024]{0:T(1024)S(1)}, u32[]{:S(2)}) copy-start(f32[1024]{0:T(1024)S(1)} %get-tuple-element.136) | copy-start | bytes 12292
  342.7 21.0 %collective-permute-start.5 = (f32[256]{0:T(256)S(1)}, f32[256]{0:T(256)S(1)}, u32[]{:S(2)}, u32[]{:S(2)}) collective-permute-start(f32[256]{0:T(256)S(1)} %fusion.55), channel_id=1, source_target_pairs={{1,0},{2,1},{3,2},{4,3},{5,4},{6,5},{7,6},{8,7},{9,8},{10,9},{11,1... | collective-permute-start | bytes 3080 | tf_op jit(solution)/shard_map/ppermute | solution.py:21
  347.8 19.1 %collective-permute-start.6 = (f32[256]{0:T(256)S(1)}, f32[256]{0:T(256)S(1)}, u32[]{:S(2)}, u32[]{:S(2)}) collective-permute-start(f32[256]{0:T(256)S(1)} %fusion.54), channel_id=1, source_target_pairs={{0,2},{1,3},{2,4},{3,5},{4,6},{5,7},{6,8},{7,9},{8,10},{9,11},{10,... | collective-permute-start | bytes 3080 | tf_op jit(solution)/shard_map/ppermute | solution.py:21
  351.3 19.5 %collective-permute-start.7 = (f32[256]{0:T(256)S(1)}, f32[256]{0:T(256)S(1)}, u32[]{:S(2)}, u32[]{:S(2)}) collective-permute-start(f32[256]{0:T(256)S(1)} %fusion.53), channel_id=1, source_target_pairs={{2,0},{3,1},{4,2},{5,3},{6,4},{7,5},{8,6},{9,7},{10,8},{11,9},{12,... | collective-permute-start | bytes 3080 | tf_op jit(solution)/shard_map/ppermute | solution.py:21
  358.9 49.0 %collective-permute-start.8 = (f32[40,256]{1,0:T(8,128)S(1)}, f32[40,256]{1,0:T(8,128)S(1)}, u32[]{:S(2)}, u32[]{:S(2)}) collective-permute-start(f32[40,256]{1,0:T(8,128)S(1)} %copy_bitcast_fusion.4), channel_id=1, source_target_pairs={{0,1},{1,2},{2,3},{3,4},{4,5},{5,6},{6,7},{7,8},{8,9},{9,10},{10,1... | collective-permute-start | bytes 122888 | tf_op jit(solution)/shard_map/ppermute | solution.py:21
  361.3 46.7 %collective-permute-start.9 = (f32[40,256]{1,0:T(8,128)S(1)}, f32[40,256]{1,0:T(8,128)S(1)}, u32[]{:S(2)}, u32[]{:S(2)}) collective-permute-start(f32[40,256]{1,0:T(8,128)S(1)} %copy_bitcast_fusion.3), channel_id=1, source_target_pairs={{1,0},{2,1},{3,2},{4,3},{5,4},{6,5},{7,6},{8,7},{9,8},{10,9},{11,1... | collective-permute-start | bytes 122888 | tf_op jit(solution)/shard_map/ppermute | solution.py:21
  363.7 44.3 %collective-permute-start.10 = (f32[40,256]{1,0:T(8,128)S(1)}, f32[40,256]{1,0:T(8,128)S(1)}, u32[]{:S(2)}, u32[]{:S(2)}) collective-permute-start(f32[40,256]{1,0:T(8,128)S(1)} %copy_bitcast_fusion.2), channel_id=1, source_target_pairs={{0,2},{1,3},{2,4},{3,5},{4,6},{5,7},{6,8},{7,9},{8,10},{9,11},{10,... | collective-permute-start | bytes 122888 | tf_op jit(solution)/shard_map/ppermute | solution.py:21
  366.9 41.1 %collective-permute-start.11 = (f32[40,256]{1,0:T(8,128)S(1)}, f32[40,256]{1,0:T(8,128)S(1)}, u32[]{:S(2)}, u32[]{:S(2)}) collective-permute-start(f32[40,256]{1,0:T(8,128)S(1)} %copy_bitcast_fusion.1), channel_id=1, source_target_pairs={{2,0},{3,1},{4,2},{5,3},{6,4},{7,5},{8,6},{9,7},{10,8},{11,9},{12,... | collective-permute-start | bytes 122888 | tf_op jit(solution)/shard_map/ppermute | solution.py:21
  427.2 4.0 copy-start.8
where the time goes:
time: 443 us; the launch traced here: 438 us
  local copies, waits for them, and re-layouts  303 us (68%)
  starting transfers between devices  110 us (25%)
  other arithmetic  13.1 us (3%)
  waiting for transfers between devices  9.77 us (2%)
    gather x36, local copies, waits for them, and re-layouts, substep(): jnp.take(extended, neighbours[column]) - height  221 us
    ppermute x32, starting transfers between devices, from_behind(): return lax.ppermute(value, axis, pairs)  110 us
    gather x6, local copies, waits for them, and re-layouts, shards(): near_levels = jnp.take(ext_levels, index)  36.9 us
    gather x6, local copies, waits for them, and re-layouts, shards(): near_tracer = jnp.take(ext_tracer, index, axis=1)  22.8 us
    gather x32, local copies, waits for them, and re-layouts, outgoing(): chosen = jnp.take(blocks, picked_row, axis=-2) * filled_row[:, None]  17.8 us
    ppermute x32, waiting for transfers between devices, from_behind(): return lax.ppermute(value, axis, pairs)  9.77 us
  transfers between devices with their start and end apart: 32, of which 6 were waited for; matrix products, arithmetic and copies ran while one was open for 64% of the time, Pallas kernels for 0%

commit v1 on v0

v1 whole, which is shorter than its diff:
```python
import functools

import jax
import jax.numpy as jnp
from jax import lax
from jax.experimental import pallas as pl
from jax.experimental.pallas import tpu as pltpu
from jax.sharding import PartitionSpec as P

LANES = 128
SUBS = 8
SUBSTEPS = 6
OFFSETS = (1, -1, 2, -2)
horizontal_rate = 0.5
vertical_rate = 0.5
tracer_step = 0.2
barotropic_step = 0.5
friction = 0.05
ABSENT = 3e38
PRESENT = 1e38

SMEM = pl.BlockSpec(memory_space=pltpu.SMEM)
VMEM = pl.BlockSpec(memory_space=pltpu.VMEM)


def even_swap(count, by):
    return [(i, i ^ by) for i in range(count)]


def odd_swap(count, by):
    pairs = [(i, i + by) for i in range(by, count - by) if (i // by) % 2 == 1]
    pairs += [(b, a) for a, b in pairs]
    busy = {a for a, _ in pairs}
    rest = [i for i in range(count) if i not in busy]
    pairs += list(zip(rest[0::2], rest[1::2])) + list(zip(rest[1::2], rest[0::2]))
    return pairs


def exchange(payloads, count):
    ways = (even_swap(count, 1), odd_swap(count, 1), even_swap(count, 2), odd_swap(count, 2))
    return [lax.ppermute(value, "dom", way) for value, way in zip(payloads, ways)]


def column(scalars, tile):
    rows = lax.broadcasted_iota(jnp.int32, (SUBS, LANES), 0)
    value = jnp.zeros((SUBS, LANES), jnp.float32)
    for k in range(SUBS):
        value = jnp.where(rows == k, scalars[tile * SUBS + k], value)
    return value


def localize(index, place, count, cells, send):
    span = send * LANES
    result = index
    for g, offset in enumerate(OFFSETS):
        source = place - offset
        inside = jnp.logical_and(source >= 0, source < count)
        swapped = (place // abs(offset)) % 2 == 0
        step = jnp.where(swapped, span if g % 2 == 0 else -span, 0)
        low = cells + g * span
        mine = jnp.logical_and(index >= low, index < low + span)
        moved = jnp.where(inside, index + step, cells + 4 * span)
        result = jnp.where(mine, moved, result)
    return result


def chosen_slot(meta, way, slot, send):
    place = meta[0]
    offset = 1 if way < 2 else 2
    first = (place // offset) % 2 == 0
    base = 0 if way < 2 else 2
    near = meta[1 + (base + way % 2) * send + slot]
    far = meta[1 + (base + 1 - way % 2) * send + slot]
    return jnp.where(first, near, far)


def pick_rows(meta, field, outs, send, row=0):
    for way in range(4):
        for slot in range(send):
            block = chosen_slot(meta, way, slot, send)
            filled = (block >= 0).astype(jnp.float32)
            outs[way][row + slot : row + slot + 1, :] = (
                field[pl.ds(jnp.maximum(block, 0), 1), :] * filled
            )


def prepare(
    meta, thick, tracer, bottom, index, weight, ssh, forcing, index_out, weight_out, *outs,
    count, send,
):
    levels, cells = tracer.shape
    tiles = levels // SUBS
    blocks = cells // LANES
    rows = lax.broadcasted_iota(jnp.int32, (SUBS, LANES), 0)
    place = meta[0]
    thicks = [column(thick, k) for k in range(tiles)]
    for way in range(4):
        for slot in range(send):
            block = chosen_slot(meta, way, slot, send)
            safe = jnp.maximum(block, 0)
            depth = jnp.where(block >= 0, bottom[pl.ds(safe, 1), :], 0)
            at = pl.multiple_of(safe * LANES, LANES)
            for k in range(tiles):
                value = tracer[k * SUBS : (k + 1) * SUBS, pl.ds(at, LANES)]
                base = slot * levels + k * SUBS
                outs[way][base : base + SUBS, :] = jnp.where(rows + k * SUBS < depth, value, ABSENT)
    pick_rows(meta, ssh, outs, send, send * levels)
    for b in range(blocks):
        top = jnp.zeros((SUBS, LANES), jnp.float32)
        low = jnp.zeros((SUBS, LANES), jnp.float32)
        depth = bottom[b : b + 1, :]
        for k in range(tiles):
            layer = jnp.where(rows + k * SUBS < depth, thicks[k], 0.0)
            top = top + layer * tracer[k * SUBS : (k + 1) * SUBS, b * LANES : (b + 1) * LANES]
            low = low + layer
        forcing[b : b + 1, :] = jnp.sum(top, axis=0, keepdims=True) / jnp.sum(
            low, axis=0, keepdims=True
        )
    edges = index.shape[0]
    for b in range(blocks):
        for j in range(edges):
            row = index[j : j + 1, b * LANES : (b + 1) * LANES]
            index_out[j, b : b + 1, :] = row
            weight_out[j, b : b + 1, :] = weight[j : j + 1, b * LANES : (b + 1) * LANES]
    for j in range(edges):
        index_out[j] = localize(index_out[j], place, count, cells, send)


def advance(height, speed, total, forcing, index, weight, arrived, row, send):
    blocks = height.shape[0]
    own = height[...]
    laplace = jnp.zeros_like(own)
    for j in range(index.shape[0]):
        near = index[j]
        lane = jnp.bitwise_and(near, LANES - 1)
        block = jnp.right_shift(near, 7)
        got = jnp.zeros_like(own)
        for r in range(blocks + 4 * send):
            if r < blocks:
                source = height[r : r + 1, :]
            else:
                at = row + (r - blocks) % send
                source = arrived[(r - blocks) // send][at : at + 1, :]
            source = jnp.broadcast_to(source, own.shape)
            got = jnp.where(block == r, jnp.take_along_axis(source, lane, axis=1), got)
        laplace = laplace + weight[j] * (got - own)
    faster = (1.0 - friction) * speed[...] + barotropic_step * (laplace + forcing[...])
    return own + barotropic_step * faster, faster, total[...] + faster


def substep(
    meta, height, speed, total, forcing, index, weight, a, b, c, d, new_height, new_speed,
    new_total, *outs, row, send,
):
    new_height[...], new_speed[...], new_total[...] = advance(
        height, speed, total, forcing, index, weight, (a, b, c, d), row, send
    )
    pick_rows(meta, new_height, outs, send)


def last_substep(
    profile, height, speed, total, forcing, index, weight, a, b, c, d, bottom, base, new_height,
    new_speed, out, mean, *, row, send,
):
    new_height[...], new_speed[...], whole = advance(
        height, speed, total, forcing, index, weight, (a, b, c, d), row, send
    )
    mean[...] = whole / SUBSTEPS
    rows = lax.broadcasted_iota(jnp.int32, (SUBS, LANES), 0)
    for k in range(out.shape[0] // SUBS):
        shape = column(profile, k)
        for i in range(out.shape[1] // LANES):
            at = (slice(k * SUBS, (k + 1) * SUBS), slice(i * LANES, (i + 1) * LANES))
            added = jnp.where(rows + k * SUBS < bottom[i : i + 1, :], shape, 0.0)
            out[at] = base[at] + added * mean[i : i + 1, :]


def tracer_base(
    meta, tracer, bottom, index, weight, a, b, c, d, out, held, *, count, send
):
    levels, cells = tracer.shape
    tiles = levels // SUBS
    blocks = cells // LANES
    edges = index.shape[0]
    arrived = (a, b, c, d)
    rows = lax.broadcasted_iota(jnp.int32, (SUBS, LANES), 0)
    place = meta[0]
    for i in range(blocks):
        depth = bottom[i : i + 1, :]
        for k in range(tiles):
            at = (slice(k * SUBS, (k + 1) * SUBS), slice(i * LANES, (i + 1) * LANES))
            held[at] = jnp.where(rows + k * SUBS < depth, tracer[at], ABSENT)

    def cell_block(i, carry):
        at = pl.multiple_of(i * LANES, LANES)
        lanes = pl.ds(at, LANES)
        depth = bottom[pl.ds(i, 1), :]
        mine = [tracer[k * SUBS : (k + 1) * SUBS, lanes] for k in range(tiles)]
        flat = [jnp.zeros((SUBS, LANES), jnp.float32) for _ in range(tiles)]
        for j in range(edges):
            near = localize(index[j : j + 1, lanes], place, count, cells, send)
            near = jnp.broadcast_to(near, (SUBS, LANES))
            lane = jnp.bitwise_and(near, LANES - 1)
            block = jnp.right_shift(near, 7)
            factor = weight[j : j + 1, lanes]
            got = [jnp.full((SUBS, LANES), ABSENT, jnp.float32) for _ in range(tiles)]
            for r in range(blocks + 4 * send):
                here = block == r
                for k in range(tiles):
                    if r < blocks:
                        source = held[k * SUBS : (k + 1) * SUBS, r * LANES : (r + 1) * LANES]
                    else:
                        base = (r - blocks) % send * levels + k * SUBS
                        source = arrived[(r - blocks) // send][base : base + SUBS, :]
                    got[k] = jnp.where(here, jnp.take_along_axis(source, lane, axis=1), got[k])
            for k in range(tiles):
                flat[k] = flat[k] + factor * jnp.where(got[k] < PRESENT, got[k] - mine[k], 0.0)
        for k in range(tiles):
            first = rows + k * SUBS
            value = mine[k]
            up = pltpu.roll(value, SUBS - 1, 0)
            if k + 1 < tiles:
                up = jnp.where(rows == SUBS - 1, pltpu.roll(mine[k + 1], SUBS - 1, 0), up)
            down = pltpu.roll(value, 1, 0)
            if k > 0:
                down = jnp.where(rows == 0, pltpu.roll(mine[k - 1], 1, 0), down)
            below = jnp.where(first + 1 < jnp.minimum(depth, levels), up - value, 0.0)
            above = jnp.where(first > 0, down - value, 0.0)
            active = first < depth
            moved = horizontal_rate * flat[k] + vertical_rate * (below + above)
            out[k * SUBS : (k + 1) * SUBS, lanes] = value + tracer_step * jnp.where(
                active, moved, 0.0
            )
        return carry

    lax.fori_loop(0, blocks, cell_block, 0)


def shards(
    tracer, bottom_levels, neighbours, edge_weight, ssh, velocity, send_blocks, thickness, profile
):
    count = lax.axis_size("dom")
    levels, cells = tracer.shape
    send = send_blocks.shape[-1]
    edges = neighbours.shape[0]
    blocks = cells // LANES
    tile = (blocks, LANES)
    place = lax.axis_index("dom").astype(jnp.int32)
    meta = jnp.concatenate([place[None], send_blocks.reshape(-1)])
    bottom = bottom_levels.reshape(tile)
    height = ssh.reshape(tile)
    speed = velocity.reshape(tile)
    cell = jax.ShapeDtypeStruct(tile, jnp.float32)
    packed = send * levels + SUBS
    small = jax.ShapeDtypeStruct((send, LANES), jnp.float32)
    forcing, index, weight, *out = pl.pallas_call(
        functools.partial(prepare, count=count, send=send),
        out_shape=[
            cell,
            jax.ShapeDtypeStruct((edges,) + tile, jnp.int32),
            jax.ShapeDtypeStruct((edges,) + tile, jnp.float32),
        ]
        + [jax.ShapeDtypeStruct((packed, LANES), jnp.float32)] * 4,
        in_specs=[SMEM, SMEM] + [VMEM] * 5,
        cost_estimate=pl.CostEstimate(flops=4000000, bytes_accessed=600000, transcendentals=0),
        name="prepare",
    )(meta, thickness, tracer, bottom, neighbours, edge_weight, height)
    first = exchange(out, count)
    base = pl.pallas_call(
        functools.partial(tracer_base, count=count, send=send),
        out_shape=jax.ShapeDtypeStruct(tracer.shape, jnp.float32),
        in_specs=[SMEM] + [VMEM] * 8,
        scratch_shapes=[pltpu.VMEM(tracer.shape, jnp.float32)],
        cost_estimate=pl.CostEstimate(flops=20000000, bytes_accessed=800000, transcendentals=0),
        name="tracer_base",
    )(meta, tracer, bottom, neighbours, edge_weight, *first)
    total = jnp.zeros(tile, jnp.float32)
    arrived = first
    for number in range(SUBSTEPS - 1):
        row = send * levels if number == 0 else 0
        height, speed, total, *out = pl.pallas_call(
            functools.partial(substep, row=row, send=send),
            out_shape=[cell] * 3 + [small] * 4,
            in_specs=[SMEM] + [VMEM] * 10,
            cost_estimate=pl.CostEstimate(flops=500000, bytes_accessed=100000, transcendentals=0),
            name="substep",
        )(meta, height, speed, total, forcing, index, weight, *arrived)
        arrived = exchange(out, count)
    height, speed, result = pl.pallas_call(
        functools.partial(last_substep, row=0, send=send),
        out_shape=[cell, cell, jax.ShapeDtypeStruct(tracer.shape, jnp.float32)],
        in_specs=[SMEM] + [VMEM] * 12,
        scratch_shapes=[pltpu.VMEM(tile, jnp.float32)],
        cost_estimate=pl.CostEstimate(flops=1000000, bytes_accessed=500000, transcendentals=0),
        name="last_substep",
    )(profile, height, speed, total, forcing, index, weight, *arrived, bottom, base)
    return (result, height.reshape(-1), speed.reshape(-1))


def solution(mesh):
    placed = (
        P(None, "dom"),
        P("dom"),
        P(None, "dom"),
        P(None, "dom"),
        P("dom"),
        P("dom"),
        P("dom", None, None),
        P(),
        P(),
    )
    return jax.shard_map(
        shards,
        mesh=mesh,
        in_specs=placed,
        out_specs=(P(None, "dom"), P("dom"), P("dom")),
        check_vma=False,
    )
```

time: 443 us -> 76.6 us (0.17)
  local copies, waits for them, and re-layouts: 303 us -> 10.9 us
  starting transfers between devices: 110 us -> 34.4 us
  Pallas kernels: 0 us -> 18.6 us
  other arithmetic: 13.1 us -> 0.65 us
    gather x80 -> x0, local copies, waits for them, and re-layouts: 299 us -> none  [the longest x36 221 us: substep(): jnp.take(extended, neighbours[column]) - height]
    ppermute x32 -> x24, starting transfers between devices: 110 us -> 34.4 us  [exchange(): lax.ppermute(value, 'dom', way)]
    pallas_call x0 -> x8, Pallas kernels: none -> 18.6 us  [the longest x5 8.27 us: shards(): pl.pallas_call(functools.partial(substep, row=row, send=send), out_shape=...]
    unnamed x31 -> x91, local copies, waits for them, and re-layouts: 2.25 us -> 10.2 us
    add x13 -> x0, other arithmetic: 6.39 us -> none  [the longest x1 6.2 us: shards(): tracer + tracer_step * tendency]
    ppermute x32 -> x24, waiting for transfers between devices: 9.77 us -> 10.4 us  [exchange(): lax.ppermute(value, 'dom', way)]
  transfers between devices with their start and end apart: 32 -> 24, of which waited for: 6 -> 8; matrix products, arithmetic and copies ran while one was open for 64% -> 0% of each run, Pallas kernels for 0% -> 9%
where the time goes in v1:
time: 76.6 us; the launch traced here: 75.8 us
  starting transfers between devices  34.4 us (45%)
  Pallas kernels  18.6 us (24%)
  local copies, waits for them, and re-layouts  10.9 us (14%)
  waiting for transfers between devices  10.4 us (14%)
  between operations  0.89 us (1%)
    ppermute x24, starting transfers between devices, exchange(): lax.ppermute(value, 'dom', way)  34.4 us
    ppermute x24, waiting for transfers between devices, exchange(): lax.ppermute(value, 'dom', way)  10.4 us
    unnamed x91, local copies, waits for them, and re-layouts  10.2 us
    pallas_call x5, Pallas kernels, shards(): pl.pallas_call(functools.partial(substep, row=row, send=send), out_shape=...  8.27 us
    pallas_call x1, Pallas kernels, shards(): pl.pallas_call(functools.partial(tracer_base, count=count, send=send), ou...  6.69 us
    pallas_call x1, Pallas kernels, shards(): pl.pallas_call(functools.partial(last_substep, row=0, send=send), out_sha...  1.89 us
    pallas_call x1, Pallas kernels, shards(): pl.pallas_call(functools.partial(prepare, count=count, send=send), out_sh...  1.72 us
  transfers between devices with their start and end apart: 24, of which 8 were waited for; matrix products, arithmetic and copies ran while one was open for 0% of the time, Pallas kernels for 9%

profile of v1, /device:TPU:9, one launch (start us, length us, event | category | flops | bytes accessed | tf_op | source)
XLA Modules:
  0.0 75.8 jit_solution(7417092498680999447)
XLA Ops:
  0.6 0.7 copy-done.24
  1.3 0.1 copy.13
  1.4 0.1 reshape.24
  1.5 0.7 pad_add_fusion.meta
  2.1 1.7 %prepare.1 = (f32[8,128]{1,0:T(8,128)}, s32[6,8,128]{2,1,0:T(8,128)}, f32[6,8,128]{2,1,0:T(8,128)}, f32[88,128]{1,0:T(8,128)}, f32[88,128]{1,0:T(8,128)}, /*index=5*/f32[88,128]{1,0:T(8,128)}, f32[88,128]{1,0:T(8,128)}) custom-call(s32[9]{0:T(128)} %pad_add_fusion.meta, f32[40]{0:T(128)} %thick.1, f32[40,1024]{1,0:T(8,128)} %tracer.3, s32[8,128]{1,0:T(8,128)} %bitcast.6, ...), custom_call_target="tpu_custom_call" | custom-call | flops 4000000 | bytes 600000 | tf_op jit(solution)/shard_map/prepare/pallas_call | solution.py:256
  3.9 0.7 collective-permute-start
  4.5 1.2 %collective-permute-start.1 = (f32[88,128]{1,0:T(8,128)}, f32[88,128]{1,0:T(8,128)S(1)}, u32[]{:S(2)}, u32[]{:S(2)}) collective-permute-start(f32[88,128]{1,0:T(8,128)} %get-tuple-element.52), channel_id=1, source_target_pairs={{1,2},{3,4},{5,6},{7,8},{9,10},{11,12},{13,14},{15,16},{17,18},{19... | collective-permute-start | bytes 135176 | tf_op jit(solution)/shard_map/ppermute | solution.py:41
  5.7 1.2 %collective-permute-start.2 = (f32[88,128]{1,0:T(8,128)}, f32[88,128]{1,0:T(8,128)S(1)}, u32[]{:S(2)}, u32[]{:S(2)}) collective-permute-start(f32[88,128]{1,0:T(8,128)} %get-tuple-element.53), channel_id=1, source_target_pairs={{0,2},{1,3},{2,0},{3,1},{4,6},{5,7},{6,4},{7,5},{8,10},{9,11},{10,... | collective-permute-start | bytes 135176 | tf_op jit(solution)/shard_map/ppermute | solution.py:41
  6.9 1.1 %collective-permute-start.3 = (f32[88,128]{1,0:T(8,128)}, f32[88,128]{1,0:T(8,128)S(1)}, u32[]{:S(2)}, u32[]{:S(2)}) collective-permute-start(f32[88,128]{1,0:T(8,128)} %get-tuple-element.54), channel_id=1, source_target_pairs={{2,4},{3,5},{6,8},{7,9},{10,12},{11,13},{14,16},{15,17},{18,20},{1... | collective-permute-start | bytes 135176 | tf_op jit(solution)/shard_map/ppermute | solution.py:41
  8.0 0.0 collective-permute-done.a
  8.0 0.3 collective-permute-done.1.b
  8.4 1.1 %collective-permute-done.2.c = f32[88,128]{1,0:T(8,128)S(1)} collective-permute-done((f32[88,128]{1,0:T(8,128)}, f32[88,128]{1,0:T(8,128)S(1)}, u32[]{:S(2)}, u32[]{:S(2)}) %collective-permute-start.2) | collective-permute-done | bytes 45088 | tf_op jit(solution)/shard_map/ppermute | solution.py:41
  9.5 2.3 %collective-permute-done.3.d = f32[88,128]{1,0:T(8,128)S(1)} collective-permute-done((f32[88,128]{1,0:T(8,128)}, f32[88,128]{1,0:T(8,128)S(1)}, u32[]{:S(2)}, u32[]{:S(2)}) %collective-permute-start.3) | collective-permute-done | bytes 45088 | tf_op jit(solution)/shard_map/ppermute | solution.py:41
  11.8 0.6 broadcast_in_dim.7.total
  12.4 1.8 %substep.5 = (f32[8,128]{1,0:T(8,128)}, f32[8,128]{1,0:T(8,128)}, f32[8,128]{1,0:T(8,128)}, f32[2,128]{1,0:T(2,128)}, f32[2,128]{1,0:T(2,128)}, /*index=5*/f32[2,128]{1,0:T(2,128)}, f32[2,128]{1,0:T(2,128)}) custom-call(s32[9]{0:T(128)} %pad_add_fusion.meta, f32[8,128]{1,0:T(8,128)} %bitcast.10, f32[8,128]{1,0:T(8,128)} %bitcast.11, ...), custom_call_target="tpu_custom_call" | custom-call | flops 500000 | bytes 100000 | tf_op jit(solution)/shard_map/substep/pallas_call | solution.py:281
  14.2 0.7 copy-done.44
  14.9 1.2 %collective-permute-start.4 = (f32[2,128]{1,0:T(2,128)S(1)}, f32[2,128]{1,0:T(2,128)S(1)}, u32[]{:S(2)}, u32[]{:S(2)}) collective-permute-start(f32[2,128]{1,0:T(2,128)S(1)} %copy-done.44), channel_id=1, source_target_pairs={{0,1},{1,0},{2,3},{3,2},{4,5},{5,4},{6,7},{7,6},{8,9},{9,8},{10,11... | collective-permute-start | bytes 3080 | tf_op jit(solution)/shard_map/ppermute | solution.py:41
  16.1 1.4 %collective-permute-start.5 = (f32[2,128]{1,0:T(2,128)S(1)}, f32[2,128]{1,0:T(2,128)S(1)}, u32[]{:S(2)}, u32[]{:S(2)}) collective-permute-start(f32[2,128]{1,0:T(2,128)S(1)} %copy-done.43), channel_id=1, source_target_pairs={{1,2},{3,4},{5,6},{7,8},{9,10},{11,12},{13,14},{15,16},{17,18},{19... | collective-permute-start | bytes 3080 | tf_op jit(solution)/shard_map/ppermute | solution.py:41
  17.5 0.7 collective-permute-start.6
  18.2 2.6 %collective-permute-start.7 = (f32[2,128]{1,0:T(2,128)S(1)}, f32[2,128]{1,0:T(2,128)S(1)}, u32[]{:S(2)}, u32[]{:S(2)}) collective-permute-start(f32[2,128]{1,0:T(2,128)S(1)} %copy-done.35), channel_id=1, source_target_pairs={{2,4},{3,5},{6,8},{7,9},{10,12},{11,13},{14,16},{15,17},{18,20},{1... | collective-permute-start | bytes 3080 | tf_op jit(solution)/shard_map/ppermute | solution.py:41
  20.9 0.0 collective-permute-done.4.a
  20.9 0.0 collective-permute-done.6.c
  20.9 1.5 %collective-permute-done.7.d = f32[2,128]{1,0:T(2,128)S(1)} collective-permute-done((f32[2,128]{1,0:T(2,128)S(1)}, f32[2,128]{1,0:T(2,128)S(1)}, u32[]{:S(2)}, u32[]{:S(2)}) %collective-permute-start.7) | collective-permute-done | bytes 1056 | tf_op jit(solution)/shard_map/ppermute | solution.py:41
  22.5 0.6 copy-done.20
  23.0 1.6 %substep.6 = (f32[8,128]{1,0:T(8,128)}, f32[8,128]{1,0:T(8,128)}, f32[8,128]{1,0:T(8,128)}, f32[2,128]{1,0:T(2,128)}, f32[2,128]{1,0:T(2,128)}, /*index=5*/f32[2,128]{1,0:T(2,128)}, f32[2,128]{1,0:T(2,128)}) custom-call(s32[9]{0:T(128)} %pad_add_fusion.meta, f32[8,128]{1,0:T(8,128)} %get-tuple-element.55.height, f32[8,128]{1,0:T(8,128)} %get-tuple-element.56.speed, ...), custom_call_target="tpu_custom_call" | custom-call | flops 500000 | bytes 100000 | tf_op jit(solution)/shard_map/substep/pallas_call | solution.py:281
  24.7 0.7 copy-done.40
  25.3 0.1 collective-permute-start.10
  25.4 0.6 copy-done.36
  26.0 2.6 %collective-permute-start.11 = (f32[2,128]{1,0:T(2,128)S(1)}, f32[2,128]{1,0:T(2,128)S(1)}, u32[]{:S(2)}, u32[]{:S(2)}) collective-permute-start(f32[2,128]{1,0:T(2,128)S(1)} %copy-done.36), channel_id=1, source_target_pairs={{2,4},{3,5},{6,8},{7,9},{10,12},{11,13},{14,16},{15,17},{18,20},{1... | collective-permute-start | bytes 3080 | tf_op jit(solution)/shard_map/ppermute | solution.py:41
  28.7 3.6 %collective-permute-start.8 = (f32[2,128]{1,0:T(2,128)S(1)}, f32[2,128]{1,0:T(2,128)S(1)}, u32[]{:S(2)}, u32[]{:S(2)}) collective-permute-start(f32[2,128]{1,0:T(2,128)S(1)} %copy-done.31), channel_id=1, source_target_pairs={{0,1},{1,0},{2,3},{3,2},{4,5},{5,4},{6,7},{7,6},{8,9},{9,8},{10,11... | collective-permute-start | bytes 3080 | tf_op jit(solution)/shard_map/ppermute | solution.py:41
  32.3 0.0 collective-permute-start.9
  32.3 0.8 %collective-permute-done.8.a = f32[2,128]{1,0:T(2,128)S(1)} collective-permute-done((f32[2,128]{1,0:T(2,128)S(1)}, f32[2,128]{1,0:T(2,128)S(1)}, u32[]{:S(2)}, u32[]{:S(2)}) %collective-permute-start.8) | collective-permute-done | bytes 1056 | tf_op jit(solution)/shard_map/ppermute | solution.py:41
  33.1 2.2 %collective-permute-done.9.b = f32[2,128]{1,0:T(2,128)S(1)} collective-permute-done((f32[2,128]{1,0:T(2,128)S(1)}, f32[2,128]{1,0:T(2,128)S(1)}, u32[]{:S(2)}, u32[]{:S(2)}) %collective-permute-start.9) | collective-permute-done | bytes 1056 | tf_op jit(solution)/shard_map/ppermute | solution.py:41
  35.3 0.5 copy-done.21
  35.8 1.6 %substep.7 = (f32[8,128]{1,0:T(8,128)}, f32[8,128]{1,0:T(8,128)}, f32[8,128]{1,0:T(8,128)}, f32[2,128]{1,0:T(2,128)}, f32[2,128]{1,0:T(2,128)}, /*index=5*/f32[2,128]{1,0:T(2,128)}, f32[2,128]{1,0:T(2,128)}) custom-call(s32[9]{0:T(128)} %pad_add_fusion.meta, f32[8,128]{1,0:T(8,128)} %get-tuple-element.62.height, f32[8,128]{1,0:T(8,128)} %get-tuple-element.63.speed, ...), custom_call_target="tpu_custom_call" | custom-call | flops 500000 | bytes 100000 | tf_op jit(solution)/shard_map/substep/pallas_call | solution.py:281
  37.5 0.7 copy-done.41
  38.1 2.5 %collective-permute-start.12 = (f32[2,128]{1,0:T(2,128)S(1)}, f32[2,128]{1,0:T(2,128)S(1)}, u32[]{:S(2)}, u32[]{:S(2)}) collective-permute-start(f32[2,128]{1,0:T(2,128)S(1)} %copy-done.41), channel_id=1, source_target_pairs={{0,1},{1,0},{2,3},{3,2},{4,5},{5,4},{6,7},{7,6},{8,9},{9,8},{10,11... | collective-permute-start | bytes 3080 | tf_op jit(solution)/shard_map/ppermute | solution.py:41
  40.6 0.7 copy-done.32
  41.3 0.7 copy-done.28
  42.0 3.1 %collective-permute-start.15 = (f32[2,128]{1,0:T(2,128)S(1)}, f32[2,128]{1,0:T(2,128)S(1)}, u32[]{:S(2)}, u32[]{:S(2)}) collective-permute-start(f32[2,128]{1,0:T(2,128)S(1)} %copy-done.28), channel_id=1, source_target_pairs={{2,4},{3,5},{6,8},{7,9},{10,12},{11,13},{14,16},{15,17},{18,20},{1... | collective-permute-start | bytes 3080 | tf_op jit(solution)/shard_map/ppermute | solution.py:41
  45.1 1.0 %collective-permute-done.15.d = f32[2,128]{1,0:T(2,128)S(1)} collective-permute-done((f32[2,128]{1,0:T(2,128)S(1)}, f32[2,128]{1,0:T(2,128)S(1)}, u32[]{:S(2)}, u32[]{:S(2)}) %collective-permute-start.15) | collective-permute-done | bytes 1056 | tf_op jit(solution)/shard_map/ppermute | solution.py:41
  46.2 0.6 copy-done.22
  46.8 1.6 %substep.8 = (f32[8,128]{1,0:T(8,128)}, f32[8,128]{1,0:T(8,128)}, f32[8,128]{1,0:T(8,128)}, f32[2,128]{1,0:T(2,128)}, f32[2,128]{1,0:T(2,128)}, /*index=5*/f32[2,128]{1,0:T(2,128)}, f32[2,128]{1,0:T(2,128)}) custom-call(s32[9]{0:T(128)} %pad_add_fusion.meta, f32[8,128]{1,0:T(8,128)} %get-tuple-element.69.height, f32[8,128]{1,0:T(8,128)} %get-tuple-element.70.speed, ...), custom_call_target="tpu_custom_call" | custom-call | flops 500000 | bytes 100000 | tf_op jit(solution)/shard_map/substep/pallas_call | solution.py:281
  48.4 0.7 copy-done.42
  49.1 1.9 %collective-permute-start.16 = (f32[2,128]{1,0:T(2,128)S(1)}, f32[2,128]{1,0:T(2,128)S(1)}, u32[]{:S(2)}, u32[]{:S(2)}) collective-permute-start(f32[2,128]{1,0:T(2,128)S(1)} %copy-done.42), channel_id=1, source_target_pairs={{0,1},{1,0},{2,3},{3,2},{4,5},{5,4},{6,7},{7,6},{8,9},{9,8},{10,11... | collective-permute-start | bytes 3080 | tf_op jit(solution)/shard_map/ppermute | solution.py:41
  51.0 0.6 collective-permute-start.17
  51.6 0.1 copy-done.33
  51.7 0.0 collective-permute-start.18
  51.7 0.6 copy-done.29
  52.4 3.1 %collective-permute-start.19 = (f32[2,128]{1,0:T(2,128)S(1)}, f32[2,128]{1,0:T(2,128)S(1)}, u32[]{:S(2)}, u32[]{:S(2)}) collective-permute-start(f32[2,128]{1,0:T(2,128)S(1)} %copy-done.29), channel_id=1, source_target_pairs={{2,4},{3,5},{6,8},{7,9},{10,12},{11,13},{14,16},{15,17},{18,20},{1... | collective-permute-start | bytes 3080 | tf_op jit(solution)/shard_map/ppermute | solution.py:41
  55.5 1.0 %collective-permute-done.19.d = f32[2,128]{1,0:T(2,128)S(1)} collective-permute-done((f32[2,128]{1,0:T(2,128)S(1)}, f32[2,128]{1,0:T(2,128)S(1)}, u32[]{:S(2)}, u32[]{:S(2)}) %collective-permute-start.19) | collective-permute-done | bytes 1056 | tf_op jit(solution)/shard_map/ppermute | solution.py:41
  56.6 0.5 copy-done.23
  57.1 1.6 %substep.9 = (f32[8,128]{1,0:T(8,128)}, f32[8,128]{1,0:T(8,128)}, f32[8,128]{1,0:T(8,128)}, f32[2,128]{1,0:T(2,128)}, f32[2,128]{1,0:T(2,128)}, /*index=5*/f32[2,128]{1,0:T(2,128)}, f32[2,128]{1,0:T(2,128)}) custom-call(s32[9]{0:T(128)} %pad_add_fusion.meta, f32[8,128]{1,0:T(8,128)} %get-tuple-element.76.height, f32[8,128]{1,0:T(8,128)} %get-tuple-element.77.speed, ...), custom_call_target="tpu_custom_call" | custom-call | flops 500000 | bytes 100000 | tf_op jit(solution)/shard_map/substep/pallas_call | solution.py:281
  58.7 0.6 copy-done.34
  59.4 2.7 %collective-permute-start.20 = (f32[2,128]{1,0:T(2,128)S(1)}, f32[2,128]{1,0:T(2,128)S(1)}, u32[]{:S(2)}, u32[]{:S(2)}) collective-permute-start(f32[2,128]{1,0:T(2,128)S(1)} %copy-done.34), channel_id=1, source_target_pairs={{0,1},{1,0},{2,3},{3,2},{4,5},{5,4},{6,7},{7,6},{8,9},{9,8},{10,11... | collective-permute-start | bytes 3080 | tf_op jit(solution)/shard_map/ppermute | solution.py:41
  62.1 0.7 collective-permute-start.21
  62.8 0.1 collective-permute-start.22
  63.0 0.6 copy-done.25
  63.5 3.1 %collective-permute-start.23 = (f32[2,128]{1,0:T(2,128)S(1)}, f32[2,128]{1,0:T(2,128)S(1)}, u32[]{:S(2)}, u32[]{:S(2)}) collective-permute-start(f32[2,128]{1,0:T(2,128)S(1)} %copy-done.25), channel_id=1, source_target_pairs={{2,4},{3,5},{6,8},{7,9},{10,12},{11,13},{14,16},{15,17},{18,20},{1... | collective-permute-start | bytes 3080 | tf_op jit(solution)/shard_map/ppermute | solution.py:41
  66.6 6.7 %tracer_base.1.base = f32[40,1024]{1,0:T(8,128)} custom-call(s32[9]{0:T(128)} %pad_add_fusion.meta, f32[40,1024]{1,0:T(8,128)} %tracer.3, s32[8,128]{1,0:T(8,128)} %bitcast.7, s32[6,1024]{1,0:T(8,128)} %index.3, f32[6,1024]{1,0:T(8,128)} %weight.3, f32[88,128]{1,0:T(8,128)} %copy-done, f32[88,128]{1,0:T(8,128)} %copy-done.1, f32[88,128]{1,0:T(8,128)} %copy-done.2, ...), custom_call_target="tpu_custom_call" | custom-call | flops 20000000 | bytes 800000 | tf_op jit(solution)/shard_map/tracer_base/pallas_call | solution.py:269
  73.4 0.5 copy-done.4
  73.9 0.0 copy-done.10
  73.9 0.0 copy-done.15
  73.9 1.9 %last_substep.1 = (f32[8,128]{1,0:T(8,128)}, f32[8,128]{1,0:T(8,128)}, f32[40,1024]{1,0:T(8,128)}) custom-call(f32[40]{0:T(128)} %profile.1, f32[8,128]{1,0:T(8,128)} %get-tuple-element.83.height, f32[8,128]{1,0:T(8,128)} %get-tuple-element.84.speed, f32[8,128]{1,0:T(8,128)} %get-tuple-element.85.total, f32[8,128]{1,0:T(8,128)} %get-tuple-element.48.forcing, ...), custom_call_target="tpu_custom_call" | custom-call | flops 1000000 | bytes 500000 | tf_op jit(solution)/shard_map/last_substep/pallas_call | solution.py:289
  (86 shorter events, 0.2 us)
Async XLA Ops:
  0.6 0.7 copy-start.24
  3.9 4.2 %collective-permute-start = (f32[88,128]{1,0:T(8,128)}, f32[88,128]{1,0:T(8,128)S(1)}, u32[]{:S(2)}, u32[]{:S(2)}) collective-permute-start(f32[88,128]{1,0:T(8,128)} %get-tuple-element.51), channel_id=1, source_target_pairs={{0,1},{1,0},{2,3},{3,2},{4,5},{5,4},{6,7},{7,6},{8,9},{9,8},{10,11... | collective-permute-start | bytes 135176 | tf_op jit(solution)/shard_map/ppermute | solution.py:41
  4.5 3.8 %collective-permute-start.1 = (f32[88,128]{1,0:T(8,128)}, f32[88,128]{1,0:T(8,128)S(1)}, u32[]{:S(2)}, u32[]{:S(2)}) collective-permute-start(f32[88,128]{1,0:T(8,128)} %get-tuple-element.52), channel_id=1, source_target_pairs={{1,2},{3,4},{5,6},{7,8},{9,10},{11,12},{13,14},{15,16},{17,18},{19... | collective-permute-start | bytes 135176 | tf_op jit(solution)/shard_map/ppermute | solution.py:41
  5.7 3.8 %collective-permute-start.2 = (f32[88,128]{1,0:T(8,128)}, f32[88,128]{1,0:T(8,128)S(1)}, u32[]{:S(2)}, u32[]{:S(2)}) collective-permute-start(f32[88,128]{1,0:T(8,128)} %get-tuple-element.53), channel_id=1, source_target_pairs={{0,2},{1,3},{2,0},{3,1},{4,6},{5,7},{6,4},{7,5},{8,10},{9,11},{10,... | collective-permute-start | bytes 135176 | tf_op jit(solution)/shard_map/ppermute | solution.py:41
  6.9 4.9 %collective-permute-start.3 = (f32[88,128]{1,0:T(8,128)}, f32[88,128]{1,0:T(8,128)S(1)}, u32[]{:S(2)}, u32[]{:S(2)}) collective-permute-start(f32[88,128]{1,0:T(8,128)} %get-tuple-element.54), channel_id=1, source_target_pairs={{2,4},{3,5},{6,8},{7,9},{10,12},{11,13},{14,16},{15,17},{18,20},{1... | collective-permute-start | bytes 135176 | tf_op jit(solution)/shard_map/ppermute | solution.py:41
  8.0 4.4 %copy-start = (f32[88,128]{1,0:T(8,128)}, f32[88,128]{1,0:T(8,128)S(1)}, u32[]{:S(2)}) copy-start(f32[88,128]{1,0:T(8,128)S(1)} %collective-permute-done.a) | copy-start | bytes 135172
  8.4 4.1 %copy-start.1 = (f32[88,128]{1,0:T(8,128)}, f32[88,128]{1,0:T(8,128)S(1)}, u32[]{:S(2)}) copy-start(f32[88,128]{1,0:T(8,128)S(1)} %collective-permute-done.1.b) | copy-start | bytes 135172
  9.5 3.0 %copy-start.2 = (f32[88,128]{1,0:T(8,128)}, f32[88,128]{1,0:T(8,128)S(1)}, u32[]{:S(2)}) copy-start(f32[88,128]{1,0:T(8,128)S(1)} %collective-permute-done.2.c) | copy-start | bytes 135172
  11.8 0.6 copy-start.3
  14.2 0.7 copy-start.44
  14.9 1.2 %copy-start.43 = (f32[2,128]{1,0:T(2,128)S(1)}, f32[2,128]{1,0:T(2,128)}, u32[]{:S(2)}) copy-start(f32[2,128]{1,0:T(2,128)} %get-tuple-element.59) | copy-start | bytes 3076
  14.9 6.0 %collective-permute-start.4 = (f32[2,128]{1,0:T(2,128)S(1)}, f32[2,128]{1,0:T(2,128)S(1)}, u32[]{:S(2)}, u32[]{:S(2)}) collective-permute-start(f32[2,128]{1,0:T(2,128)S(1)} %copy-done.44), channel_id=1, source_target_pairs={{0,1},{1,0},{2,3},{3,2},{4,5},{5,4},{6,7},{7,6},{8,9},{9,8},{10,11... | collective-permute-start | bytes 3080 | tf_op jit(solution)/shard_map/ppermute | solution.py:41
  16.1 1.4 %copy-start.39 = (f32[2,128]{1,0:T(2,128)S(1)}, f32[2,128]{1,0:T(2,128)}, u32[]{:S(2)}) copy-start(f32[2,128]{1,0:T(2,128)} %get-tuple-element.60) | copy-start | bytes 3076
  16.1 4.7 %collective-permute-start.5 = (f32[2,128]{1,0:T(2,128)S(1)}, f32[2,128]{1,0:T(2,128)S(1)}, u32[]{:S(2)}, u32[]{:S(2)}) collective-permute-start(f32[2,128]{1,0:T(2,128)S(1)} %copy-done.43), channel_id=1, source_target_pairs={{1,2},{3,4},{5,6},{7,8},{9,10},{11,12},{13,14},{15,16},{17,18},{19... | collective-permute-start | bytes 3080 | tf_op jit(solution)/shard_map/ppermute | solution.py:41
  17.5 0.7 copy-start.35
  17.5 3.3 %collective-permute-start.6 = (f32[2,128]{1,0:T(2,128)S(1)}, f32[2,128]{1,0:T(2,128)S(1)}, u32[]{:S(2)}, u32[]{:S(2)}) collective-permute-start(f32[2,128]{1,0:T(2,128)S(1)} %copy-done.39), channel_id=1, source_target_pairs={{0,2},{1,3},{2,0},{3,1},{4,6},{5,7},{6,4},{7,5},{8,10},{9,11},{10,... | collective-permute-start | bytes 3080 | tf_op jit(solution)/shard_map/ppermute | solution.py:41
  18.2 4.2 %collective-permute-start.7 = (f32[2,128]{1,0:T(2,128)S(1)}, f32[2,128]{1,0:T(2,128)S(1)}, u32[]{:S(2)}, u32[]{:S(2)}) collective-permute-start(f32[2,128]{1,0:T(2,128)S(1)} %copy-done.35), channel_id=1, source_target_pairs={{2,4},{3,5},{6,8},{7,9},{10,12},{11,13},{14,16},{15,17},{18,20},{1... | collective-permute-start | bytes 3080 | tf_op jit(solution)/shard_map/ppermute | solution.py:41
  20.9 1.6 %copy-start.6 = (f32[2,128]{1,0:T(2,128)}, f32[2,128]{1,0:T(2,128)S(1)}, u32[]{:S(2)}) copy-start(f32[2,128]{1,0:T(2,128)S(1)} %collective-permute-done.4.a) | copy-start | bytes 3076
  20.9 1.6 %copy-start.11 = (f32[2,128]{1,0:T(2,128)}, f32[2,128]{1,0:T(2,128)S(1)}, u32[]{:S(2)}) copy-start(f32[2,128]{1,0:T(2,128)S(1)} %collective-permute-done.5.b) | copy-start | bytes 3076
  20.9 1.6 %copy-start.16 = (f32[2,128]{1,0:T(2,128)}, f32[2,128]{1,0:T(2,128)S(1)}, u32[]{:S(2)}) copy-start(f32[2,128]{1,0:T(2,128)S(1)} %collective-permute-done.6.c) | copy-start | bytes 3076
  22.4 0.6 copy-start.20
  24.7 0.7 copy-start.40
  25.3 0.7 copy-start.36
  25.3 7.0 %collective-permute-start.10 = (f32[2,128]{1,0:T(2,128)S(1)}, f32[2,128]{1,0:T(2,128)S(1)}, u32[]{:S(2)}, u32[]{:S(2)}) collective-permute-start(f32[2,128]{1,0:T(2,128)S(1)} %copy-done.40), channel_id=1, source_target_pairs={{0,2},{1,3},{2,0},{3,1},{4,6},{5,7},{6,4},{7,5},{8,10},{9,11},{10,... | collective-permute-start | bytes 3080 | tf_op jit(solution)/shard_map/ppermute | solution.py:41
  26.0 2.6 %copy-start.31 = (f32[2,128]{1,0:T(2,128)S(1)}, f32[2,128]{1,0:T(2,128)}, u32[]{:S(2)}) copy-start(f32[2,128]{1,0:T(2,128)} %get-tuple-element.65) | copy-start | bytes 3076
  26.0 6.3 %collective-permute-start.11 = (f32[2,128]{1,0:T(2,128)S(1)}, f32[2,128]{1,0:T(2,128)S(1)}, u32[]{:S(2)}, u32[]{:S(2)}) collective-permute-start(f32[2,128]{1,0:T(2,128)S(1)} %copy-done.36), channel_id=1, source_target_pairs={{2,4},{3,5},{6,8},{7,9},{10,12},{11,13},{14,16},{15,17},{18,20},{1... | collective-permute-start | bytes 3080 | tf_op jit(solution)/shard_map/ppermute | solution.py:41
  28.6 3.6 %copy-start.27 = (f32[2,128]{1,0:T(2,128)S(1)}, f32[2,128]{1,0:T(2,128)}, u32[]{:S(2)}) copy-start(f32[2,128]{1,0:T(2,128)} %get-tuple-element.66) | copy-start | bytes 3076
  28.7 4.5 %collective-permute-start.8 = (f32[2,128]{1,0:T(2,128)S(1)}, f32[2,128]{1,0:T(2,128)S(1)}, u32[]{:S(2)}, u32[]{:S(2)}) collective-permute-start(f32[2,128]{1,0:T(2,128)S(1)} %copy-done.31), channel_id=1, source_target_pairs={{0,1},{1,0},{2,3},{3,2},{4,5},{5,4},{6,7},{7,6},{8,9},{9,8},{10,11... | collective-permute-start | bytes 3080 | tf_op jit(solution)/shard_map/ppermute | solution.py:41
  32.3 3.0 %collective-permute-start.9 = (f32[2,128]{1,0:T(2,128)S(1)}, f32[2,128]{1,0:T(2,128)S(1)}, u32[]{:S(2)}, u32[]{:S(2)}) collective-permute-start(f32[2,128]{1,0:T(2,128)S(1)} %copy-done.27), channel_id=1, source_target_pairs={{1,2},{3,4},{5,6},{7,8},{9,10},{11,12},{13,14},{15,16},{17,18},{19... | collective-permute-start | bytes 3080 | tf_op jit(solution)/shard_map/ppermute | solution.py:41
  32.3 3.0 %copy-start.7 = (f32[2,128]{1,0:T(2,128)}, f32[2,128]{1,0:T(2,128)S(1)}, u32[]{:S(2)}) copy-start(f32[2,128]{1,0:T(2,128)S(1)} %collective-permute-done.10.c) | copy-start | bytes 3076
  32.3 3.0 %copy-start.12 = (f32[2,128]{1,0:T(2,128)}, f32[2,128]{1,0:T(2,128)S(1)}, u32[]{:S(2)}) copy-start(f32[2,128]{1,0:T(2,128)S(1)} %collective-permute-done.11.d) | copy-start | bytes 3076
  33.1 2.2 %copy-start.17 = (f32[2,128]{1,0:T(2,128)}, f32[2,128]{1,0:T(2,128)S(1)}, u32[]{:S(2)}) copy-start(f32[2,128]{1,0:T(2,128)S(1)} %collective-permute-done.8.a) | copy-start | bytes 3076
  37.5 0.7 copy-start.41
  38.1 2.5 %copy-start.37 = (f32[2,128]{1,0:T(2,128)S(1)}, f32[2,128]{1,0:T(2,128)}, u32[]{:S(2)}) copy-start(f32[2,128]{1,0:T(2,128)} %get-tuple-element.73) | copy-start | bytes 3076
  38.1 7.0 %collective-permute-start.12 = (f32[2,128]{1,0:T(2,128)S(1)}, f32[2,128]{1,0:T(2,128)S(1)}, u32[]{:S(2)}, u32[]{:S(2)}) collective-permute-start(f32[2,128]{1,0:T(2,128)S(1)} %copy-done.41), channel_id=1, source_target_pairs={{0,1},{1,0},{2,3},{3,2},{4,5},{5,4},{6,7},{7,6},{8,9},{9,8},{10,11... | collective-permute-start | bytes 3080 | tf_op jit(solution)/shard_map/ppermute | solution.py:41
  40.6 0.7 copy-start.32
  40.6 4.5 %collective-permute-start.13 = (f32[2,128]{1,0:T(2,128)S(1)}, f32[2,128]{1,0:T(2,128)S(1)}, u32[]{:S(2)}, u32[]{:S(2)}) collective-permute-start(f32[2,128]{1,0:T(2,128)S(1)} %copy-done.37), channel_id=1, source_target_pairs={{1,2},{3,4},{5,6},{7,8},{9,10},{11,12},{13,14},{15,16},{17,18},{19... | collective-permute-start | bytes 3080 | tf_op jit(solution)/shard_map/ppermute | solution.py:41
  41.3 0.7 copy-start.28
  41.3 3.8 %collective-permute-start.14 = (f32[2,128]{1,0:T(2,128)S(1)}, f32[2,128]{1,0:T(2,128)S(1)}, u32[]{:S(2)}, u32[]{:S(2)}) collective-permute-start(f32[2,128]{1,0:T(2,128)S(1)} %copy-done.32), channel_id=1, source_target_pairs={{0,2},{1,3},{2,0},{3,1},{4,6},{5,7},{6,4},{7,5},{8,10},{9,11},{10,... | collective-permute-start | bytes 3080 | tf_op jit(solution)/shard_map/ppermute | solution.py:41
  42.0 4.2 %collective-permute-start.15 = (f32[2,128]{1,0:T(2,128)S(1)}, f32[2,128]{1,0:T(2,128)S(1)}, u32[]{:S(2)}, u32[]{:S(2)}) collective-permute-start(f32[2,128]{1,0:T(2,128)S(1)} %copy-done.28), channel_id=1, source_target_pairs={{2,4},{3,5},{6,8},{7,9},{10,12},{11,13},{14,16},{15,17},{18,20},{1... | collective-permute-start | bytes 3080 | tf_op jit(solution)/shard_map/ppermute | solution.py:41
  45.1 1.1 %copy-start.8 = (f32[2,128]{1,0:T(2,128)}, f32[2,128]{1,0:T(2,128)S(1)}, u32[]{:S(2)}) copy-start(f32[2,128]{1,0:T(2,128)S(1)} %collective-permute-done.12.a) | copy-start | bytes 3076
  45.1 1.1 %copy-start.13 = (f32[2,128]{1,0:T(2,128)}, f32[2,128]{1,0:T(2,128)S(1)}, u32[]{:S(2)}) copy-start(f32[2,128]{1,0:T(2,128)S(1)} %collective-permute-done.13.b) | copy-start | bytes 3076
  45.1 1.1 %copy-start.18 = (f32[2,128]{1,0:T(2,128)}, f32[2,128]{1,0:T(2,128)S(1)}, u32[]{:S(2)}) copy-start(f32[2,128]{1,0:T(2,128)S(1)} %collective-permute-done.14.c) | copy-start | bytes 3076
  46.2 0.6 copy-start.22
  48.4 0.7 copy-start.42
  49.0 1.9 %copy-start.38 = (f32[2,128]{1,0:T(2,128)S(1)}, f32[2,128]{1,0:T(2,128)}, u32[]{:S(2)}) copy-start(f32[2,128]{1,0:T(2,128)} %get-tuple-element.80) | copy-start | bytes 3076
  49.1 6.4 %collective-permute-start.16 = (f32[2,128]{1,0:T(2,128)S(1)}, f32[2,128]{1,0:T(2,128)S(1)}, u32[]{:S(2)}, u32[]{:S(2)}) collective-permute-start(f32[2,128]{1,0:T(2,128)S(1)} %copy-done.42), channel_id=1, source_target_pairs={{0,1},{1,0},{2,3},{3,2},{4,5},{5,4},{6,7},{7,6},{8,9},{9,8},{10,11... | collective-permute-start | bytes 3080 | tf_op jit(solution)/shard_map/ppermute | solution.py:41
  51.0 0.7 copy-start.33
  51.0 4.5 %collective-permute-start.17 = (f32[2,128]{1,0:T(2,128)S(1)}, f32[2,128]{1,0:T(2,128)S(1)}, u32[]{:S(2)}, u32[]{:S(2)}) collective-permute-start(f32[2,128]{1,0:T(2,128)S(1)} %copy-done.38), channel_id=1, source_target_pairs={{1,2},{3,4},{5,6},{7,8},{9,10},{11,12},{13,14},{15,16},{17,18},{19... | collective-permute-start | bytes 3080 | tf_op jit(solution)/shard_map/ppermute | solution.py:41
  51.7 0.7 copy-start.29
  51.7 3.8 %collective-permute-start.18 = (f32[2,128]{1,0:T(2,128)S(1)}, f32[2,128]{1,0:T(2,128)S(1)}, u32[]{:S(2)}, u32[]{:S(2)}) collective-permute-start(f32[2,128]{1,0:T(2,128)S(1)} %copy-done.33), channel_id=1, source_target_pairs={{0,2},{1,3},{2,0},{3,1},{4,6},{5,7},{6,4},{7,5},{8,10},{9,11},{10,... | collective-permute-start | bytes 3080 | tf_op jit(solution)/shard_map/ppermute | solution.py:41
  52.4 4.2 %collective-permute-start.19 = (f32[2,128]{1,0:T(2,128)S(1)}, f32[2,128]{1,0:T(2,128)S(1)}, u32[]{:S(2)}, u32[]{:S(2)}) collective-permute-start(f32[2,128]{1,0:T(2,128)S(1)} %copy-done.29), channel_id=1, source_target_pairs={{2,4},{3,5},{6,8},{7,9},{10,12},{11,13},{14,16},{15,17},{18,20},{1... | collective-permute-start | bytes 3080 | tf_op jit(solution)/shard_map/ppermute | solution.py:41
  55.5 1.1 %copy-start.9 = (f32[2,128]{1,0:T(2,128)}, f32[2,128]{1,0:T(2,128)S(1)}, u32[]{:S(2)}) copy-start(f32[2,128]{1,0:T(2,128)S(1)} %collective-permute-done.16.a) | copy-start | bytes 3076
  55.5 1.1 %copy-start.14 = (f32[2,128]{1,0:T(2,128)}, f32[2,128]{1,0:T(2,128)S(1)}, u32[]{:S(2)}) copy-start(f32[2,128]{1,0:T(2,128)S(1)} %collective-permute-done.17.b) | copy-start | bytes 3076
  55.5 1.1 %copy-start.19 = (f32[2,128]{1,0:T(2,128)}, f32[2,128]{1,0:T(2,128)S(1)}, u32[]{:S(2)}) copy-start(f32[2,128]{1,0:T(2,128)S(1)} %collective-permute-done.18.c) | copy-start | bytes 3076
  58.7 0.6 copy-start.34
  59.4 2.7 %copy-start.30 = (f32[2,128]{1,0:T(2,128)S(1)}, f32[2,128]{1,0:T(2,128)}, u32[]{:S(2)}) copy-start(f32[2,128]{1,0:T(2,128)} %get-tuple-element.87) | copy-start | bytes 3076
  59.4 13.9 %collective-permute-start.20 = (f32[2,128]{1,0:T(2,128)S(1)}, f32[2,128]{1,0:T(2,128)S(1)}, u32[]{:S(2)}, u32[]{:S(2)}) collective-permute-start(f32[2,128]{1,0:T(2,128)S(1)} %copy-done.34), channel_id=1, source_target_pairs={{0,1},{1,0},{2,3},{3,2},{4,5},{5,4},{6,7},{7,6},{8,9},{9,8},{10,11... | collective-permute-start | bytes 3080 | tf_op jit(solution)/shard_map/ppermute | solution.py:41
  62.1 0.7 copy-start.26
  62.1 11.2 %collective-permute-start.21 = (f32[2,128]{1,0:T(2,128)S(1)}, f32[2,128]{1,0:T(2,128)S(1)}, u32[]{:S(2)}, u32[]{:S(2)}) collective-permute-start(f32[2,128]{1,0:T(2,128)S(1)} %copy-done.30), channel_id=1, source_target_pairs={{1,2},{3,4},{5,6},{7,8},{9,10},{11,12},{13,14},{15,16},{17,18},{19... | collective-permute-start | bytes 3080 | tf_op jit(solution)/shard_map/ppermute | solution.py:41
  62.8 0.7 copy-start.25
  62.8 10.5 %collective-permute-start.22 = (f32[2,128]{1,0:T(2,128)S(1)}, f32[2,128]{1,0:T(2,128)S(1)}, u32[]{:S(2)}, u32[]{:S(2)}) collective-permute-start(f32[2,128]{1,0:T(2,128)S(1)} %copy-done.26), channel_id=1, source_target_pairs={{0,2},{1,3},{2,0},{3,1},{4,6},{5,7},{6,4},{7,5},{8,10},{9,11},{10,... | collective-permute-start | bytes 3080 | tf_op jit(solution)/shard_map/ppermute | solution.py:41
  63.5 9.8 %collective-permute-start.23 = (f32[2,128]{1,0:T(2,128)S(1)}, f32[2,128]{1,0:T(2,128)S(1)}, u32[]{:S(2)}, u32[]{:S(2)}) collective-permute-start(f32[2,128]{1,0:T(2,128)S(1)} %copy-done.25), channel_id=1, source_target_pairs={{2,4},{3,5},{6,8},{7,9},{10,12},{11,13},{14,16},{15,17},{18,20},{1... | collective-permute-start | bytes 3080 | tf_op jit(solution)/shard_map/ppermute | solution.py:41
  73.3 0.6 copy-start.4
  (5 other events, 2.8 us)

commit v2 on v1

--- a/solution.py
+++ b/solution.py
@@ -264,6 +264,7 @@
         in_specs=[SMEM, SMEM] + [VMEM] * 5,
         cost_estimate=pl.CostEstimate(flops=4000000, bytes_accessed=600000, transcendentals=0),
         name="prepare",
+        compiler_params=pltpu.CompilerParams(vmem_limit_bytes=4 << 20),
     )(meta, thickness, tracer, bottom, neighbours, edge_weight, height)
     first = exchange(out, count)
     base = pl.pallas_call(
@@ -273,6 +274,7 @@
         scratch_shapes=[pltpu.VMEM(tracer.shape, jnp.float32)],
         cost_estimate=pl.CostEstimate(flops=20000000, bytes_accessed=800000, transcendentals=0),
         name="tracer_base",
+        compiler_params=pltpu.CompilerParams(vmem_limit_bytes=4 << 20),
     )(meta, tracer, bottom, neighbours, edge_weight, *first)
     total = jnp.zeros(tile, jnp.float32)
     arrived = first
@@ -284,6 +286,7 @@
             in_specs=[SMEM] + [VMEM] * 10,
             cost_estimate=pl.CostEstimate(flops=500000, bytes_accessed=100000, transcendentals=0),
             name="substep",
+            compiler_params=pltpu.CompilerParams(vmem_limit_bytes=2 << 20),
         )(meta, height, speed, total, forcing, index, weight, *arrived)
         arrived = exchange(out, count)
     height, speed, result = pl.pallas_call(
@@ -293,6 +296,7 @@
         scratch_shapes=[pltpu.VMEM(tile, jnp.float32)],
         cost_estimate=pl.CostEstimate(flops=1000000, bytes_accessed=500000, transcendentals=0),
         name="last_substep",
+        compiler_params=pltpu.CompilerParams(vmem_limit_bytes=4 << 20),
     )(profile, height, speed, total, forcing, index, weight, *arrived, bottom, base)
     return (result, height.reshape(-1), speed.reshape(-1))
 

time: 76.6 us -> 63.3 us (0.83)
  Pallas kernels: 18.6 us -> 11.4 us
  local copies, waits for them, and re-layouts: 10.9 us -> 5.28 us
    unnamed x91 -> x25, local copies, waits for them, and re-layouts: 10.2 us -> 5.2 us
    pallas_call x5, Pallas kernels: 8.27 us -> 3.72 us  [shards(): pl.pallas_call(functools.partial(substep, row=row, send=send), out_shape=...]
    pallas_call x1, Pallas kernels: 6.69 us -> 5.6 us  [shards(): pl.pallas_call(functools.partial(tracer_base, count=count, send=send), ou...]
    pallas_call x1, Pallas kernels: 1.72 us -> 0.68 us  [shards(): pl.pallas_call(functools.partial(prepare, count=count, send=send), out_sh...]
where the time goes in v2:
time: 63.3 us; the launch traced here: 62.6 us
  starting transfers between devices  34.3 us (54%)
  Pallas kernels  11.4 us (18%)
  waiting for transfers between devices  10.7 us (17%)
  local copies, waits for them, and re-layouts  5.28 us (8%)
  between operations  0.76 us (1%)
    ppermute x24, starting transfers between devices, exchange(): lax.ppermute(value, 'dom', way)  34.3 us
    ppermute x24, waiting for transfers between devices, exchange(): lax.ppermute(value, 'dom', way)  10.7 us
    pallas_call x1, Pallas kernels, shards(): pl.pallas_call(functools.partial(tracer_base, count=count, send=send), ou...  5.6 us
    unnamed x25, local copies, waits for them, and re-layouts  5.2 us
    pallas_call x5, Pallas kernels, shards(): pl.pallas_call(functools.partial(substep, row=row, send=send), out_shape=...  3.72 us
    pallas_call x1, Pallas kernels, shards(): pl.pallas_call(functools.partial(last_substep, row=0, send=send), out_sha...  1.43 us
  transfers between devices with their start and end apart: 24, of which 8 were waited for; matrix products, arithmetic and copies ran while one was open for 0% of the time, Pallas kernels for 9%

profile of v2, /device:TPU:9, one launch (start us, length us, event | category | flops | bytes accessed | tf_op | source)
XLA Modules:
  0.0 62.6 jit_solution(7566223934293688534)
XLA Ops:
  0.6 0.7 %copy-done.11 = s32[1,4,2]{1,2,0:T(2,128)S(1)} copy-done((s32[1,4,2]{1,2,0:T(2,128)S(1)}, s32[1,4,2]{1,2,0:T(2,128)}, u32[]{:S(2)}) %copy-start.11) | copy-done | bytes 56
  1.3 0.1 copy.13
  1.4 0.1 reshape.24
  1.5 0.1 pad_add_fusion.meta
  1.6 0.6 copy-done.7
  2.2 0.0 copy-done.6
  2.2 0.0 copy-done.9
  2.2 0.9 %copy-done = f32[40,1024]{1,0:T(8,128)S(1)} copy-done((f32[40,1024]{1,0:T(8,128)S(1)}, f32[40,1024]{1,0:T(8,128)}, u32[]{:S(2)}) %copy-start) | copy-done | bytes 163864
  3.1 0.8 %copy-done.2 = s32[6,1024]{1,0:T(8,128)S(1)} copy-done((s32[6,1024]{1,0:T(8,128)S(1)}, s32[6,1024]{1,0:T(8,128)}, u32[]{:S(2)}) %copy-start.2) | copy-done | bytes 24600
  3.9 0.8 %copy-done.4 = f32[6,1024]{1,0:T(8,128)S(1)} copy-done((f32[6,1024]{1,0:T(8,128)S(1)}, f32[6,1024]{1,0:T(8,128)}, u32[]{:S(2)}) %copy-start.4) | copy-done | bytes 24600
  4.7 0.7 %prepare.1 = (f32[8,128]{1,0:T(8,128)S(1)}, s32[6,8,128]{2,1,0:T(8,128)S(1)}, f32[6,8,128]{2,1,0:T(8,128)S(1)}, f32[88,128]{1,0:T(8,128)S(1)}, f32[88,128]{1,0:T...) custom-call(s32[9]{0:T(128)S(1)} %pad_add_fusion.meta, f32[40]{0:T(128)S(1)} %copy-done.9, ...), custom_call_target="tpu_custom_call" | custom-call | flops 4000000 | bytes 600000 | tf_op jit(solution)/shard_map/prepare/pallas_call | solution.py:256
  5.3 0.7 %collective-permute-start = (f32[88,128]{1,0:T(8,128)S(1)}, f32[88,128]{1,0:T(8,128)S(1)}, u32[]{:S(2)}, u32[]{:S(2)}) collective-permute-start(f32[88,128]{1,0:T(8,128)S(1)} %get-tuple-element.51), channel_id=1, source_target_pairs={{0,1},{1,0},{2,3},{3,2},{4,5},{5,4},{6,7},{7,6},{8,9},{9,8},{10,11... | collective-permute-start | bytes 135176 | tf_op jit(solution)/shard_map/ppermute | solution.py:41
  6.1 1.2 %collective-permute-start.1 = (f32[88,128]{1,0:T(8,128)S(1)}, f32[88,128]{1,0:T(8,128)S(1)}, u32[]{:S(2)}, u32[]{:S(2)}) collective-permute-start(f32[88,128]{1,0:T(8,128)S(1)} %get-tuple-element.52), channel_id=1, source_target_pairs={{1,2},{3,4},{5,6},{7,8},{9,10},{11,12},{13,14},{15,16},{17,18},{19... | collective-permute-start | bytes 135176 | tf_op jit(solution)/shard_map/ppermute | solution.py:41
  7.3 1.2 %collective-permute-start.2 = (f32[88,128]{1,0:T(8,128)S(1)}, f32[88,128]{1,0:T(8,128)S(1)}, u32[]{:S(2)}, u32[]{:S(2)}) collective-permute-start(f32[88,128]{1,0:T(8,128)S(1)} %get-tuple-element.53), channel_id=1, source_target_pairs={{0,2},{1,3},{2,0},{3,1},{4,6},{5,7},{6,4},{7,5},{8,10},{9,11},{10,... | collective-permute-start | bytes 135176 | tf_op jit(solution)/shard_map/ppermute | solution.py:41
  8.5 1.1 %collective-permute-start.3 = (f32[88,128]{1,0:T(8,128)S(1)}, f32[88,128]{1,0:T(8,128)S(1)}, u32[]{:S(2)}, u32[]{:S(2)}) collective-permute-start(f32[88,128]{1,0:T(8,128)S(1)} %get-tuple-element.54), channel_id=1, source_target_pairs={{2,4},{3,5},{6,8},{7,9},{10,12},{11,13},{14,16},{15,17},{18,20},{1... | collective-permute-start | bytes 135176 | tf_op jit(solution)/shard_map/ppermute | solution.py:41
  9.6 0.0 collective-permute-done.a
  9.6 0.1 collective-permute-done.1.b
  9.7 1.1 %collective-permute-done.2.c = f32[88,128]{1,0:T(8,128)S(1)} collective-permute-done((f32[88,128]{1,0:T(8,128)S(1)}, f32[88,128]{1,0:T(8,128)S(1)}, u32[]{:S(2)}, u32[]{:S(2)}) %collective-permute-start.2) | collective-permute-done | bytes 45088 | tf_op jit(solution)/shard_map/ppermute | solution.py:41
  10.8 2.3 %collective-permute-done.3.d = f32[88,128]{1,0:T(8,128)S(1)} collective-permute-done((f32[88,128]{1,0:T(8,128)S(1)}, f32[88,128]{1,0:T(8,128)S(1)}, u32[]{:S(2)}, u32[]{:S(2)}) %collective-permute-start.3) | collective-permute-done | bytes 45088 | tf_op jit(solution)/shard_map/ppermute | solution.py:41
  13.2 0.7 %copy-done.8 = f32[1024]{0:T(1024)S(1)} copy-done((f32[1024]{0:T(1024)S(1)}, f32[1024]{0:T(1024)}, u32[]{:S(2)}) %copy-start.8) | copy-done | bytes 4120
  13.9 0.7 %substep.5 = (f32[8,128]{1,0:T(8,128)S(1)}, f32[8,128]{1,0:T(8,128)S(1)}, f32[8,128]{1,0:T(8,128)S(1)}, f32[2,128]{1,0:T(2,128)S(1)}, f32[2,128]{1,0:T(2,128)S(1...) custom-call(s32[9]{0:T(128)S(1)} %pad_add_fusion.meta, f32[8,128]{1,0:T(8,128)S(1)} %bitcast.10, f32[8,128]{1,0:T(8,128)S(1)} %bitcast.11, ...), custom_call_target="tpu_custom_call" | custom-call | flops 500000 | bytes 100000 | tf_op jit(solution)/shard_map/substep/pallas_call | solution.py:283
  14.6 1.3 %collective-permute-start.4 = (f32[2,128]{1,0:T(2,128)S(1)}, f32[2,128]{1,0:T(2,128)S(1)}, u32[]{:S(2)}, u32[]{:S(2)}) collective-permute-start(f32[2,128]{1,0:T(2,128)S(1)} %get-tuple-element.58), channel_id=1, source_target_pairs={{0,1},{1,0},{2,3},{3,2},{4,5},{5,4},{6,7},{7,6},{8,9},{9,8},{10,11... | collective-permute-start | bytes 3080 | tf_op jit(solution)/shard_map/ppermute | solution.py:41
  15.9 0.8 %collective-permute-start.5 = (f32[2,128]{1,0:T(2,128)S(1)}, f32[2,128]{1,0:T(2,128)S(1)}, u32[]{:S(2)}, u32[]{:S(2)}) collective-permute-start(f32[2,128]{1,0:T(2,128)S(1)} %get-tuple-element.59), channel_id=1, source_target_pairs={{1,2},{3,4},{5,6},{7,8},{9,10},{11,12},{13,14},{15,16},{17,18},{19... | collective-permute-start | bytes 3080 | tf_op jit(solution)/shard_map/ppermute | solution.py:41
  16.7 0.7 %collective-permute-start.6 = (f32[2,128]{1,0:T(2,128)S(1)}, f32[2,128]{1,0:T(2,128)S(1)}, u32[]{:S(2)}, u32[]{:S(2)}) collective-permute-start(f32[2,128]{1,0:T(2,128)S(1)} %get-tuple-element.60), channel_id=1, source_target_pairs={{0,2},{1,3},{2,0},{3,1},{4,6},{5,7},{6,4},{7,5},{8,10},{9,11},{10,... | collective-permute-start | bytes 3080 | tf_op jit(solution)/shard_map/ppermute | solution.py:41
  17.4 2.6 %collective-permute-start.7 = (f32[2,128]{1,0:T(2,128)S(1)}, f32[2,128]{1,0:T(2,128)S(1)}, u32[]{:S(2)}, u32[]{:S(2)}) collective-permute-start(f32[2,128]{1,0:T(2,128)S(1)} %get-tuple-element.61), channel_id=1, source_target_pairs={{2,4},{3,5},{6,8},{7,9},{10,12},{11,13},{14,16},{15,17},{18,20},{1... | collective-permute-start | bytes 3080 | tf_op jit(solution)/shard_map/ppermute | solution.py:41
  20.0 0.0 collective-permute-done.4.a
  20.0 0.0 collective-permute-done.5.b
  20.0 0.0 collective-permute-done.6.c
  20.0 1.6 %collective-permute-done.7.d = f32[2,128]{1,0:T(2,128)S(1)} collective-permute-done((f32[2,128]{1,0:T(2,128)S(1)}, f32[2,128]{1,0:T(2,128)S(1)}, u32[]{:S(2)}, u32[]{:S(2)}) %collective-permute-start.7) | collective-permute-done | bytes 1056 | tf_op jit(solution)/shard_map/ppermute | solution.py:41
  21.6 0.7 %substep.6 = (f32[8,128]{1,0:T(8,128)S(1)}, f32[8,128]{1,0:T(8,128)S(1)}, f32[8,128]{1,0:T(8,128)S(1)}, f32[2,128]{1,0:T(2,128)S(1)}, f32[2,128]{1,0:T(2,128)S(1...) custom-call(s32[9]{0:T(128)S(1)} %pad_add_fusion.meta, f32[8,128]{1,0:T(8,128)S(1)} %get-tuple-element.55.height, ...), custom_call_target="tpu_custom_call" | custom-call | flops 500000 | bytes 100000 | tf_op jit(solution)/shard_map/substep/pallas_call | solution.py:283
  22.3 0.1 collective-permute-start.10
  22.5 2.9 %collective-permute-start.11 = (f32[2,128]{1,0:T(2,128)S(1)}, f32[2,128]{1,0:T(2,128)S(1)}, u32[]{:S(2)}, u32[]{:S(2)}) collective-permute-start(f32[2,128]{1,0:T(2,128)S(1)} %get-tuple-element.68), channel_id=1, source_target_pairs={{2,4},{3,5},{6,8},{7,9},{10,12},{11,13},{14,16},{15,17},{18,20},{1... | collective-permute-start | bytes 3080 | tf_op jit(solution)/shard_map/ppermute | solution.py:41
  25.3 4.0 %collective-permute-start.8 = (f32[2,128]{1,0:T(2,128)S(1)}, f32[2,128]{1,0:T(2,128)S(1)}, u32[]{:S(2)}, u32[]{:S(2)}) collective-permute-start(f32[2,128]{1,0:T(2,128)S(1)} %get-tuple-element.65), channel_id=1, source_target_pairs={{0,1},{1,0},{2,3},{3,2},{4,5},{5,4},{6,7},{7,6},{8,9},{9,8},{10,11... | collective-permute-start | bytes 3080 | tf_op jit(solution)/shard_map/ppermute | solution.py:41
  29.3 0.0 collective-permute-start.9
  29.4 0.0 collective-permute-done.10.c
  29.4 0.0 collective-permute-done.11.d
  29.4 0.8 %collective-permute-done.8.a = f32[2,128]{1,0:T(2,128)S(1)} collective-permute-done((f32[2,128]{1,0:T(2,128)S(1)}, f32[2,128]{1,0:T(2,128)S(1)}, u32[]{:S(2)}, u32[]{:S(2)}) %collective-permute-start.8) | collective-permute-done | bytes 1056 | tf_op jit(solution)/shard_map/ppermute | solution.py:41
  30.2 2.2 %collective-permute-done.9.b = f32[2,128]{1,0:T(2,128)S(1)} collective-permute-done((f32[2,128]{1,0:T(2,128)S(1)}, f32[2,128]{1,0:T(2,128)S(1)}, u32[]{:S(2)}, u32[]{:S(2)}) %collective-permute-start.9) | collective-permute-done | bytes 1056 | tf_op jit(solution)/shard_map/ppermute | solution.py:41
  32.3 0.7 %substep.7 = (f32[8,128]{1,0:T(8,128)S(1)}, f32[8,128]{1,0:T(8,128)S(1)}, f32[8,128]{1,0:T(8,128)S(1)}, f32[2,128]{1,0:T(2,128)S(1)}, f32[2,128]{1,0:T(2,128)S(1...) custom-call(s32[9]{0:T(128)S(1)} %pad_add_fusion.meta, f32[8,128]{1,0:T(8,128)S(1)} %get-tuple-element.62.height, ...), custom_call_target="tpu_custom_call" | custom-call | flops 500000 | bytes 100000 | tf_op jit(solution)/shard_map/substep/pallas_call | solution.py:283
  33.1 1.9 %collective-permute-start.12 = (f32[2,128]{1,0:T(2,128)S(1)}, f32[2,128]{1,0:T(2,128)S(1)}, u32[]{:S(2)}, u32[]{:S(2)}) collective-permute-start(f32[2,128]{1,0:T(2,128)S(1)} %get-tuple-element.72), channel_id=1, source_target_pairs={{0,1},{1,0},{2,3},{3,2},{4,5},{5,4},{6,7},{7,6},{8,9},{9,8},{10,11... | collective-permute-start | bytes 3080 | tf_op jit(solution)/shard_map/ppermute | solution.py:41
  35.0 0.0 collective-permute-start.13
  35.0 0.0 collective-permute-start.14
  35.0 3.2 %collective-permute-start.15 = (f32[2,128]{1,0:T(2,128)S(1)}, f32[2,128]{1,0:T(2,128)S(1)}, u32[]{:S(2)}, u32[]{:S(2)}) collective-permute-start(f32[2,128]{1,0:T(2,128)S(1)} %get-tuple-element.75), channel_id=1, source_target_pairs={{2,4},{3,5},{6,8},{7,9},{10,12},{11,13},{14,16},{15,17},{18,20},{1... | collective-permute-start | bytes 3080 | tf_op jit(solution)/shard_map/ppermute | solution.py:41
  38.2 0.0 collective-permute-done.12.a
  38.2 0.0 collective-permute-done.13.b
  38.2 0.0 collective-permute-done.14.c
  38.2 1.2 %collective-permute-done.15.d = f32[2,128]{1,0:T(2,128)S(1)} collective-permute-done((f32[2,128]{1,0:T(2,128)S(1)}, f32[2,128]{1,0:T(2,128)S(1)}, u32[]{:S(2)}, u32[]{:S(2)}) %collective-permute-start.15) | collective-permute-done | bytes 1056 | tf_op jit(solution)/shard_map/ppermute | solution.py:41
  39.4 0.7 %substep.8 = (f32[8,128]{1,0:T(8,128)S(1)}, f32[8,128]{1,0:T(8,128)S(1)}, f32[8,128]{1,0:T(8,128)S(1)}, f32[2,128]{1,0:T(2,128)S(1)}, f32[2,128]{1,0:T(2,128)S(1...) custom-call(s32[9]{0:T(128)S(1)} %pad_add_fusion.meta, f32[8,128]{1,0:T(8,128)S(1)} %get-tuple-element.69.height, ...), custom_call_target="tpu_custom_call" | custom-call | flops 500000 | bytes 100000 | tf_op jit(solution)/shard_map/substep/pallas_call | solution.py:283
  40.2 3.1 %collective-permute-start.16 = (f32[2,128]{1,0:T(2,128)S(1)}, f32[2,128]{1,0:T(2,128)S(1)}, u32[]{:S(2)}, u32[]{:S(2)}) collective-permute-start(f32[2,128]{1,0:T(2,128)S(1)} %get-tuple-element.79), channel_id=1, source_target_pairs={{0,1},{1,0},{2,3},{3,2},{4,5},{5,4},{6,7},{7,6},{8,9},{9,8},{10,11... | collective-permute-start | bytes 3080 | tf_op jit(solution)/shard_map/ppermute | solution.py:41
  43.3 0.0 collective-permute-start.17
  43.3 0.0 collective-permute-start.18
  43.3 3.2 %collective-permute-start.19 = (f32[2,128]{1,0:T(2,128)S(1)}, f32[2,128]{1,0:T(2,128)S(1)}, u32[]{:S(2)}, u32[]{:S(2)}) collective-permute-start(f32[2,128]{1,0:T(2,128)S(1)} %get-tuple-element.82), channel_id=1, source_target_pairs={{2,4},{3,5},{6,8},{7,9},{10,12},{11,13},{14,16},{15,17},{18,20},{1... | collective-permute-start | bytes 3080 | tf_op jit(solution)/shard_map/ppermute | solution.py:41
  46.5 0.0 collective-permute-done.16.a
  46.5 0.0 collective-permute-done.17.b
  46.5 1.2 %collective-permute-done.19.d = f32[2,128]{1,0:T(2,128)S(1)} collective-permute-done((f32[2,128]{1,0:T(2,128)S(1)}, f32[2,128]{1,0:T(2,128)S(1)}, u32[]{:S(2)}, u32[]{:S(2)}) %collective-permute-start.19) | collective-permute-done | bytes 1056 | tf_op jit(solution)/shard_map/ppermute | solution.py:41
  47.8 0.7 %substep.9 = (f32[8,128]{1,0:T(8,128)S(1)}, f32[8,128]{1,0:T(8,128)S(1)}, f32[8,128]{1,0:T(8,128)S(1)}, f32[2,128]{1,0:T(2,128)S(1)}, f32[2,128]{1,0:T(2,128)S(1...) custom-call(s32[9]{0:T(128)S(1)} %pad_add_fusion.meta, f32[8,128]{1,0:T(8,128)S(1)} %get-tuple-element.76.height, ...), custom_call_target="tpu_custom_call" | custom-call | flops 500000 | bytes 100000 | tf_op jit(solution)/shard_map/substep/pallas_call | solution.py:283
  48.5 3.1 %collective-permute-start.20 = (f32[2,128]{1,0:T(2,128)S(1)}, f32[2,128]{1,0:T(2,128)S(1)}, u32[]{:S(2)}, u32[]{:S(2)}) collective-permute-start(f32[2,128]{1,0:T(2,128)S(1)} %get-tuple-element.86), channel_id=1, source_target_pairs={{0,1},{1,0},{2,3},{3,2},{4,5},{5,4},{6,7},{7,6},{8,9},{9,8},{10,11... | collective-permute-start | bytes 3080 | tf_op jit(solution)/shard_map/ppermute | solution.py:41
  51.6 0.8 %collective-permute-start.21 = (f32[2,128]{1,0:T(2,128)S(1)}, f32[2,128]{1,0:T(2,128)S(1)}, u32[]{:S(2)}, u32[]{:S(2)}) collective-permute-start(f32[2,128]{1,0:T(2,128)S(1)} %get-tuple-element.87), channel_id=1, source_target_pairs={{1,2},{3,4},{5,6},{7,8},{9,10},{11,12},{13,14},{15,16},{17,18},{19... | collective-permute-start | bytes 3080 | tf_op jit(solution)/shard_map/ppermute | solution.py:41
  52.4 0.0 collective-permute-start.22
  52.5 2.4 %collective-permute-start.23 = (f32[2,128]{1,0:T(2,128)S(1)}, f32[2,128]{1,0:T(2,128)S(1)}, u32[]{:S(2)}, u32[]{:S(2)}) collective-permute-start(f32[2,128]{1,0:T(2,128)S(1)} %get-tuple-element.89), channel_id=1, source_target_pairs={{2,4},{3,5},{6,8},{7,9},{10,12},{11,13},{14,16},{15,17},{18,20},{1... | collective-permute-start | bytes 3080 | tf_op jit(solution)/shard_map/ppermute | solution.py:41
  54.9 5.6 %tracer_base.1.base = f32[40,1024]{1,0:T(8,128)S(1)} custom-call(s32[9]{0:T(128)S(1)} %pad_add_fusion.meta, f32[40,1024]{1,0:T(8,128)S(1)} %copy-done.1, s32[8,128]{1,0:T(8,128)S(1)} %bitcast.7, s32[6,1024]{1,0:T(8,128)S(1)} %copy-done.3, f32[6,1024]{1,0:T(8,128)S(1)} %copy-done.5, f32[88,128]{1,0:T(8,128)S(1)} %collective-permute-done.a, ...), custom_call_target="tpu_custom_call" | custom-call | flops 20000000 | bytes 800000 | tf_op jit(solution)/shard_map/tracer_base/pallas_call | solution.py:270
  60.5 0.0 copy-start.10
  60.5 0.6 %copy-done.10 = f32[40]{0:T(128)S(1)} copy-done((f32[40]{0:T(128)S(1)}, f32[40]{0:T(128)}, u32[]{:S(2)}) %copy-start.10) | copy-done | bytes 184
  61.2 1.4 %last_substep.1 = (f32[8,128]{1,0:T(8,128)}, f32[8,128]{1,0:T(8,128)}, f32[40,1024]{1,0:T(8,128)}) custom-call(f32[40]{0:T(128)S(1)} %copy-done.10, f32[8,128]{1,0:T(8,128)S(1)} %get-tuple-element.83.height, f32[8,128]{1,0:T(8,128)S(1)} %get-tuple-element.84.speed, f32[8,128]{1,0:T(8,128)S(1)} %get-tuple-element.85.total, ...), custom_call_target="tpu_custom_call" | custom-call | flops 1000000 | bytes 500000 | tf_op jit(solution)/shard_map/last_substep/pallas_call | solution.py:292
  (20 shorter events, 0.0 us)
Async XLA Ops:
  0.6 0.7 %copy-start.11 = (s32[1,4,2]{1,2,0:T(2,128)S(1)}, s32[1,4,2]{1,2,0:T(2,128)}, u32[]{:S(2)}) copy-start(s32[1,4,2]{1,2,0:T(2,128)} %param.15) | copy-start | bytes 100
  1.5 0.7 %copy-start.7 = (f32[1024]{0:T(1024)S(1)}, f32[1024]{0:T(1024)}, u32[]{:S(2)}) copy-start(f32[1024]{0:T(1024)} %param.13) | copy-start | bytes 12292
  1.5 0.7 %copy-start.6 = (s32[1024]{0:T(1024)S(1)}, s32[1024]{0:T(1024)}, u32[]{:S(2)}) copy-start(s32[1024]{0:T(1024)} %param.10) | copy-start | bytes 12292
  1.6 0.7 %copy-start.9 = (f32[40]{0:T(128)S(1)}, f32[40]{0:T(128)}, u32[]{:S(2)}) copy-start(f32[40]{0:T(128)} %thick.1) | copy-start | bytes 484
  2.2 0.9 %copy-start = (f32[40,1024]{1,0:T(8,128)S(1)}, f32[40,1024]{1,0:T(8,128)}, u32[]{:S(2)}) copy-start(f32[40,1024]{1,0:T(8,128)} %tracer.3) | copy-start | bytes 491524
  3.1 0.8 %copy-start.2 = (s32[6,1024]{1,0:T(8,128)S(1)}, s32[6,1024]{1,0:T(8,128)}, u32[]{:S(2)}) copy-start(s32[6,1024]{1,0:T(8,128)} %index.3) | copy-start | bytes 73732
  3.9 0.8 %copy-start.4 = (f32[6,1024]{1,0:T(8,128)S(1)}, f32[6,1024]{1,0:T(8,128)}, u32[]{:S(2)}) copy-start(f32[6,1024]{1,0:T(8,128)} %weight.3) | copy-start | bytes 73732
  5.3 4.2 %collective-permute-start = (f32[88,128]{1,0:T(8,128)S(1)}, f32[88,128]{1,0:T(8,128)S(1)}, u32[]{:S(2)}, u32[]{:S(2)}) collective-permute-start(f32[88,128]{1,0:T(8,128)S(1)} %get-tuple-element.51), channel_id=1, source_target_pairs={{0,1},{1,0},{2,3},{3,2},{4,5},{5,4},{6,7},{7,6},{8,9},{9,8},{10,11... | collective-permute-start | bytes 135176 | tf_op jit(solution)/shard_map/ppermute | solution.py:41
  6.1 3.6 %collective-permute-start.1 = (f32[88,128]{1,0:T(8,128)S(1)}, f32[88,128]{1,0:T(8,128)S(1)}, u32[]{:S(2)}, u32[]{:S(2)}) collective-permute-start(f32[88,128]{1,0:T(8,128)S(1)} %get-tuple-element.52), channel_id=1, source_target_pairs={{1,2},{3,4},{5,6},{7,8},{9,10},{11,12},{13,14},{15,16},{17,18},{19... | collective-permute-start | bytes 135176 | tf_op jit(solution)/shard_map/ppermute | solution.py:41
  7.3 3.6 %collective-permute-start.2 = (f32[88,128]{1,0:T(8,128)S(1)}, f32[88,128]{1,0:T(8,128)S(1)}, u32[]{:S(2)}, u32[]{:S(2)}) collective-permute-start(f32[88,128]{1,0:T(8,128)S(1)} %get-tuple-element.53), channel_id=1, source_target_pairs={{0,2},{1,3},{2,0},{3,1},{4,6},{5,7},{6,4},{7,5},{8,10},{9,11},{10,... | collective-permute-start | bytes 135176 | tf_op jit(solution)/shard_map/ppermute | solution.py:41
  8.5 4.7 %collective-permute-start.3 = (f32[88,128]{1,0:T(8,128)S(1)}, f32[88,128]{1,0:T(8,128)S(1)}, u32[]{:S(2)}, u32[]{:S(2)}) collective-permute-start(f32[88,128]{1,0:T(8,128)S(1)} %get-tuple-element.54), channel_id=1, source_target_pairs={{2,4},{3,5},{6,8},{7,9},{10,12},{11,13},{14,16},{15,17},{18,20},{1... | collective-permute-start | bytes 135176 | tf_op jit(solution)/shard_map/ppermute | solution.py:41
  13.2 0.7 %copy-start.8 = (f32[1024]{0:T(1024)S(1)}, f32[1024]{0:T(1024)}, u32[]{:S(2)}) copy-start(f32[1024]{0:T(1024)} %param.14) | copy-start | bytes 12292
  14.6 5.4 %collective-permute-start.4 = (f32[2,128]{1,0:T(2,128)S(1)}, f32[2,128]{1,0:T(2,128)S(1)}, u32[]{:S(2)}, u32[]{:S(2)}) collective-permute-start(f32[2,128]{1,0:T(2,128)S(1)} %get-tuple-element.58), channel_id=1, source_target_pairs={{0,1},{1,0},{2,3},{3,2},{4,5},{5,4},{6,7},{7,6},{8,9},{9,8},{10,11... | collective-permute-start | bytes 3080 | tf_op jit(solution)/shard_map/ppermute | solution.py:41
  15.9 4.1 %collective-permute-start.5 = (f32[2,128]{1,0:T(2,128)S(1)}, f32[2,128]{1,0:T(2,128)S(1)}, u32[]{:S(2)}, u32[]{:S(2)}) collective-permute-start(f32[2,128]{1,0:T(2,128)S(1)} %get-tuple-element.59), channel_id=1, source_target_pairs={{1,2},{3,4},{5,6},{7,8},{9,10},{11,12},{13,14},{15,16},{17,18},{19... | collective-permute-start | bytes 3080 | tf_op jit(solution)/shard_map/ppermute | solution.py:41
  16.7 3.3 %collective-permute-start.6 = (f32[2,128]{1,0:T(2,128)S(1)}, f32[2,128]{1,0:T(2,128)S(1)}, u32[]{:S(2)}, u32[]{:S(2)}) collective-permute-start(f32[2,128]{1,0:T(2,128)S(1)} %get-tuple-element.60), channel_id=1, source_target_pairs={{0,2},{1,3},{2,0},{3,1},{4,6},{5,7},{6,4},{7,5},{8,10},{9,11},{10,... | collective-permute-start | bytes 3080 | tf_op jit(solution)/shard_map/ppermute | solution.py:41
  17.4 4.2 %collective-permute-start.7 = (f32[2,128]{1,0:T(2,128)S(1)}, f32[2,128]{1,0:T(2,128)S(1)}, u32[]{:S(2)}, u32[]{:S(2)}) collective-permute-start(f32[2,128]{1,0:T(2,128)S(1)} %get-tuple-element.61), channel_id=1, source_target_pairs={{2,4},{3,5},{6,8},{7,9},{10,12},{11,13},{14,16},{15,17},{18,20},{1... | collective-permute-start | bytes 3080 | tf_op jit(solution)/shard_map/ppermute | solution.py:41
  21.6 33.3 %copy-start.1 = (f32[40,1024]{1,0:T(8,128)S(1)}, f32[40,1024]{1,0:T(8,128)}, u32[]{:S(2)}) copy-start(f32[40,1024]{1,0:T(8,128)} %tracer.3) | copy-start | bytes 491524
  22.3 7.0 %collective-permute-start.10 = (f32[2,128]{1,0:T(2,128)S(1)}, f32[2,128]{1,0:T(2,128)S(1)}, u32[]{:S(2)}, u32[]{:S(2)}) collective-permute-start(f32[2,128]{1,0:T(2,128)S(1)} %get-tuple-element.67), channel_id=1, source_target_pairs={{0,2},{1,3},{2,0},{3,1},{4,6},{5,7},{6,4},{7,5},{8,10},{9,11},{10,... | collective-permute-start | bytes 3080 | tf_op jit(solution)/shard_map/ppermute | solution.py:41
  22.5 6.9 %collective-permute-start.11 = (f32[2,128]{1,0:T(2,128)S(1)}, f32[2,128]{1,0:T(2,128)S(1)}, u32[]{:S(2)}, u32[]{:S(2)}) collective-permute-start(f32[2,128]{1,0:T(2,128)S(1)} %get-tuple-element.68), channel_id=1, source_target_pairs={{2,4},{3,5},{6,8},{7,9},{10,12},{11,13},{14,16},{15,17},{18,20},{1... | collective-permute-start | bytes 3080 | tf_op jit(solution)/shard_map/ppermute | solution.py:41
  25.3 4.8 %collective-permute-start.8 = (f32[2,128]{1,0:T(2,128)S(1)}, f32[2,128]{1,0:T(2,128)S(1)}, u32[]{:S(2)}, u32[]{:S(2)}) collective-permute-start(f32[2,128]{1,0:T(2,128)S(1)} %get-tuple-element.65), channel_id=1, source_target_pairs={{0,1},{1,0},{2,3},{3,2},{4,5},{5,4},{6,7},{7,6},{8,9},{9,8},{10,11... | collective-permute-start | bytes 3080 | tf_op jit(solution)/shard_map/ppermute | solution.py:41
  29.3 3.0 %collective-permute-start.9 = (f32[2,128]{1,0:T(2,128)S(1)}, f32[2,128]{1,0:T(2,128)S(1)}, u32[]{:S(2)}, u32[]{:S(2)}) collective-permute-start(f32[2,128]{1,0:T(2,128)S(1)} %get-tuple-element.66), channel_id=1, source_target_pairs={{1,2},{3,4},{5,6},{7,8},{9,10},{11,12},{13,14},{15,16},{17,18},{19... | collective-permute-start | bytes 3080 | tf_op jit(solution)/shard_map/ppermute | solution.py:41
  33.1 5.1 %collective-permute-start.12 = (f32[2,128]{1,0:T(2,128)S(1)}, f32[2,128]{1,0:T(2,128)S(1)}, u32[]{:S(2)}, u32[]{:S(2)}) collective-permute-start(f32[2,128]{1,0:T(2,128)S(1)} %get-tuple-element.72), channel_id=1, source_target_pairs={{0,1},{1,0},{2,3},{3,2},{4,5},{5,4},{6,7},{7,6},{8,9},{9,8},{10,11... | collective-permute-start | bytes 3080 | tf_op jit(solution)/shard_map/ppermute | solution.py:41
  35.0 3.2 %collective-permute-start.13 = (f32[2,128]{1,0:T(2,128)S(1)}, f32[2,128]{1,0:T(2,128)S(1)}, u32[]{:S(2)}, u32[]{:S(2)}) collective-permute-start(f32[2,128]{1,0:T(2,128)S(1)} %get-tuple-element.73), channel_id=1, source_target_pairs={{1,2},{3,4},{5,6},{7,8},{9,10},{11,12},{13,14},{15,16},{17,18},{19... | collective-permute-start | bytes 3080 | tf_op jit(solution)/shard_map/ppermute | solution.py:41
  35.0 3.2 %collective-permute-start.14 = (f32[2,128]{1,0:T(2,128)S(1)}, f32[2,128]{1,0:T(2,128)S(1)}, u32[]{:S(2)}, u32[]{:S(2)}) collective-permute-start(f32[2,128]{1,0:T(2,128)S(1)} %get-tuple-element.74), channel_id=1, source_target_pairs={{0,2},{1,3},{2,0},{3,1},{4,6},{5,7},{6,4},{7,5},{8,10},{9,11},{10,... | collective-permute-start | bytes 3080 | tf_op jit(solution)/shard_map/ppermute | solution.py:41
  35.0 4.5 %collective-permute-start.15 = (f32[2,128]{1,0:T(2,128)S(1)}, f32[2,128]{1,0:T(2,128)S(1)}, u32[]{:S(2)}, u32[]{:S(2)}) collective-permute-start(f32[2,128]{1,0:T(2,128)S(1)} %get-tuple-element.75), channel_id=1, source_target_pairs={{2,4},{3,5},{6,8},{7,9},{10,12},{11,13},{14,16},{15,17},{18,20},{1... | collective-permute-start | bytes 3080 | tf_op jit(solution)/shard_map/ppermute | solution.py:41
  40.2 6.3 %collective-permute-start.16 = (f32[2,128]{1,0:T(2,128)S(1)}, f32[2,128]{1,0:T(2,128)S(1)}, u32[]{:S(2)}, u32[]{:S(2)}) collective-permute-start(f32[2,128]{1,0:T(2,128)S(1)} %get-tuple-element.79), channel_id=1, source_target_pairs={{0,1},{1,0},{2,3},{3,2},{4,5},{5,4},{6,7},{7,6},{8,9},{9,8},{10,11... | collective-permute-start | bytes 3080 | tf_op jit(solution)/shard_map/ppermute | solution.py:41
  43.3 3.2 %collective-permute-start.17 = (f32[2,128]{1,0:T(2,128)S(1)}, f32[2,128]{1,0:T(2,128)S(1)}, u32[]{:S(2)}, u32[]{:S(2)}) collective-permute-start(f32[2,128]{1,0:T(2,128)S(1)} %get-tuple-element.80), channel_id=1, source_target_pairs={{1,2},{3,4},{5,6},{7,8},{9,10},{11,12},{13,14},{15,16},{17,18},{19... | collective-permute-start | bytes 3080 | tf_op jit(solution)/shard_map/ppermute | solution.py:41
  43.3 3.2 %collective-permute-start.18 = (f32[2,128]{1,0:T(2,128)S(1)}, f32[2,128]{1,0:T(2,128)S(1)}, u32[]{:S(2)}, u32[]{:S(2)}) collective-permute-start(f32[2,128]{1,0:T(2,128)S(1)} %get-tuple-element.81), channel_id=1, source_target_pairs={{0,2},{1,3},{2,0},{3,1},{4,6},{5,7},{6,4},{7,5},{8,10},{9,11},{10,... | collective-permute-start | bytes 3080 | tf_op jit(solution)/shard_map/ppermute | solution.py:41
  43.3 4.5 %collective-permute-start.19 = (f32[2,128]{1,0:T(2,128)S(1)}, f32[2,128]{1,0:T(2,128)S(1)}, u32[]{:S(2)}, u32[]{:S(2)}) collective-permute-start(f32[2,128]{1,0:T(2,128)S(1)} %get-tuple-element.82), channel_id=1, source_target_pairs={{2,4},{3,5},{6,8},{7,9},{10,12},{11,13},{14,16},{15,17},{18,20},{1... | collective-permute-start | bytes 3080 | tf_op jit(solution)/shard_map/ppermute | solution.py:41
  47.8 7.1 %copy-start.3 = (s32[6,1024]{1,0:T(8,128)S(1)}, s32[6,1024]{1,0:T(8,128)}, u32[]{:S(2)}) copy-start(s32[6,1024]{1,0:T(8,128)} %index.3) | copy-start | bytes 73732
  47.8 7.1 %copy-start.5 = (f32[6,1024]{1,0:T(8,128)S(1)}, f32[6,1024]{1,0:T(8,128)}, u32[]{:S(2)}) copy-start(f32[6,1024]{1,0:T(8,128)} %weight.3) | copy-start | bytes 73732
  48.5 12.0 %collective-permute-start.20 = (f32[2,128]{1,0:T(2,128)S(1)}, f32[2,128]{1,0:T(2,128)S(1)}, u32[]{:S(2)}, u32[]{:S(2)}) collective-permute-start(f32[2,128]{1,0:T(2,128)S(1)} %get-tuple-element.86), channel_id=1, source_target_pairs={{0,1},{1,0},{2,3},{3,2},{4,5},{5,4},{6,7},{7,6},{8,9},{9,8},{10,11... | collective-permute-start | bytes 3080 | tf_op jit(solution)/shard_map/ppermute | solution.py:41
  51.6 8.9 %collective-permute-start.21 = (f32[2,128]{1,0:T(2,128)S(1)}, f32[2,128]{1,0:T(2,128)S(1)}, u32[]{:S(2)}, u32[]{:S(2)}) collective-permute-start(f32[2,128]{1,0:T(2,128)S(1)} %get-tuple-element.87), channel_id=1, source_target_pairs={{1,2},{3,4},{5,6},{7,8},{9,10},{11,12},{13,14},{15,16},{17,18},{19... | collective-permute-start | bytes 3080 | tf_op jit(solution)/shard_map/ppermute | solution.py:41
  52.4 8.1 %collective-permute-start.22 = (f32[2,128]{1,0:T(2,128)S(1)}, f32[2,128]{1,0:T(2,128)S(1)}, u32[]{:S(2)}, u32[]{:S(2)}) collective-permute-start(f32[2,128]{1,0:T(2,128)S(1)} %get-tuple-element.88), channel_id=1, source_target_pairs={{0,2},{1,3},{2,0},{3,1},{4,6},{5,7},{6,4},{7,5},{8,10},{9,11},{10,... | collective-permute-start | bytes 3080 | tf_op jit(solution)/shard_map/ppermute | solution.py:41
  52.5 8.0 %collective-permute-start.23 = (f32[2,128]{1,0:T(2,128)S(1)}, f32[2,128]{1,0:T(2,128)S(1)}, u32[]{:S(2)}, u32[]{:S(2)}) collective-permute-start(f32[2,128]{1,0:T(2,128)S(1)} %get-tuple-element.89), channel_id=1, source_target_pairs={{2,4},{3,5},{6,8},{7,9},{10,12},{11,13},{14,16},{15,17},{18,20},{1... | collective-permute-start | bytes 3080 | tf_op jit(solution)/shard_map/ppermute | solution.py:41
  60.5 0.7 %copy-start.10 = (f32[40]{0:T(128)S(1)}, f32[40]{0:T(128)}, u32[]{:S(2)}) copy-start(f32[40]{0:T(128)} %profile.1) | copy-start | bytes 484

commit v3 on v1

v3 whole, which is shorter than its diff:
```python
import functools

import jax
import jax.numpy as jnp
from jax import lax
from jax.experimental import pallas as pl
from jax.experimental.pallas import tpu as pltpu
from jax.sharding import PartitionSpec as P

LANES = 128
SUBS = 8
SUBSTEPS = 6
TEAM = 4
OFFSETS = (1, -1, 2, -2)
horizontal_rate = 0.5
vertical_rate = 0.5
tracer_step = 0.2
barotropic_step = 0.5
friction = 0.05
ABSENT = 3e38
PRESENT = 1e38

SMEM = pl.BlockSpec(memory_space=pltpu.SMEM)
VMEM = pl.BlockSpec(memory_space=pltpu.VMEM)
HBM = pl.BlockSpec(memory_space=pltpu.HBM)


def even_swap(count, by):
    return [(i, i ^ by) for i in range(count)]


def odd_swap(count, by):
    pairs = [(i, i + by) for i in range(by, count - by) if (i // by) % 2 == 1]
    pairs += [(b, a) for a, b in pairs]
    busy = {a for a, _ in pairs}
    rest = [i for i in range(count) if i not in busy]
    pairs += list(zip(rest[0::2], rest[1::2])) + list(zip(rest[1::2], rest[0::2]))
    return pairs


def column(scalars, tile):
    rows = lax.broadcasted_iota(jnp.int32, (SUBS, LANES), 0)
    value = jnp.zeros((SUBS, LANES), jnp.float32)
    for k in range(SUBS):
        value = jnp.where(rows == k, scalars[tile * SUBS + k], value)
    return value


def localize(index, place, count, cells, send):
    span = send * LANES
    result = index
    for g, offset in enumerate(OFFSETS):
        source = place - offset
        inside = jnp.logical_and(source >= 0, source < count)
        swapped = (place // abs(offset)) % 2 == 0
        step = jnp.where(swapped, span if g % 2 == 0 else -span, 0)
        low = cells + g * span
        mine = jnp.logical_and(index >= low, index < low + span)
        moved = jnp.where(inside, index + step, cells + 4 * span)
        result = jnp.where(mine, moved, result)
    return result


def group_of(rows, send):
    return rows // send


def blend(rows, send, parts):
    value = jnp.zeros((SUBS, LANES), jnp.float32)
    for g, part in parts.items():
        value = jnp.where(group_of(rows, send) == g, part, value)
    return value


def outgoing(field, slots):
    taken = jnp.take_along_axis(field, jnp.maximum(slots, 0), axis=0)
    return jnp.where(slots >= 0, taken, 0.0)


def prepare(
    place_ref, slots, thick, tracer_hbm, bottom_hbm, index_hbm, weight_hbm, ssh_hbm, velocity_hbm,
    near, side, far, odd, odd_side, mine, tracer, bottom, index, weight, ssh, velocity, sems,
    *, count, send,
):
    sources = (bottom_hbm, tracer_hbm, index_hbm, weight_hbm, ssh_hbm, velocity_hbm)
    targets = (bottom, tracer, index, weight, ssh, velocity)
    copies = [
        pltpu.make_async_copy(source, target, sems.at[n])
        for n, (source, target) in enumerate(zip(sources, targets))
    ]
    for copy in copies:
        copy.start()
    levels, cells = tracer.shape
    tiles = levels // SUBS
    blocks = cells // LANES
    edges = index.shape[0]
    rows = lax.broadcasted_iota(jnp.int32, (SUBS, LANES), 0)
    place = place_ref[0]
    thicks = [column(thick, k) for k in range(tiles)]
    sent = jnp.zeros((SUBS, LANES), jnp.float32)
    for g in range(4):
        for slot in range(send):
            sent = jnp.where(rows == g * send + slot, slots[0, slot, g].astype(jnp.float32), sent)
    team = (2 * edges + 3) * SUBS
    mine[team : team + SUBS, :] = sent
    copies[0].wait()
    copies[1].wait()
    for way, out in enumerate((near, odd, side, odd_side)):
        offset = 1 if way < 2 else 2
        first = (place // offset) % 2 == 0
        base = 0 if way < 2 else 2
        start = out.shape[0] - send * levels
        for slot in range(send):
            block = jnp.where(
                first, slots[0, slot, base + way % 2], slots[0, slot, base + 1 - way % 2]
            )
            safe = jnp.maximum(block, 0)
            depth = jnp.where(block >= 0, bottom[pl.ds(safe, 1), :], 0)
            at = pl.multiple_of(safe * LANES, LANES)
            for k in range(tiles):
                value = tracer[k * SUBS : (k + 1) * SUBS, pl.ds(at, LANES)]
                row = start + slot * levels + k * SUBS
                out[row : row + SUBS, :] = jnp.where(rows + k * SUBS < depth, value, ABSENT)
    for b in range(blocks):
        top = jnp.zeros((SUBS, LANES), jnp.float32)
        low = jnp.zeros((SUBS, LANES), jnp.float32)
        depth = bottom[b : b + 1, :]
        for k in range(tiles):
            layer = jnp.where(rows + k * SUBS < depth, thicks[k], 0.0)
            top = top + layer * tracer[k * SUBS : (k + 1) * SUBS, b * LANES : (b + 1) * LANES]
            low = low + layer
        row = 2 * edges * SUBS + b
        mine[row : row + 1, :] = jnp.sum(top, axis=0, keepdims=True) / jnp.sum(
            low, axis=0, keepdims=True
        )
    for copy in copies[2:]:
        copy.wait()
    for b in range(blocks):
        lanes = slice(b * LANES, (b + 1) * LANES)
        for j in range(edges):
            row = j * SUBS + b
            found = index[j : j + 1, lanes]
            mine[row : row + 1, :] = bounded(found, place, count, cells, send).astype(jnp.float32)
            row = (edges + j) * SUBS + b
            mine[row : row + 1, :] = weight[j : j + 1, lanes]
    row = (2 * edges + 1) * SUBS
    mine[row : row + SUBS, :] = velocity[...]
    mine[row + SUBS : row + 2 * SUBS, :] = ssh[...]
    for k in range(mine.shape[0] // SUBS):
        at = slice(k * SUBS, (k + 1) * SUBS)
        value = mine[at, :]
        near[at, :] = value
        side[at, :] = value
        far[at, :] = value


def bounded(index, place, count, cells, send):
    span = send * LANES
    result = index
    for g, offset in enumerate(OFFSETS):
        source = place - offset
        inside = jnp.logical_and(source >= 0, source < count)
        low = jnp.where(inside, cells + 4 * span, cells + g * span)
        mine = jnp.logical_and(index >= low, index < cells + (g + 1) * span)
        result = jnp.where(mine, cells + 4 * span, result)
    return result


def gathered(rows_of, index, weight, own, pairs):
    laplace = jnp.zeros_like(own)
    for j in range(len(index)):
        lane = jnp.bitwise_and(index[j], LANES - 1)
        block = jnp.right_shift(index[j], 7)
        got = jnp.zeros_like(own)
        for r in range(pairs):
            got = jnp.where(block == r, jnp.take_along_axis(rows_of(r), lane, axis=1), got)
        laplace = laplace + weight[j] * (got - own)
    return laplace


def stepped(laplace, forcing, own, speed):
    faster = (1.0 - friction) * speed + barotropic_step * (laplace + forcing)
    return own + barotropic_step * faster, faster


def pack_edges(heights, speeds, slots, rows, send, even, way_even, way_odd):
    out = [outgoing(h, s) for h, s in zip(heights, slots)]
    fast = [outgoing(v, slots[q]) for q, v in enumerate(speeds)]
    right = [
        heights[3],
        heights[2],
        blend(rows, send, {0: out[2], 2: out[1]}),
        blend(rows, send, {0: out[1], 1: out[3], 2: out[0]}),
        edge_rows(out[3], out[2], rows, send, True),
        edge_rows(fast[3], fast[2], rows, send, True),
    ]
    left = [
        heights[0],
        heights[1],
        blend(rows, send, {1: out[1], 3: out[2]}),
        blend(rows, send, {0: out[0], 1: out[2], 3: out[3]}),
        edge_rows(out[0], out[1], rows, send, False),
        edge_rows(fast[0], fast[1], rows, send, False),
    ]
    for k in range(len(right)):
        at = slice(k * SUBS, (k + 1) * SUBS)
        way_even[at, :] = jnp.where(even, right[k], left[k])
        way_odd[at, :] = jnp.where(even, left[k], right[k])


def edge_rows(inner, outer, rows, send, rightward):
    if rightward:
        return jnp.where(group_of(rows, send) == 3, pltpu.roll(outer, send, 0), inner)
    return jnp.where(group_of(rows, send) == 2, pltpu.roll(outer, SUBS - send, 0), inner)


def gather_team(
    place_ref, mine, near, side, far, index, weight, force, slots, height, speed, way_even, way_odd,
    *, send,
):
    edges = index.shape[1]
    place = place_ref[0]
    position = place % TEAM
    even = (place // TEAM) % 2 == 0
    rows = lax.broadcasted_iota(jnp.int32, (SUBS, LANES), 0)
    for flip, ref in enumerate((mine, near, side, far)):
        q = jnp.bitwise_xor(position, flip)
        for j in range(edges):
            index[q, j] = ref[j * SUBS : (j + 1) * SUBS, :].astype(jnp.int32)
            weight[q, j] = ref[(edges + j) * SUBS : (edges + j + 1) * SUBS, :]
        row = 2 * edges * SUBS
        force[q] = ref[row : row + SUBS, :]
        speed[q] = ref[row + SUBS : row + 2 * SUBS, :]
        height[q] = ref[row + 2 * SUBS : row + 3 * SUBS, :]
        slots[q] = ref[row + 3 * SUBS : row + 4 * SUBS, :].astype(jnp.int32)
    held = [slots[q] for q in range(TEAM)]
    pack_edges(
        [height[q] for q in range(TEAM)], [speed[q] for q in range(TEAM)], held, rows, send, even,
        way_even, way_odd,
    )

    def both(k, field):
        at = slice((6 + k) * SUBS, (7 + k) * SUBS)
        picked = [outgoing(field(q), held[q]) for q in range(TEAM)]
        right = edge_rows(picked[3], picked[2], rows, send, True)
        left = edge_rows(picked[0], picked[1], rows, send, False)
        way_even[at, :] = jnp.where(even, right, left)
        way_odd[at, :] = jnp.where(even, left, right)

    for j in range(edges):
        both(j, lambda q: index[q, j].astype(jnp.float32))
        both(edges + j, lambda q: weight[q, j])
    both(2 * edges, lambda q: force[q])


def double_step(
    place, index, weight, force, slots, height_in, speed_in, total_in, even_in, odd_in, first_even,
    first_odd, height, speed, total, ext, virtual, outer, *, send,
):
    edges = index.shape[1]
    even = (place // TEAM) % 2 == 0
    rows = lax.broadcasted_iota(jnp.int32, (SUBS, LANES), 0)
    held = [slots[q] for q in range(TEAM)]

    def side_of(k, constant, right):
        ref_even, ref_odd = (first_even, first_odd) if constant else (even_in, odd_in)
        at = slice(k * SUBS, (k + 1) * SUBS)
        a, b = ref_even[at, :], ref_odd[at, :]
        return jnp.where(even, a, b) if right else jnp.where(even, b, a)

    def fill(heights, left, right):
        out = [outgoing(h, s) for h, s in zip(heights, held)]
        halos = (
            {0: left, 1: out[1], 2: pltpu.roll(left, SUBS - send, 0), 3: out[2]},
            {0: out[0], 1: out[2], 2: left, 3: out[3]},
            {0: out[1], 1: out[3], 2: out[0], 3: right},
            {0: out[2], 1: right, 2: out[1], 3: pltpu.roll(right, send, 0)},
        )
        for q in range(TEAM):
            ext[q, 0:SUBS, :] = heights[q]
            ext[q, SUBS : 2 * SUBS, :] = blend(rows, send, halos[q])
        return out

    def advance_team(heights, speeds):
        moved = []
        for q in range(TEAM):
            laplace = gathered(
                lambda r: jnp.broadcast_to(ext[q, r : r + 1, :], (SUBS, LANES)),
                [index[q, j] for j in range(edges)],
                [weight[q, j] for j in range(edges)],
                heights[q],
                2 * SUBS,
            )
            moved.append(stepped(laplace, force[q], heights[q], speeds[q]))
        return [m[0] for m in moved], [m[1] for m in moved]

    heights = [height_in[q] for q in range(TEAM)]
    speeds = [speed_in[q] for q in range(TEAM)]
    edge = [side_of(4, False, right) for right in (False, True)]
    out = fill(heights, edge[0], edge[1])
    virtual[0, 0:SUBS, :] = side_of(0, False, False)
    virtual[0, SUBS : 2 * SUBS, :] = side_of(2, False, False) + blend(
        rows, send, {1: out[0], 3: out[1]}
    )
    virtual[1, 0:SUBS, :] = side_of(1, False, False)
    virtual[1, SUBS : 2 * SUBS, :] = side_of(3, False, False) + blend(rows, send, {3: out[0]})
    virtual[2, 0:SUBS, :] = side_of(0, False, True)
    virtual[2, SUBS : 2 * SUBS, :] = side_of(2, False, True) + blend(
        rows, send, {0: out[3], 2: out[2]}
    )
    virtual[3, 0:SUBS, :] = side_of(1, False, True)
    virtual[3, SUBS : 2 * SUBS, :] = side_of(3, False, True) + blend(rows, send, {2: out[3]})
    later, faster = advance_team(heights, speeds)
    for number, right in enumerate((False, True)):
        moved_group = 2 if right else 3
        laplace = gathered(
            lambda r: jnp.where(
                group_of(rows, send) == moved_group,
                virtual[2 * number + 1, r : r + 1, :],
                virtual[2 * number, r : r + 1, :],
            ),
            [side_of(6 + j, True, right).astype(jnp.int32) for j in range(edges)],
            [side_of(6 + edges + j, True, right) for j in range(edges)],
            edge[number],
            2 * SUBS,
        )
        edge[number] = stepped(
            laplace, side_of(6 + 2 * edges, True, right), edge[number], side_of(5, False, right)
        )[0]
    fill(later, edge[0], edge[1])
    last, fastest = advance_team(later, faster)
    for q in range(TEAM):
        height[q] = last[q]
        speed[q] = fastest[q]
        before = 0.0 if total_in is None else total_in[q]
        total[q] = before + faster[q] + fastest[q]
    return last, fastest, held, rows, even


def first_pair(
    place, index, weight, force, slots, height_in, speed_in, even_in, odd_in, height, speed, total,
    way_even, way_odd, ext, virtual, *, send,
):
    last, fastest, held, rows, even = double_step(
        place[0], index, weight, force, slots, height_in, speed_in, None, even_in, odd_in, even_in,
        odd_in, height, speed, total, ext, virtual, None, send=send,
    )
    pack_edges(last, fastest, held, rows, send, even, way_even, way_odd)


def middle_pair(
    place, index, weight, force, slots, height_in, speed_in, total_in, even_in, odd_in, first_even,
    first_odd, height, speed, total, way_even, way_odd, ext, virtual, *, send,
):
    last, fastest, held, rows, even = double_step(
        place[0], index, weight, force, slots, height_in, speed_in, total_in, even_in, odd_in,
        first_even, first_odd, height, speed, total, ext, virtual, None, send=send,
    )
    pack_edges(last, fastest, held, rows, send, even, way_even, way_odd)


def last_pair(
    place, profile, index, weight, force, slots, height_in, speed_in, total_in, even_in, odd_in,
    first_even, first_odd, bottom, base, new_height, new_speed, out, height, speed, total, ext,
    virtual, *, send,
):
    double_step(
        place[0], index, weight, force, slots, height_in, speed_in, total_in, even_in, odd_in,
        first_even, first_odd, height, speed, total, ext, virtual, None, send=send,
    )
    position = place[0] % TEAM
    new_height[...] = height[position]
    new_speed[...] = speed[position]
    ext[0, 0:SUBS, :] = total[position] / SUBSTEPS
    rows = lax.broadcasted_iota(jnp.int32, (SUBS, LANES), 0)
    for k in range(out.shape[0] // SUBS):
        shape = column(profile, k)
        for i in range(out.shape[1] // LANES):
            at = (slice(k * SUBS, (k + 1) * SUBS), slice(i * LANES, (i + 1) * LANES))
            added = jnp.where(rows + k * SUBS < bottom[i : i + 1, :], shape, 0.0)
            out[at] = base[at] + added * ext[0, i : i + 1, :]


def tracer_base(meta, tracer, bottom, index, weight, a, b, c, d, out, held, *, count, send):
    levels, cells = tracer.shape
    tiles = levels // SUBS
    blocks = cells // LANES
    edges = index.shape[0]
    arrived = (a, b, c, d)
    rows = lax.broadcasted_iota(jnp.int32, (SUBS, LANES), 0)
    place = meta[0]
    for i in range(blocks):
        depth = bottom[i : i + 1, :]
        for k in range(tiles):
            at = (slice(k * SUBS, (k + 1) * SUBS), slice(i * LANES, (i + 1) * LANES))
            held[at] = jnp.where(rows + k * SUBS < depth, tracer[at], ABSENT)

    def cell_block(i, carry):
        at = pl.multiple_of(i * LANES, LANES)
        lanes = pl.ds(at, LANES)
        depth = bottom[pl.ds(i, 1), :]
        mine = [tracer[k * SUBS : (k + 1) * SUBS, lanes] for k in range(tiles)]
        flat = [jnp.zeros((SUBS, LANES), jnp.float32) for _ in range(tiles)]
        for j in range(edges):
            near = localize(index[j : j + 1, lanes], place, count, cells, send)
            near = jnp.broadcast_to(near, (SUBS, LANES))
            lane = jnp.bitwise_and(near, LANES - 1)
            block = jnp.right_shift(near, 7)
            factor = weight[j : j + 1, lanes]
            got = [jnp.full((SUBS, LANES), ABSENT, jnp.float32) for _ in range(tiles)]
            for r in range(blocks + 4 * send):
                here = block == r
                for k in range(tiles):
                    if r < blocks:
                        source = held[k * SUBS : (k + 1) * SUBS, r * LANES : (r + 1) * LANES]
                    else:
                        ref = arrived[(r - blocks) // send]
                        start = ref.shape[0] - send * levels
                        row = start + (r - blocks) % send * levels + k * SUBS
                        source = ref[row : row + SUBS, :]
                    got[k] = jnp.where(here, jnp.take_along_axis(source, lane, axis=1), got[k])
            for k in range(tiles):
                flat[k] = flat[k] + factor * jnp.where(got[k] < PRESENT, got[k] - mine[k], 0.0)
        for k in range(tiles):
            first = rows + k * SUBS
            value = mine[k]
            up = pltpu.roll(value, SUBS - 1, 0)
            if k + 1 < tiles:
                up = jnp.where(rows == SUBS - 1, pltpu.roll(mine[k + 1], SUBS - 1, 0), up)
            down = pltpu.roll(value, 1, 0)
            if k > 0:
                down = jnp.where(rows == 0, pltpu.roll(mine[k - 1], 1, 0), down)
            below = jnp.where(first + 1 < jnp.minimum(depth, levels), up - value, 0.0)
            above = jnp.where(first > 0, down - value, 0.0)
            moved = horizontal_rate * flat[k] + vertical_rate * (below + above)
            out[k * SUBS : (k + 1) * SUBS, lanes] = value + tracer_step * jnp.where(
                first < depth, moved, 0.0
            )
        return carry

    lax.fori_loop(0, blocks, cell_block, 0)


def shards(
    tracer, bottom_levels, neighbours, edge_weight, ssh, velocity, send_blocks, thickness, profile
):
    count = lax.axis_size("dom")
    levels, cells = tracer.shape
    send = send_blocks.shape[-1]
    edges = neighbours.shape[0]
    blocks = cells // LANES
    assert blocks == SUBS and 4 * send == SUBS and levels % SUBS == 0 and count % (2 * TEAM) == 0
    assert SUBSTEPS == 6
    tile = (blocks, LANES)
    place = lax.axis_index("dom").astype(jnp.int32)[None]
    slots = jnp.swapaxes(send_blocks, 1, 2)
    bottom = bottom_levels.reshape(tile)

    def shape(rows, kind=jnp.float32):
        return jax.ShapeDtypeStruct(rows, kind)

    def call(body, name, outs, ins, scratch, flops, limit=4):
        return pl.pallas_call(
            functools.partial(body, send=send),
            out_shape=outs,
            in_specs=ins,
            scratch_shapes=scratch,
            compiler_params=pltpu.CompilerParams(vmem_limit_bytes=limit << 20),
            cost_estimate=pl.CostEstimate(flops=flops, bytes_accessed=1000, transcendentals=0),
            name=name,
        )

    own = (2 * edges + 4) * SUBS
    halo = send * levels
    near, side, far, odd, odd_side, mine = call(
        functools.partial(prepare, count=count),
        "prepare",
        [
            shape((own + halo, LANES)),
            shape((own + halo, LANES)),
            shape((own, LANES)),
            shape((halo, LANES)),
            shape((halo, LANES)),
            shape((own, LANES)),
        ],
        [SMEM, SMEM, SMEM] + [HBM] * 6,
        [
            pltpu.VMEM(tracer.shape, jnp.float32),
            pltpu.VMEM(tile, jnp.int32),
            pltpu.VMEM(neighbours.shape, jnp.int32),
            pltpu.VMEM(edge_weight.shape, jnp.float32),
            pltpu.VMEM(tile, jnp.float32),
            pltpu.VMEM(tile, jnp.float32),
            pltpu.SemaphoreType.DMA((6,)),
        ],
        4000000,
    )(
        place, slots, thickness, tracer, bottom, neighbours, edge_weight, ssh.reshape(tile),
        velocity.reshape(tile),
    )
    side = lax.ppermute(side, "dom", even_swap(count, 2))
    far = lax.ppermute(far, "dom", even_swap(count, 3))
    near = lax.ppermute(near, "dom", even_swap(count, 1))
    odd = lax.ppermute(odd, "dom", odd_swap(count, 1))
    odd_side = lax.ppermute(odd_side, "dom", odd_swap(count, 2))

    def swap(pair):
        return (
            lax.ppermute(pair[0], "dom", even_swap(count, TEAM)),
            lax.ppermute(pair[1], "dom", odd_swap(count, TEAM)),
        )

    state = [shape((TEAM,) + tile)] * 2
    entire = (6 + 2 * edges + 1) * SUBS
    *tables, height, speed, way_even, way_odd = call(
        gather_team,
        "gather_team",
        [
            shape((TEAM, edges) + tile, jnp.int32),
            shape((TEAM, edges) + tile),
            shape((TEAM,) + tile),
            shape((TEAM,) + tile, jnp.int32),
        ]
        + state
        + [shape((entire, LANES))] * 2,
        [SMEM] + [VMEM] * 4,
        [],
        500000,
    )(place, mine, near, side, far)
    constant = swap((way_even, way_odd))
    base = call(
        functools.partial(tracer_base, count=count),
        "tracer_base",
        shape(tracer.shape),
        [SMEM] + [VMEM] * 8,
        [pltpu.VMEM(tracer.shape, jnp.float32)],
        20000000,
    )(place, tracer, bottom, neighbours, edge_weight, near, odd, side, odd_side)
    scratch = [pltpu.VMEM((TEAM, 2 * SUBS, LANES), jnp.float32)] * 2
    light = [shape((6 * SUBS, LANES))] * 2
    height, speed, total, *ways = call(
        first_pair, "first_pair", state + state[:1] + light, [SMEM] + [VMEM] * 8, scratch, 2000000
    )(place, *tables, height, speed, *constant)
    arrived = swap(ways)
    height, speed, total, *ways = call(
        middle_pair, "middle_pair", state + state[:1] + light, [SMEM] + [VMEM] * 11, scratch, 2000000
    )(place, *tables, height, speed, total, *arrived, *constant)
    arrived = swap(ways)
    team_scratch = [pltpu.VMEM((TEAM,) + tile, jnp.float32)] * 3
    height, speed, result = call(
        last_pair,
        "last_pair",
        [shape(tile), shape(tile), shape(tracer.shape)],
        [SMEM, SMEM] + [VMEM] * 13,
        team_scratch + scratch,
        2500000,
    )(place, profile, *tables, height, speed, total, *arrived, *constant, bottom, base)
    return (result, height.reshape(-1), speed.reshape(-1))


def solution(mesh):
    placed = (
        P(None, "dom"),
        P("dom"),
        P(None, "dom"),
        P(None, "dom"),
        P("dom"),
        P("dom"),
        P("dom", None, None),
        P(),
        P(),
    )
    return jax.shard_map(
        shards,
        mesh=mesh,
        in_specs=placed,
        out_specs=(P(None, "dom"), P("dom"), P("dom")),
        check_vma=False,
    )
```

time: 76.6 us -> 37.9 us (0.49)
  starting transfers between devices: 34.4 us -> 12.9 us
  Pallas kernels: 18.6 us -> 11.4 us
  local copies, waits for them, and re-layouts: 10.9 us -> 3.8 us
  waiting for transfers between devices: 10.4 us -> 8.55 us
    ppermute x24 -> x11, starting transfers between devices: 34.4 us -> 12.9 us  [the longest x3 3.62 us: swap(): lax.ppermute(pair[0], 'dom', even_swap(count, TEAM))]
    pallas_call x8 -> x6, Pallas kernels: 18.6 us -> 11.4 us  [the longest x1 5.1 us: shards(): call(functools.partial(tracer_base, count=count), 'tracer_base', shape(tr...]
    unnamed x91 -> x24, local copies, waits for them, and re-layouts: 10.2 us -> 3.8 us
    ppermute x24 -> x11, waiting for transfers between devices: 10.4 us -> 8.55 us  [the longest x1 4.39 us: shards(): far = lax.ppermute(far, 'dom', even_swap(count, 3))]
  transfers between devices with their start and end apart: 24 -> 11, of which waited for: 8 -> 3; matrix products, arithmetic and copies ran while one was open for 0% -> 0% of each run, Pallas kernels for 9% -> 17%
where the time goes in v3:
time: 37.9 us; the launch traced here: 37.5 us
  starting transfers between devices  12.9 us (34%)
  Pallas kernels  11.4 us (30%)
  waiting for transfers between devices  8.55 us (23%)
  local copies, waits for them, and re-layouts  3.8 us (10%)
  between operations  0.79 us (2%)
    pallas_call x1, Pallas kernels, shards(): call(functools.partial(tracer_base, count=count), 'tracer_base', shape(tr...  5.1 us
    ppermute x1, waiting for transfers between devices, shards(): far = lax.ppermute(far, 'dom', even_swap(count, 3))  4.39 us
    unnamed x24, local copies, waits for them, and re-layouts  3.8 us
    ppermute x3, starting transfers between devices, swap(): lax.ppermute(pair[0], 'dom', even_swap(count, TEAM))  3.62 us
    ppermute x1, starting transfers between devices, shards(): odd = lax.ppermute(odd, 'dom', odd_swap(count, 1))  3.35 us
    pallas_call x1, Pallas kernels, shards(): call(last_pair, 'last_pair', [shape(tile), shape(tile), shape(tracer.shap...  2.53 us
    ppermute x3, waiting for transfers between devices, swap(): lax.ppermute(pair[0], 'dom', even_swap(count, TEAM))  2.53 us
    ppermute x1, starting transfers between devices, shards(): odd_side = lax.ppermute(odd_side, 'dom', odd_swap(count, 2))  2.05 us
  transfers between devices with their start and end apart: 11, of which 3 were waited for; matrix products, arithmetic and copies ran while one was open for 0% of the time, Pallas kernels for 17%

profile of v3, /device:TPU:9, one launch (start us, length us, event | category | flops | bytes accessed | tf_op | source)
XLA Modules:
  0.0 37.5 jit_solution(12598074846322996102)
XLA Ops:
  0.6 0.0 copy-start.10
  0.6 0.0 copy-start.8
  0.7 0.0 copy-start.7
  0.7 0.0 copy-start.6
  0.7 0.0 copy-start.9
  0.7 0.6 %copy-done.10 = f32[40]{0:T(128)S(1)} copy-done((f32[40]{0:T(128)S(1)}, f32[40]{0:T(128)}, u32[]{:S(2)}) %copy-start.10) | copy-done | bytes 184
  1.3 0.0 copy-done.8
  1.3 0.0 copy-done.7
  1.4 0.0 copy-done.6
  1.4 0.0 copy-done.9
  1.4 0.0 copy-start
  1.4 0.9 %copy-done = f32[40,1024]{1,0:T(8,128)S(1)} copy-done((f32[40,1024]{1,0:T(8,128)S(1)}, f32[40,1024]{1,0:T(8,128)}, u32[]{:S(2)}) %copy-start) | copy-done | bytes 163864
  2.3 0.0 copy-start.2
  2.3 0.8 %copy-done.2 = s32[6,1024]{1,0:T(8,128)S(1)} copy-done((s32[6,1024]{1,0:T(8,128)S(1)}, s32[6,1024]{1,0:T(8,128)}, u32[]{:S(2)}) %copy-start.2) | copy-done | bytes 24600
  3.1 0.0 copy-start.4
  3.1 0.8 %copy-done.4 = f32[6,1024]{1,0:T(8,128)S(1)} copy-done((f32[6,1024]{1,0:T(8,128)S(1)}, f32[6,1024]{1,0:T(8,128)}, u32[]{:S(2)}) %copy-start.4) | copy-done | bytes 24600
  3.8 1.1 %prepare.1 = (f32[208,128]{1,0:T(8,128)S(1)}, f32[208,128]{1,0:T(8,128)S(1)}, f32[128,128]{1,0:T(8,128)S(1)}, f32[80,128]{1,0:T(8,128)S(1)}, f32[80,128]{1,0:T(8,128)S(1)}, /*index=5*/f32[128,128]{1,0:T(8,128)S(1)}) custom-call(s32[1]{0:T(128)} %bitcast.place_ref.place.meta, s32[1,2,4]{2,1,0:T(2,128)S(1)} %bitcast.12, f32[40]{0:T(128)S(1)} %copy-done.10, ...), custom_call_target="tpu_custom_call" | custom-call | flops 4000000 | bytes 1000 | tf_op jit(solution)/shard_map/prepare/pallas_call | solution.py:475
  5.0 0.7 %collective-permute-start = (f32[208,128]{1,0:T(8,128)S(1)}, f32[208,128]{1,0:T(8,128)S(1)}, u32[]{:S(2)}, u32[]{:S(2)}) collective-permute-start(f32[208,128]{1,0:T(8,128)S(1)} %get-tuple-element.31), channel_id=1, source_target_pairs={{0,1},{1,0},{2,3},{3,2},{4,5},{5,4},{6,7},{7,6},{8,9},{9,8},{10,11... | collective-permute-start | bytes 319496 | tf_op jit(solution)/shard_map/ppermute | solution.py:503
  5.7 1.2 %collective-permute-start.1 = (f32[208,128]{1,0:T(8,128)S(1)}, f32[208,128]{1,0:T(8,128)S(1)}, u32[]{:S(2)}, u32[]{:S(2)}) collective-permute-start(f32[208,128]{1,0:T(8,128)S(1)} %get-tuple-element.32), channel_id=1, source_target_pairs={{0,2},{1,3},{2,0},{3,1},{4,6},{5,7},{6,4},{7,5},{8,10},{9,11},{10,... | collective-permute-start | bytes 319496 | tf_op jit(solution)/shard_map/ppermute | solution.py:501
  6.9 0.5 %collective-permute-start.2 = (f32[128,128]{1,0:T(8,128)S(1)}, f32[128,128]{1,0:T(8,128)S(1)}, u32[]{:S(2)}, u32[]{:S(2)}) collective-permute-start(f32[128,128]{1,0:T(8,128)S(1)} %get-tuple-element.33), channel_id=1, source_target_pairs={{0,3},{1,2},{2,1},{3,0},{4,7},{5,6},{6,5},{7,4},{8,11},{9,10},{10,... | collective-permute-start | bytes 196616 | tf_op jit(solution)/shard_map/ppermute | solution.py:502
  7.4 4.4 %collective-permute-done.2.far = f32[128,128]{1,0:T(8,128)S(1)} collective-permute-done((f32[128,128]{1,0:T(8,128)S(1)}, f32[128,128]{1,0:T(8,128)S(1)}, u32[]{:S(2)}, u32[]{:S(2)}) %collective-permute-start.2) | collective-permute-done | bytes 65568 | tf_op jit(solution)/shard_map/ppermute | solution.py:502
  11.8 0.0 collective-permute-done.near.a
  11.8 0.0 collective-permute-done.1.side.c
  11.8 0.1 gather_team.1
  11.9 1.3 %collective-permute-start.3 = (f32[152,128]{1,0:T(8,128)S(1)}, f32[152,128]{1,0:T(8,128)S(1)}, u32[]{:S(2)}, u32[]{:S(2)}) collective-permute-start(f32[152,128]{1,0:T(8,128)S(1)} %get-tuple-element.40), channel_id=1, source_target_pairs={{0,4},{1,5},{2,6},{3,7},{4,0},{5,1},{6,2},{7,3},{8,12},{9,13},{10,... | collective-permute-start | bytes 233480 | tf_op jit(solution)/shard_map/ppermute | solution.py:509
  13.2 0.0 collective-permute-start.4
  13.2 2.5 %collective-permute-done.3.even_in.first_even = f32[152,128]{1,0:T(8,128)S(1)} collective-permute-done((f32[152,128]{1,0:T(8,128)S(1)}, f32[152,128]{1,0:T(8,128)S(1)}, u32[]{:S(2)}, u32[]{:S(2)}) %collective-permute-start.3) | collective-permute-done | bytes 77856 | tf_op jit(solution)/shard_map/ppermute | solution.py:509
  15.7 1.6 %collective-permute-done.4.odd_in.first_odd = f32[152,128]{1,0:T(8,128)S(1)} collective-permute-done((f32[152,128]{1,0:T(8,128)S(1)}, f32[152,128]{1,0:T(8,128)S(1)}, u32[]{:S(2)}, u32[]{:S(2)}) %collective-permute-start.4) | collective-permute-done | bytes 77856 | tf_op jit(solution)/shard_map/ppermute | solution.py:510
  17.3 1.3 %first_pair.1 = (f32[4,8,128]{2,1,0:T(8,128)S(1)}, f32[4,8,128]{2,1,0:T(8,128)S(1)}, f32[4,8,128]{2,1,0:T(8,128)S(1)}, f32[48,128]{1,0:T(8,128)S(1)}, f32[48,128]{1,0:T(8,128)S(1)}) custom-call(s32[1]{0:T(128)} %bitcast.place_ref.place.meta, s32[4,6,8,128]{3,2,1,0:T(8,128)S(1)} %get-tuple-element.34.index, f32[4,6,8,128]{3,2,1,0:T(8,128)S(1)} %get-tuple-element.35.weight, ...), custom_call_target="tpu_custom_call" | custom-call | flops 2000000 | bytes 1000 | tf_op jit(solution)/shard_map/first_pair/pallas_call | solution.py:541
  18.6 0.4 %collective-permute-start.5 = (f32[48,128]{1,0:T(8,128)S(1)}, f32[48,128]{1,0:T(8,128)S(1)}, u32[]{:S(2)}, u32[]{:S(2)}) collective-permute-start(f32[48,128]{1,0:T(8,128)S(1)} %get-tuple-element.45), channel_id=1, source_target_pairs={{0,4},{1,5},{2,6},{3,7},{4,0},{5,1},{6,2},{7,3},{8,12},{9,13},{10,... | collective-permute-start | bytes 73736 | tf_op jit(solution)/shard_map/ppermute | solution.py:509
  19.0 0.0 collective-permute-start.6
  19.0 3.3 %collective-permute-start.9 = (f32[80,128]{1,0:T(8,128)S(1)}, f32[80,128]{1,0:T(8,128)S(1)}, u32[]{:S(2)}, u32[]{:S(2)}) collective-permute-start(f32[80,128]{1,0:T(8,128)S(1)} %get-tuple-element.52), channel_id=1, source_target_pairs={{1,2},{3,4},{5,6},{7,8},{9,10},{11,12},{13,14},{15,16},{17,18},{19... | collective-permute-start | bytes 122888 | tf_op jit(solution)/shard_map/ppermute | solution.py:504
  22.4 2.1 %collective-permute-start.10 = (f32[80,128]{1,0:T(8,128)S(1)}, f32[80,128]{1,0:T(8,128)S(1)}, u32[]{:S(2)}, u32[]{:S(2)}) collective-permute-start(f32[80,128]{1,0:T(8,128)S(1)} %get-tuple-element.53), channel_id=1, source_target_pairs={{2,4},{3,5},{6,8},{7,9},{10,12},{11,13},{14,16},{15,17},{18,20},{1... | collective-permute-start | bytes 122888 | tf_op jit(solution)/shard_map/ppermute | solution.py:505
  24.4 0.0 collective-permute-done.5.even_in
  24.4 0.0 collective-permute-done.6.odd_in
  24.4 0.0 copy-start.1
  24.4 0.0 copy-start.3
  24.5 0.0 copy-start.5
  24.5 1.3 %middle_pair.1 = (f32[4,8,128]{2,1,0:T(8,128)S(1)}, f32[4,8,128]{2,1,0:T(8,128)S(1)}, f32[4,8,128]{2,1,0:T(8,128)S(1)}, f32[48,128]{1,0:T(8,128)S(1)}, f32[48,128]{1,0:T(8,128)S(1)}) custom-call(s32[1]{0:T(128)} %bitcast.place_ref.place.meta, s32[4,6,8,128]{3,2,1,0:T(8,128)S(1)} %get-tuple-element.34.index, f32[4,6,8,128]{3,2,1,0:T(8,128)S(1)} %get-tuple-element.35.weight, ...), custom_call_target="tpu_custom_call" | custom-call | flops 2000000 | bytes 1000 | tf_op jit(solution)/shard_map/middle_pair/pallas_call | solution.py:545
  25.8 1.9 %collective-permute-start.7 = (f32[48,128]{1,0:T(8,128)S(1)}, f32[48,128]{1,0:T(8,128)S(1)}, u32[]{:S(2)}, u32[]{:S(2)}) collective-permute-start(f32[48,128]{1,0:T(8,128)S(1)} %get-tuple-element.50), channel_id=1, source_target_pairs={{0,4},{1,5},{2,6},{3,7},{4,0},{5,1},{6,2},{7,3},{8,12},{9,13},{10,... | collective-permute-start | bytes 73736 | tf_op jit(solution)/shard_map/ppermute | solution.py:509
  27.7 1.4 %collective-permute-start.8 = (f32[48,128]{1,0:T(8,128)S(1)}, f32[48,128]{1,0:T(8,128)S(1)}, u32[]{:S(2)}, u32[]{:S(2)}) collective-permute-start(f32[48,128]{1,0:T(8,128)S(1)} %get-tuple-element.51), channel_id=1, source_target_pairs={{4,8},{5,9},{6,10},{7,11},{12,16},{13,17},{14,18},{15,19},{20,24},... | collective-permute-start | bytes 73736 | tf_op jit(solution)/shard_map/ppermute | solution.py:510
  29.2 0.0 collective-permute-done.9.b
  29.2 0.0 collective-permute-done.10.d
  29.2 0.0 copy-done.1
  29.2 0.0 copy-done.3
  29.2 0.0 copy-done.5
  29.2 5.1 %tracer_base.1.base = f32[40,1024]{1,0:T(8,128)S(1)} custom-call(s32[1]{0:T(128)} %bitcast.place_ref.place.meta, f32[40,1024]{1,0:T(8,128)S(1)} %copy-done.1, s32[8,128]{1,0:T(8,128)S(1)} %bitcast.8, s32[6,1024]{1,0:T(8,128)S(1)} %copy-done.3, f32[6,1024]{1,0:T(8,128)S(1)} %copy-done.5, f32[208,128]{1,0:T(8,128)S(1)} %collective-permute-done.near.a, ...), custom_call_target="tpu_custom_call" | custom-call | flops 20000000 | bytes 1000 | tf_op jit(solution)/shard_map/tracer_base/pallas_call | solution.py:531
  34.3 0.0 collective-permute-done.7.even_in
  34.3 0.0 collective-permute-done.8.odd_in
  34.3 0.0 copy-start.11
  34.3 0.6 %copy-done.11 = f32[40]{0:T(128)S(1)} copy-done((f32[40]{0:T(128)S(1)}, f32[40]{0:T(128)}, u32[]{:S(2)}) %copy-start.11) | copy-done | bytes 184
  35.0 2.5 %last_pair.1 = (f32[8,128]{1,0:T(8,128)}, f32[8,128]{1,0:T(8,128)}, f32[40,1024]{1,0:T(8,128)}) custom-call(s32[1]{0:T(128)} %bitcast.place_ref.place.meta, f32[40]{0:T(128)S(1)} %copy-done.11, s32[4,6,8,128]{3,2,1,0:T(8,128)S(1)} %get-tuple-element.34.index, f32[4,6,8,128]{3,2,1,0:T(8,128)S(1)} %get-tuple-element.35.weight, ...), custom_call_target="tpu_custom_call" | custom-call | flops 2500000 | bytes 1000 | tf_op jit(solution)/shard_map/last_pair/pallas_call | solution.py:550
Async XLA Ops:
  0.6 0.7 %copy-start.10 = (f32[40]{0:T(128)S(1)}, f32[40]{0:T(128)}, u32[]{:S(2)}) copy-start(f32[40]{0:T(128)} %thick.1) | copy-start | bytes 484
  0.6 0.7 %copy-start.8 = (f32[1024]{0:T(1024)S(1)}, f32[1024]{0:T(1024)}, u32[]{:S(2)}) copy-start(f32[1024]{0:T(1024)} %param.14) | copy-start | bytes 12292
  0.7 0.7 %copy-start.7 = (f32[1024]{0:T(1024)S(1)}, f32[1024]{0:T(1024)}, u32[]{:S(2)}) copy-start(f32[1024]{0:T(1024)} %param.13) | copy-start | bytes 12292
  0.7 0.7 %copy-start.6 = (s32[1024]{0:T(1024)S(1)}, s32[1024]{0:T(1024)}, u32[]{:S(2)}) copy-start(s32[1024]{0:T(1024)} %param.10) | copy-start | bytes 12292
  0.7 0.7 %copy-start.9 = (s32[1,4,2]{1,2,0:T(2,128)S(1)}, s32[1,4,2]{1,2,0:T(2,128)}, u32[]{:S(2)}) copy-start(s32[1,4,2]{1,2,0:T(2,128)} %param.15) | copy-start | bytes 100
  1.4 0.9 %copy-start = (f32[40,1024]{1,0:T(8,128)S(1)}, f32[40,1024]{1,0:T(8,128)}, u32[]{:S(2)}) copy-start(f32[40,1024]{1,0:T(8,128)} %tracer.1) | copy-start | bytes 491524
  2.3 0.8 %copy-start.2 = (s32[6,1024]{1,0:T(8,128)S(1)}, s32[6,1024]{1,0:T(8,128)}, u32[]{:S(2)}) copy-start(s32[6,1024]{1,0:T(8,128)} %index.1) | copy-start | bytes 73732
  3.1 0.8 %copy-start.4 = (f32[6,1024]{1,0:T(8,128)S(1)}, f32[6,1024]{1,0:T(8,128)}, u32[]{:S(2)}) copy-start(f32[6,1024]{1,0:T(8,128)} %weight.1) | copy-start | bytes 73732
  5.0 6.8 %collective-permute-start = (f32[208,128]{1,0:T(8,128)S(1)}, f32[208,128]{1,0:T(8,128)S(1)}, u32[]{:S(2)}, u32[]{:S(2)}) collective-permute-start(f32[208,128]{1,0:T(8,128)S(1)} %get-tuple-element.31), channel_id=1, source_target_pairs={{0,1},{1,0},{2,3},{3,2},{4,5},{5,4},{6,7},{7,6},{8,9},{9,8},{10,11... | collective-permute-start | bytes 319496 | tf_op jit(solution)/shard_map/ppermute | solution.py:503
  5.7 6.1 %collective-permute-start.1 = (f32[208,128]{1,0:T(8,128)S(1)}, f32[208,128]{1,0:T(8,128)S(1)}, u32[]{:S(2)}, u32[]{:S(2)}) collective-permute-start(f32[208,128]{1,0:T(8,128)S(1)} %get-tuple-element.32), channel_id=1, source_target_pairs={{0,2},{1,3},{2,0},{3,1},{4,6},{5,7},{6,4},{7,5},{8,10},{9,11},{10,... | collective-permute-start | bytes 319496 | tf_op jit(solution)/shard_map/ppermute | solution.py:501
  6.9 4.9 %collective-permute-start.2 = (f32[128,128]{1,0:T(8,128)S(1)}, f32[128,128]{1,0:T(8,128)S(1)}, u32[]{:S(2)}, u32[]{:S(2)}) collective-permute-start(f32[128,128]{1,0:T(8,128)S(1)} %get-tuple-element.33), channel_id=1, source_target_pairs={{0,3},{1,2},{2,1},{3,0},{4,7},{5,6},{6,5},{7,4},{8,11},{9,10},{10,... | collective-permute-start | bytes 196616 | tf_op jit(solution)/shard_map/ppermute | solution.py:502
  11.9 3.8 %collective-permute-start.3 = (f32[152,128]{1,0:T(8,128)S(1)}, f32[152,128]{1,0:T(8,128)S(1)}, u32[]{:S(2)}, u32[]{:S(2)}) collective-permute-start(f32[152,128]{1,0:T(8,128)S(1)} %get-tuple-element.40), channel_id=1, source_target_pairs={{0,4},{1,5},{2,6},{3,7},{4,0},{5,1},{6,2},{7,3},{8,12},{9,13},{10,... | collective-permute-start | bytes 233480 | tf_op jit(solution)/shard_map/ppermute | solution.py:509
  13.2 4.1 %collective-permute-start.4 = (f32[152,128]{1,0:T(8,128)S(1)}, f32[152,128]{1,0:T(8,128)S(1)}, u32[]{:S(2)}, u32[]{:S(2)}) collective-permute-start(f32[152,128]{1,0:T(8,128)S(1)} %get-tuple-element.41), channel_id=1, source_target_pairs={{4,8},{5,9},{6,10},{7,11},{12,16},{13,17},{14,18},{15,19},{20,24},... | collective-permute-start | bytes 233480 | tf_op jit(solution)/shard_map/ppermute | solution.py:510
  18.6 5.8 %collective-permute-start.5 = (f32[48,128]{1,0:T(8,128)S(1)}, f32[48,128]{1,0:T(8,128)S(1)}, u32[]{:S(2)}, u32[]{:S(2)}) collective-permute-start(f32[48,128]{1,0:T(8,128)S(1)} %get-tuple-element.45), channel_id=1, source_target_pairs={{0,4},{1,5},{2,6},{3,7},{4,0},{5,1},{6,2},{7,3},{8,12},{9,13},{10,... | collective-permute-start | bytes 73736 | tf_op jit(solution)/shard_map/ppermute | solution.py:509
  19.0 5.4 %collective-permute-start.6 = (f32[48,128]{1,0:T(8,128)S(1)}, f32[48,128]{1,0:T(8,128)S(1)}, u32[]{:S(2)}, u32[]{:S(2)}) collective-permute-start(f32[48,128]{1,0:T(8,128)S(1)} %get-tuple-element.46), channel_id=1, source_target_pairs={{4,8},{5,9},{6,10},{7,11},{12,16},{13,17},{14,18},{15,19},{20,24},... | collective-permute-start | bytes 73736 | tf_op jit(solution)/shard_map/ppermute | solution.py:510
  19.0 10.1 %collective-permute-start.9 = (f32[80,128]{1,0:T(8,128)S(1)}, f32[80,128]{1,0:T(8,128)S(1)}, u32[]{:S(2)}, u32[]{:S(2)}) collective-permute-start(f32[80,128]{1,0:T(8,128)S(1)} %get-tuple-element.52), channel_id=1, source_target_pairs={{1,2},{3,4},{5,6},{7,8},{9,10},{11,12},{13,14},{15,16},{17,18},{19... | collective-permute-start | bytes 122888 | tf_op jit(solution)/shard_map/ppermute | solution.py:504
  22.4 6.8 %collective-permute-start.10 = (f32[80,128]{1,0:T(8,128)S(1)}, f32[80,128]{1,0:T(8,128)S(1)}, u32[]{:S(2)}, u32[]{:S(2)}) collective-permute-start(f32[80,128]{1,0:T(8,128)S(1)} %get-tuple-element.53), channel_id=1, source_target_pairs={{2,4},{3,5},{6,8},{7,9},{10,12},{11,13},{14,16},{15,17},{18,20},{1... | collective-permute-start | bytes 122888 | tf_op jit(solution)/shard_map/ppermute | solution.py:505
  24.4 4.7 %copy-start.1 = (f32[40,1024]{1,0:T(8,128)S(1)}, f32[40,1024]{1,0:T(8,128)}, u32[]{:S(2)}) copy-start(f32[40,1024]{1,0:T(8,128)} %tracer.1) | copy-start | bytes 491524
  24.4 4.7 %copy-start.3 = (s32[6,1024]{1,0:T(8,128)S(1)}, s32[6,1024]{1,0:T(8,128)}, u32[]{:S(2)}) copy-start(s32[6,1024]{1,0:T(8,128)} %index.1) | copy-start | bytes 73732
  24.5 4.7 %copy-start.5 = (f32[6,1024]{1,0:T(8,128)S(1)}, f32[6,1024]{1,0:T(8,128)}, u32[]{:S(2)}) copy-start(f32[6,1024]{1,0:T(8,128)} %weight.1) | copy-start | bytes 73732
  25.8 8.5 %collective-permute-start.7 = (f32[48,128]{1,0:T(8,128)S(1)}, f32[48,128]{1,0:T(8,128)S(1)}, u32[]{:S(2)}, u32[]{:S(2)}) collective-permute-start(f32[48,128]{1,0:T(8,128)S(1)} %get-tuple-element.50), channel_id=1, source_target_pairs={{0,4},{1,5},{2,6},{3,7},{4,0},{5,1},{6,2},{7,3},{8,12},{9,13},{10,... | collective-permute-start | bytes 73736 | tf_op jit(solution)/shard_map/ppermute | solution.py:509
  27.7 6.6 %collective-permute-start.8 = (f32[48,128]{1,0:T(8,128)S(1)}, f32[48,128]{1,0:T(8,128)S(1)}, u32[]{:S(2)}, u32[]{:S(2)}) collective-permute-start(f32[48,128]{1,0:T(8,128)S(1)} %get-tuple-element.51), channel_id=1, source_target_pairs={{4,8},{5,9},{6,10},{7,11},{12,16},{13,17},{14,18},{15,19},{20,24},... | collective-permute-start | bytes 73736 | tf_op jit(solution)/shard_map/ppermute | solution.py:510
  34.3 0.7 %copy-start.11 = (f32[40]{0:T(128)S(1)}, f32[40]{0:T(128)}, u32[]{:S(2)}) copy-start(f32[40]{0:T(128)} %profile.1) | copy-start | bytes 484

commit v4 on v3

--- a/solution.py
+++ b/solution.py
@@ -79,7 +79,7 @@
 
 def prepare(
     place_ref, slots, thick, tracer_hbm, bottom_hbm, index_hbm, weight_hbm, ssh_hbm, velocity_hbm,
-    near, side, far, odd, odd_side, mine, tracer, bottom, index, weight, ssh, velocity, sems,
+    near, side, far, odd, odd_side, tracer, bottom, index, weight, ssh, velocity, sems,
     *, count, send,
 ):
     sources = (bottom_hbm, tracer_hbm, index_hbm, weight_hbm, ssh_hbm, velocity_hbm)
@@ -96,13 +96,6 @@
     edges = index.shape[0]
     rows = lax.broadcasted_iota(jnp.int32, (SUBS, LANES), 0)
     place = place_ref[0]
-    thicks = [column(thick, k) for k in range(tiles)]
-    sent = jnp.zeros((SUBS, LANES), jnp.float32)
-    for g in range(4):
-        for slot in range(send):
-            sent = jnp.where(rows == g * send + slot, slots[0, slot, g].astype(jnp.float32), sent)
-    team = (2 * edges + 3) * SUBS
-    mine[team : team + SUBS, :] = sent
     copies[0].wait()
     copies[1].wait()
     for way, out in enumerate((near, odd, side, odd_side)):
@@ -121,6 +114,30 @@
                 value = tracer[k * SUBS : (k + 1) * SUBS, pl.ds(at, LANES)]
                 row = start + slot * levels + k * SUBS
                 out[row : row + SUBS, :] = jnp.where(rows + k * SUBS < depth, value, ABSENT)
+    for copy in copies[2:]:
+        copy.wait()
+    own_tables(place, slots, thick, tracer, bottom, index, weight, ssh, velocity, far, count, send)
+    for k in range(far.shape[0] // SUBS):
+        at = slice(k * SUBS, (k + 1) * SUBS)
+        near[at, :] = far[at, :]
+        side[at, :] = far[at, :]
+
+
+def own_tables(
+    place, slots, thick, tracer, bottom, index, weight, ssh, velocity, mine, count, send
+):
+    levels, cells = tracer.shape
+    tiles = levels // SUBS
+    blocks = cells // LANES
+    edges = index.shape[0]
+    rows = lax.broadcasted_iota(jnp.int32, (SUBS, LANES), 0)
+    thicks = [column(thick, k) for k in range(tiles)]
+    sent = jnp.zeros((SUBS, LANES), jnp.float32)
+    for g in range(4):
+        for slot in range(send):
+            sent = jnp.where(rows == g * send + slot, slots[0, slot, g].astype(jnp.float32), sent)
+    team = (2 * edges + 3) * SUBS
+    mine[team : team + SUBS, :] = sent
     for b in range(blocks):
         top = jnp.zeros((SUBS, LANES), jnp.float32)
         low = jnp.zeros((SUBS, LANES), jnp.float32)
@@ -133,25 +150,19 @@
         mine[row : row + 1, :] = jnp.sum(top, axis=0, keepdims=True) / jnp.sum(
             low, axis=0, keepdims=True
         )
-    for copy in copies[2:]:
-        copy.wait()
     for b in range(blocks):
         lanes = slice(b * LANES, (b + 1) * LANES)
         for j in range(edges):
             row = j * SUBS + b
-            found = index[j : j + 1, lanes]
-            mine[row : row + 1, :] = bounded(found, place, count, cells, send).astype(jnp.float32)
+            mine[row : row + 1, :] = index[j : j + 1, lanes].astype(jnp.float32)
             row = (edges + j) * SUBS + b
             mine[row : row + 1, :] = weight[j : j + 1, lanes]
+    for j in range(edges):
+        at = slice(j * SUBS, (j + 1) * SUBS)
+        mine[at, :] = bounded(mine[at, :], place, count, cells, send)
     row = (2 * edges + 1) * SUBS
     mine[row : row + SUBS, :] = velocity[...]
     mine[row + SUBS : row + 2 * SUBS, :] = ssh[...]
-    for k in range(mine.shape[0] // SUBS):
-        at = slice(k * SUBS, (k + 1) * SUBS)
-        value = mine[at, :]
-        near[at, :] = value
-        side[at, :] = value
-        far[at, :] = value
 
 
 def bounded(index, place, count, cells, send):
@@ -161,8 +172,9 @@
         source = place - offset
         inside = jnp.logical_and(source >= 0, source < count)
         low = jnp.where(inside, cells + 4 * span, cells + g * span)
+        low = low.astype(index.dtype)
         mine = jnp.logical_and(index >= low, index < cells + (g + 1) * span)
-        result = jnp.where(mine, cells + 4 * span, result)
+        result = jnp.where(mine, jnp.asarray(cells + 4 * span, index.dtype), result)
     return result
 
 
@@ -255,7 +267,7 @@
 
 def double_step(
     place, index, weight, force, slots, height_in, speed_in, total_in, even_in, odd_in, first_even,
-    first_odd, height, speed, total, ext, virtual, outer, *, send,
+    first_odd, height, speed, total, ext, virtual, only, *, send,
 ):
     edges = index.shape[1]
     even = (place // TEAM) % 2 == 0
@@ -328,6 +340,22 @@
             laplace, side_of(6 + 2 * edges, True, right), edge[number], side_of(5, False, right)
         )[0]
     fill(later, edge[0], edge[1])
+    if only is not None:
+        for q in range(TEAM):
+            height[q] = later[q]
+            speed[q] = faster[q]
+        q = only
+        laplace = gathered(
+            lambda r: jnp.broadcast_to(ext[q, r : r + 1, :], (SUBS, LANES)),
+            [index[q, j] for j in range(edges)],
+            [weight[q, j] for j in range(edges)],
+            height[q],
+            2 * SUBS,
+        )
+        before = total_in[q] + speed[q]
+        height[q], speed[q] = stepped(laplace, force[q], height[q], speed[q])
+        total[q] = before + speed[q]
+        return None
     last, fastest = advance_team(later, faster)
     for q in range(TEAM):
         height[q] = last[q]
@@ -360,67 +388,85 @@
 
 
 def last_pair(
-    place, profile, index, weight, force, slots, height_in, speed_in, total_in, even_in, odd_in,
-    first_even, first_odd, bottom, base, new_height, new_speed, out, height, speed, total, ext,
-    virtual, *, send,
-):
+    place_ref, index, weight, force, slots, height_in, speed_in, total_in, even_in, odd_in,
+    first_even, first_odd, bottom, base, shape, new_height, new_speed, out_hbm, out, height, speed,
+    total, ext, virtual, sems, *, send,
+):
+    position = place_ref[0] % TEAM
     double_step(
-        place[0], index, weight, force, slots, height_in, speed_in, total_in, even_in, odd_in,
-        first_even, first_odd, height, speed, total, ext, virtual, None, send=send,
-    )
-    position = place[0] % TEAM
+        place_ref[0], index, weight, force, slots, height_in, speed_in, total_in, even_in, odd_in,
+        first_even, first_odd, height, speed, total, ext, virtual, position, send=send,
+    )
     new_height[...] = height[position]
     new_speed[...] = speed[position]
     ext[0, 0:SUBS, :] = total[position] / SUBSTEPS
     rows = lax.broadcasted_iota(jnp.int32, (SUBS, LANES), 0)
+    copies = []
     for k in range(out.shape[0] // SUBS):
-        shape = column(profile, k)
+        levels = slice(k * SUBS, (k + 1) * SUBS)
         for i in range(out.shape[1] // LANES):
-            at = (slice(k * SUBS, (k + 1) * SUBS), slice(i * LANES, (i + 1) * LANES))
-            added = jnp.where(rows + k * SUBS < bottom[i : i + 1, :], shape, 0.0)
+            at = (levels, slice(i * LANES, (i + 1) * LANES))
+            added = jnp.where(rows + k * SUBS < bottom[i : i + 1, :], shape[levels, :], 0.0)
             out[at] = base[at] + added * ext[0, i : i + 1, :]
-
-
-def tracer_base(meta, tracer, bottom, index, weight, a, b, c, d, out, held, *, count, send):
+        copies.append(
+            pltpu.make_async_copy(out.at[levels, :], out_hbm.at[levels, :], sems.at[k])
+        )
+        copies[-1].start()
+    for copy in copies:
+        copy.wait()
+
+
+def collected(sources, index, weight, mine, tiles):
+    flat = [jnp.zeros((SUBS, LANES), jnp.float32) for _ in range(tiles)]
+    for near, factor in zip(index, weight):
+        near = jnp.broadcast_to(near, (SUBS, LANES))
+        lane = jnp.bitwise_and(near, LANES - 1)
+        block = jnp.right_shift(near, 7)
+        got = [jnp.full((SUBS, LANES), ABSENT, jnp.float32) for _ in range(tiles)]
+        for r, source in sources:
+            here = block == r
+            for k in range(tiles):
+                found = jnp.take_along_axis(source(k), lane, axis=1)
+                got[k] = jnp.where(here, found, got[k])
+        for k in range(tiles):
+            flat[k] = flat[k] + factor * jnp.where(got[k] < PRESENT, got[k] - mine[k], 0.0)
+    return flat
+
+
+def tracer_own(
+    place_ref, slots, thick, profile, tracer, bottom, index, weight, ssh, velocity, out, shape, mine_out,
+    held, *, count, send,
+):
+    own_tables(
+        place_ref[0], slots, thick, tracer, bottom, index, weight, ssh, velocity, mine_out, count, send
+    )
     levels, cells = tracer.shape
     tiles = levels // SUBS
     blocks = cells // LANES
     edges = index.shape[0]
-    arrived = (a, b, c, d)
-    rows = lax.broadcasted_iota(jnp.int32, (SUBS, LANES), 0)
-    place = meta[0]
+    rows = lax.broadcasted_iota(jnp.int32, (SUBS, LANES), 0)
     for i in range(blocks):
         depth = bottom[i : i + 1, :]
         for k in range(tiles):
             at = (slice(k * SUBS, (k + 1) * SUBS), slice(i * LANES, (i + 1) * LANES))
             held[at] = jnp.where(rows + k * SUBS < depth, tracer[at], ABSENT)
+    for k in range(tiles):
+        shape[k * SUBS : (k + 1) * SUBS, :] = column(profile, k)
+
+    def source(r):
+        return lambda k: held[k * SUBS : (k + 1) * SUBS, r * LANES : (r + 1) * LANES]
 
     def cell_block(i, carry):
-        at = pl.multiple_of(i * LANES, LANES)
-        lanes = pl.ds(at, LANES)
+        lanes = pl.ds(pl.multiple_of(i * LANES, LANES), LANES)
         depth = bottom[pl.ds(i, 1), :]
         mine = [tracer[k * SUBS : (k + 1) * SUBS, lanes] for k in range(tiles)]
-        flat = [jnp.zeros((SUBS, LANES), jnp.float32) for _ in range(tiles)]
-        for j in range(edges):
-            near = localize(index[j : j + 1, lanes], place, count, cells, send)
-            near = jnp.broadcast_to(near, (SUBS, LANES))
-            lane = jnp.bitwise_and(near, LANES - 1)
-            block = jnp.right_shift(near, 7)
-            factor = weight[j : j + 1, lanes]
-            got = [jnp.full((SUBS, LANES), ABSENT, jnp.float32) for _ in range(tiles)]
-            for r in range(blocks + 4 * send):
-                here = block == r
-                for k in range(tiles):
-                    if r < blocks:
-                        source = held[k * SUBS : (k + 1) * SUBS, r * LANES : (r + 1) * LANES]
-                    else:
-                        ref = arrived[(r - blocks) // send]
-                        start = ref.shape[0] - send * levels
-                        row = start + (r - blocks) % send * levels + k * SUBS
-                        source = ref[row : row + SUBS, :]
-                    got[k] = jnp.where(here, jnp.take_along_axis(source, lane, axis=1), got[k])
-            for k in range(tiles):
-                flat[k] = flat[k] + factor * jnp.where(got[k] < PRESENT, got[k] - mine[k], 0.0)
+        flat = collected(
+            [(r, source(r)) for r in range(blocks)],
+            [index[j : j + 1, lanes] for j in range(edges)],
+            [weight[j : j + 1, lanes] for j in range(edges)],
+            mine,
+            tiles,
+        )
         for k in range(tiles):
             first = rows + k * SUBS
             value = mine[k]
@@ -441,6 +487,43 @@
     lax.fori_loop(0, blocks, cell_block, 0)
 
 
+def tracer_halo(place_ref, tracer, bottom, index, weight, part, a, b, c, d, out, *, count, send):
+    levels, cells = tracer.shape
+    tiles = levels // SUBS
+    blocks = cells // LANES
+    edges = index.shape[0]
+    arrived = (a, b, c, d)
+    rows = lax.broadcasted_iota(jnp.int32, (SUBS, LANES), 0)
+    place = place_ref[0]
+
+    def source(r):
+        ref = arrived[r // send]
+        start = ref.shape[0] - send * levels + r % send * levels
+        return lambda k: ref[start + k * SUBS : start + (k + 1) * SUBS, :]
+
+    def cell_block(i, carry):
+        lanes = pl.ds(pl.multiple_of(i * LANES, LANES), LANES)
+        depth = bottom[pl.ds(i, 1), :]
+        mine = [tracer[k * SUBS : (k + 1) * SUBS, lanes] for k in range(tiles)]
+        flat = collected(
+            [(blocks + r, source(r)) for r in range(4 * send)],
+            [
+                localize(index[j : j + 1, lanes], place, count, cells, send)
+                for j in range(edges)
+            ],
+            [weight[j : j + 1, lanes] for j in range(edges)],
+            mine,
+            tiles,
+        )
+        for k in range(tiles):
+            at = (slice(k * SUBS, (k + 1) * SUBS), lanes)
+            added = jnp.where(rows + k * SUBS < depth, horizontal_rate * flat[k], 0.0)
+            out[at] = part[at] + tracer_step * added
+        return carry
+
+    lax.fori_loop(0, blocks, cell_block, 0)
+
+
 def shards(
     tracer, bottom_levels, neighbours, edge_weight, ssh, velocity, send_blocks, thickness, profile
 ):
@@ -472,7 +555,7 @@
 
     own = (2 * edges + 4) * SUBS
     halo = send * levels
-    near, side, far, odd, odd_side, mine = call(
+    near, side, far, odd, odd_side = call(
         functools.partial(prepare, count=count),
         "prepare",
         [
@@ -481,7 +564,6 @@
             shape((own, LANES)),
             shape((halo, LANES)),
             shape((halo, LANES)),
-            shape((own, LANES)),
         ],
         [SMEM, SMEM, SMEM] + [HBM] * 6,
         [
@@ -494,9 +576,21 @@
             pltpu.SemaphoreType.DMA((6,)),
         ],
         4000000,
+        60,
     )(
         place, slots, thickness, tracer, bottom, neighbours, edge_weight, ssh.reshape(tile),
         velocity.reshape(tile),
+    )
+    part, columns, mine = call(
+        functools.partial(tracer_own, count=count),
+        "tracer_own",
+        [shape(tracer.shape), shape((levels, LANES)), shape((own, LANES))],
+        [SMEM] * 4 + [VMEM] * 6,
+        [pltpu.VMEM(tracer.shape, jnp.float32)],
+        10000000,
+    )(
+        place, slots, thickness, profile, tracer, bottom, neighbours, edge_weight,
+        ssh.reshape(tile), velocity.reshape(tile),
     )
     side = lax.ppermute(side, "dom", even_swap(count, 2))
     far = lax.ppermute(far, "dom", even_swap(count, 3))
@@ -529,13 +623,13 @@
     )(place, mine, near, side, far)
     constant = swap((way_even, way_odd))
     base = call(
-        functools.partial(tracer_base, count=count),
-        "tracer_base",
+        functools.partial(tracer_halo, count=count),
+        "tracer_halo",
         shape(tracer.shape),
-        [SMEM] + [VMEM] * 8,
-        [pltpu.VMEM(tracer.shape, jnp.float32)],
-        20000000,
-    )(place, tracer, bottom, neighbours, edge_weight, near, odd, side, odd_side)
+        [SMEM] + [VMEM] * 9,
+        [],
+        10000000,
+    )(place, tracer, bottom, neighbours, edge_weight, part, near, odd, side, odd_side)
     scratch = [pltpu.VMEM((TEAM, 2 * SUBS, LANES), jnp.float32)] * 2
     light = [shape((6 * SUBS, LANES))] * 2
     height, speed, total, *ways = call(
@@ -547,14 +641,19 @@
     )(place, *tables, height, speed, total, *arrived, *constant)
     arrived = swap(ways)
     team_scratch = [pltpu.VMEM((TEAM,) + tile, jnp.float32)] * 3
-    height, speed, result = call(
-        last_pair,
-        "last_pair",
-        [shape(tile), shape(tile), shape(tracer.shape)],
-        [SMEM, SMEM] + [VMEM] * 13,
-        team_scratch + scratch,
-        2500000,
-    )(place, profile, *tables, height, speed, total, *arrived, *constant, bottom, base)
+    height, speed, result = pl.pallas_call(
+        functools.partial(last_pair, send=send),
+        out_shape=[shape(tile), shape(tile), shape(tracer.shape)],
+        in_specs=[SMEM] + [VMEM] * 14,
+        out_specs=[VMEM, VMEM, HBM],
+        scratch_shapes=[pltpu.VMEM(tracer.shape, jnp.float32)]
+        + team_scratch
+        + scratch
+        + [pltpu.SemaphoreType.DMA((levels // SUBS,))],
+        compiler_params=pltpu.CompilerParams(vmem_limit_bytes=4 << 20),
+        cost_estimate=pl.CostEstimate(flops=2500000, bytes_accessed=1000, transcendentals=0),
+        name="last_pair",
+    )(place, *tables, height, speed, total, *arrived, *constant, bottom, base, columns)
     return (result, height.reshape(-1), speed.reshape(-1))
 
 

time: 37.9 us -> 33.6 us (0.89)
  local copies, waits for them, and re-layouts: 3.8 us -> 0.05 us
  waiting for transfers between devices: 8.55 us -> 5.19 us
  Pallas kernels: 11.4 us -> 14.1 us
    unnamed x24 -> x22, local copies, waits for them, and re-layouts: 3.8 us -> 0.05 us
    ppermute x1, waiting for transfers between devices: 4.39 us -> 1.03 us  [shards(): far = lax.ppermute(far, 'dom', even_swap(count, 3))]
    pallas_call x1, Pallas kernels: 1.14 us -> 2.63 us  [shards(): call(functools.partial(prepare, count=count), 'prepare', [shape((own + ha...]
    pallas_call x2 -> x3, Pallas kernels: 7.63 us -> 8.77 us  [the longest x1 3.48 us: shards(): call(functools.partial(tracer_own, count=count), 'tracer_own', [shape(tra...]
  transfers between devices with their start and end apart: 11 -> 11, of which waited for: 3 -> 3; matrix products, arithmetic and copies ran while one was open for 0% -> 0% of each run, Pallas kernels for 17% -> 23%
where the time goes in v4:
time: 33.6 us; the launch traced here: 33 us
  Pallas kernels  14.1 us (42%)
  starting transfers between devices  12.9 us (38%)
  waiting for transfers between devices  5.19 us (15%)
  between operations  0.81 us (2%)
    ppermute x3, starting transfers between devices, swap(): lax.ppermute(pair[0], 'dom', even_swap(count, TEAM))  3.62 us
    pallas_call x1, Pallas kernels, shards(): call(functools.partial(tracer_own, count=count), 'tracer_own', [shape(tra...  3.48 us
    ppermute x1, starting transfers between devices, shards(): odd = lax.ppermute(odd, 'dom', odd_swap(count, 1))  3.34 us
    pallas_call x1, Pallas kernels, shards(): call(functools.partial(tracer_halo, count=count), 'tracer_halo', shape(tr...  2.95 us
    pallas_call x1, Pallas kernels, shards(): call(functools.partial(prepare, count=count), 'prepare', [shape((own + ha...  2.63 us
    ppermute x3, waiting for transfers between devices, swap(): lax.ppermute(pair[0], 'dom', even_swap(count, TEAM))  2.55 us
    pallas_call x1, Pallas kernels, shards(): pl.pallas_call(functools.partial(last_pair, send=send), out_shape=[shape(...  2.34 us
    ppermute x1, starting transfers between devices, shards(): odd_side = lax.ppermute(odd_side, 'dom', odd_swap(count, 2))  2.05 us
  transfers between devices with their start and end apart: 11, of which 3 were waited for; matrix products, arithmetic and copies ran while one was open for 0% of the time, Pallas kernels for 23%

profile of v4, /device:TPU:9, one launch (start us, length us, event | category | flops | bytes accessed | tf_op | source)
XLA Modules:
  0.0 33.0 jit_solution(11981629544446789805)
XLA Ops:
  0.6 0.0 copy-start
  0.6 0.0 copy-start.1
  0.7 0.0 copy-start.2
  0.7 0.0 copy-start.4
  0.7 0.0 copy-start.5
  0.7 0.0 copy-start.8
  0.7 2.6 %prepare.1 = (f32[208,128]{1,0:T(8,128)}, f32[208,128]{1,0:T(8,128)}, f32[128,128]{1,0:T(8,128)}, f32[80,128]{1,0:T(8,128)}, f32[80,128]{1,0:T(8,128)}) custom-call(s32[1]{0:T(128)} %bitcast.place_ref.place, s32[1,2,4]{2,1,0:T(2,128)} %bitcast.15, f32[40]{0:T(128)} %thick.3, f32[40,1024]{1,0:T(8,128)} %tracer.3, s32[8,128]{1,0:T(8,128)} %bitcast.7, ...), custom_call_target="tpu_custom_call" | custom-call | flops 4000000 | bytes 1000 | tf_op jit(solution)/shard_map/prepare/pallas_call | solution.py:558
  3.3 0.0 copy-start.3
  3.4 0.7 %collective-permute-start = (f32[208,128]{1,0:T(8,128)}, f32[208,128]{1,0:T(8,128)S(1)}, u32[]{:S(2)}, u32[]{:S(2)}) collective-permute-start(f32[208,128]{1,0:T(8,128)} %get-tuple-element.33), channel_id=1, source_target_pairs={{0,1},{1,0},{2,3},{3,2},{4,5},{5,4},{6,7},{7,6},{8,9},{9,8},{10,11... | collective-permute-start | bytes 319496 | tf_op jit(solution)/shard_map/ppermute | solution.py:597
  4.1 0.0 copy-start.6
  4.1 0.0 copy-start.7
  4.1 1.2 %collective-permute-start.1 = (f32[208,128]{1,0:T(8,128)}, f32[208,128]{1,0:T(8,128)S(1)}, u32[]{:S(2)}, u32[]{:S(2)}) collective-permute-start(f32[208,128]{1,0:T(8,128)} %get-tuple-element.34), channel_id=1, source_target_pairs={{0,2},{1,3},{2,0},{3,1},{4,6},{5,7},{6,4},{7,5},{8,10},{9,11},{10,... | collective-permute-start | bytes 319496 | tf_op jit(solution)/shard_map/ppermute | solution.py:595
  5.3 0.5 %collective-permute-start.2 = (f32[128,128]{1,0:T(8,128)}, f32[128,128]{1,0:T(8,128)S(1)}, u32[]{:S(2)}, u32[]{:S(2)}) collective-permute-start(f32[128,128]{1,0:T(8,128)} %get-tuple-element.35), channel_id=1, source_target_pairs={{0,3},{1,2},{2,1},{3,0},{4,7},{5,6},{6,5},{7,4},{8,11},{9,10},{10,... | collective-permute-start | bytes 196616 | tf_op jit(solution)/shard_map/ppermute | solution.py:596
  5.8 0.0 copy-done
  5.8 0.0 copy-done.1
  5.8 0.0 copy-done.2
  5.8 0.0 copy-done.4
  5.8 0.0 copy-done.5
  5.8 0.0 copy-done.8
  5.9 0.0 copy-done.3
  5.9 0.0 copy-done.6
  5.9 0.0 copy-done.7
  5.9 3.5 %tracer_own.1 = (f32[40,1024]{1,0:T(8,128)S(1)}, f32[40,128]{1,0:T(8,128)S(1)}, f32[128,128]{1,0:T(8,128)S(1)}) custom-call(s32[1]{0:T(128)} %bitcast.place_ref.place, s32[1,2,4]{2,1,0:T(2,128)S(1)} %bitcast.16, f32[40]{0:T(128)S(1)} %copy-done.7, f32[40]{0:T(128)S(1)} %copy-done.8, f32[40,1024]{1,0:T(8,128)S(1)} %copy-done, s32[8,128]{1,0:T(8,128)S(1)} %bitcast.8, ...), custom_call_target="tpu_custom_call" | custom-call | flops 10000000 | bytes 1000 | tf_op jit(solution)/shard_map/tracer_own/pallas_call | solution.py:584
  9.4 1.0 %collective-permute-done.2.far = f32[128,128]{1,0:T(8,128)S(1)} collective-permute-done((f32[128,128]{1,0:T(8,128)}, f32[128,128]{1,0:T(8,128)S(1)}, u32[]{:S(2)}, u32[]{:S(2)}) %collective-permute-start.2) | collective-permute-done | bytes 65568 | tf_op jit(solution)/shard_map/ppermute | solution.py:596
  10.4 0.0 collective-permute-done.near.a
  10.4 0.0 collective-permute-done.1.side.c
  10.4 0.1 gather_team.1
  10.5 1.3 %collective-permute-start.3 = (f32[152,128]{1,0:T(8,128)S(1)}, f32[152,128]{1,0:T(8,128)S(1)}, u32[]{:S(2)}, u32[]{:S(2)}) collective-permute-start(f32[152,128]{1,0:T(8,128)S(1)} %get-tuple-element.42), channel_id=1, source_target_pairs={{0,4},{1,5},{2,6},{3,7},{4,0},{5,1},{6,2},{7,3},{8,12},{9,13},{10,... | collective-permute-start | bytes 233480 | tf_op jit(solution)/shard_map/ppermute | solution.py:603
  11.8 0.0 collective-permute-start.4
  11.8 2.5 %collective-permute-done.3.even_in.first_even = f32[152,128]{1,0:T(8,128)S(1)} collective-permute-done((f32[152,128]{1,0:T(8,128)S(1)}, f32[152,128]{1,0:T(8,128)S(1)}, u32[]{:S(2)}, u32[]{:S(2)}) %collective-permute-start.3) | collective-permute-done | bytes 77856 | tf_op jit(solution)/shard_map/ppermute | solution.py:603
  14.3 1.6 %collective-permute-done.4.odd_in.first_odd = f32[152,128]{1,0:T(8,128)S(1)} collective-permute-done((f32[152,128]{1,0:T(8,128)S(1)}, f32[152,128]{1,0:T(8,128)S(1)}, u32[]{:S(2)}, u32[]{:S(2)}) %collective-permute-start.4) | collective-permute-done | bytes 77856 | tf_op jit(solution)/shard_map/ppermute | solution.py:604
  15.9 0.0 copy-start.10
  15.9 0.0 copy-start.9
  15.9 1.3 %first_pair.1 = (f32[4,8,128]{2,1,0:T(8,128)S(1)}, f32[4,8,128]{2,1,0:T(8,128)S(1)}, f32[4,8,128]{2,1,0:T(8,128)S(1)}, f32[48,128]{1,0:T(8,128)S(1)}, f32[48,128]{1,0:T(8,128)S(1)}) custom-call(s32[1]{0:T(128)} %bitcast.place_ref.place, s32[4,6,8,128]{3,2,1,0:T(8,128)S(1)} %get-tuple-element.36.index, f32[4,6,8,128]{3,2,1,0:T(8,128)S(1)} %get-tuple-element.37.weight, ...), custom_call_target="tpu_custom_call" | custom-call | flops 2000000 | bytes 1000 | tf_op jit(solution)/shard_map/first_pair/pallas_call | solution.py:635
  17.2 0.4 %collective-permute-start.5 = (f32[48,128]{1,0:T(8,128)S(1)}, f32[48,128]{1,0:T(8,128)S(1)}, u32[]{:S(2)}, u32[]{:S(2)}) collective-permute-start(f32[48,128]{1,0:T(8,128)S(1)} %get-tuple-element.47), channel_id=1, source_target_pairs={{0,4},{1,5},{2,6},{3,7},{4,0},{5,1},{6,2},{7,3},{8,12},{9,13},{10,... | collective-permute-start | bytes 73736 | tf_op jit(solution)/shard_map/ppermute | solution.py:603
  17.6 0.0 collective-permute-start.6
  17.6 0.0 copy-done.10
  17.6 3.3 %collective-permute-start.9 = (f32[80,128]{1,0:T(8,128)S(1)}, f32[80,128]{1,0:T(8,128)S(1)}, u32[]{:S(2)}, u32[]{:S(2)}) collective-permute-start(f32[80,128]{1,0:T(8,128)S(1)} %copy-done.10), channel_id=1, source_target_pairs={{1,2},{3,4},{5,6},{7,8},{9,10},{11,12},{13,14},{15,16},{17,18},{19... | collective-permute-start | bytes 122888 | tf_op jit(solution)/shard_map/ppermute | solution.py:598
  21.0 0.0 copy-done.9
  21.0 2.1 %collective-permute-start.10 = (f32[80,128]{1,0:T(8,128)S(1)}, f32[80,128]{1,0:T(8,128)S(1)}, u32[]{:S(2)}, u32[]{:S(2)}) collective-permute-start(f32[80,128]{1,0:T(8,128)S(1)} %copy-done.9), channel_id=1, source_target_pairs={{2,4},{3,5},{6,8},{7,9},{10,12},{11,13},{14,16},{15,17},{18,20},{1... | collective-permute-start | bytes 122888 | tf_op jit(solution)/shard_map/ppermute | solution.py:599
  23.0 0.0 collective-permute-done.5.even_in
  23.0 0.0 collective-permute-done.6.odd_in
  23.1 1.3 %middle_pair.1 = (f32[4,8,128]{2,1,0:T(8,128)S(1)}, f32[4,8,128]{2,1,0:T(8,128)S(1)}, f32[4,8,128]{2,1,0:T(8,128)S(1)}, f32[48,128]{1,0:T(8,128)S(1)}, f32[48,128]{1,0:T(8,128)S(1)}) custom-call(s32[1]{0:T(128)} %bitcast.place_ref.place, s32[4,6,8,128]{3,2,1,0:T(8,128)S(1)} %get-tuple-element.36.index, f32[4,6,8,128]{3,2,1,0:T(8,128)S(1)} %get-tuple-element.37.weight, ...), custom_call_target="tpu_custom_call" | custom-call | flops 2000000 | bytes 1000 | tf_op jit(solution)/shard_map/middle_pair/pallas_call | solution.py:639
  24.4 1.9 %collective-permute-start.7 = (f32[48,128]{1,0:T(8,128)S(1)}, f32[48,128]{1,0:T(8,128)S(1)}, u32[]{:S(2)}, u32[]{:S(2)}) collective-permute-start(f32[48,128]{1,0:T(8,128)S(1)} %get-tuple-element.52), channel_id=1, source_target_pairs={{0,4},{1,5},{2,6},{3,7},{4,0},{5,1},{6,2},{7,3},{8,12},{9,13},{10,... | collective-permute-start | bytes 73736 | tf_op jit(solution)/shard_map/ppermute | solution.py:603
  26.3 1.4 %collective-permute-start.8 = (f32[48,128]{1,0:T(8,128)S(1)}, f32[48,128]{1,0:T(8,128)S(1)}, u32[]{:S(2)}, u32[]{:S(2)}) collective-permute-start(f32[48,128]{1,0:T(8,128)S(1)} %get-tuple-element.53), channel_id=1, source_target_pairs={{4,8},{5,9},{6,10},{7,11},{12,16},{13,17},{14,18},{15,19},{20,24},... | collective-permute-start | bytes 73736 | tf_op jit(solution)/shard_map/ppermute | solution.py:604
  27.7 0.0 collective-permute-done.9.b
  27.7 0.0 collective-permute-done.10.d
  27.7 2.9 %tracer_halo.1.base = f32[40,1024]{1,0:T(8,128)S(1)} custom-call(s32[1]{0:T(128)} %bitcast.place_ref.place, f32[40,1024]{1,0:T(8,128)S(1)} %copy-done, s32[8,128]{1,0:T(8,128)S(1)} %bitcast.9, s32[6,1024]{1,0:T(8,128)S(1)} %copy-done.1, f32[6,1024]{1,0:T(8,128)S(1)} %copy-done.2, f32[40,1024]{1,0:T(8,128)S(1)} %get-tuple-element.54.part, ...), custom_call_target="tpu_custom_call" | custom-call | flops 10000000 | bytes 1000 | tf_op jit(solution)/shard_map/tracer_halo/pallas_call | solution.py:625
  30.7 0.0 collective-permute-done.7.even_in
  30.7 0.0 collective-permute-done.8.odd_in
  30.7 2.3 %last_pair.1 = (f32[8,128]{1,0:T(8,128)}, f32[8,128]{1,0:T(8,128)}, f32[40,1024]{1,0:T(8,128)}) custom-call(s32[1]{0:T(128)} %bitcast.place_ref.place, s32[4,6,8,128]{3,2,1,0:T(8,128)S(1)} %get-tuple-element.36.index, f32[4,6,8,128]{3,2,1,0:T(8,128)S(1)} %get-tuple-element.37.weight, f32[4,8,128]{2,1,0:T(8,128)S(1)} %get-tuple-element.38.force, ...), custom_call_target="tpu_custom_call" | custom-call | flops 2500000 | bytes 1000 | tf_op jit(solution)/shard_map/last_pair/pallas_call | solution.py:644
Async XLA Ops:
  0.6 5.2 %copy-start = (f32[40,1024]{1,0:T(8,128)S(1)}, f32[40,1024]{1,0:T(8,128)}, u32[]{:S(2)}) copy-start(f32[40,1024]{1,0:T(8,128)} %tracer.3) | copy-start | bytes 491524
  0.6 5.2 %copy-start.1 = (s32[6,1024]{1,0:T(8,128)S(1)}, s32[6,1024]{1,0:T(8,128)}, u32[]{:S(2)}) copy-start(s32[6,1024]{1,0:T(8,128)} %index.3) | copy-start | bytes 73732
  0.7 5.2 %copy-start.2 = (f32[6,1024]{1,0:T(8,128)S(1)}, f32[6,1024]{1,0:T(8,128)}, u32[]{:S(2)}) copy-start(f32[6,1024]{1,0:T(8,128)} %weight.3) | copy-start | bytes 73732
  0.7 5.2 %copy-start.4 = (f32[1024]{0:T(1024)S(1)}, f32[1024]{0:T(1024)}, u32[]{:S(2)}) copy-start(f32[1024]{0:T(1024)} %param.13) | copy-start | bytes 12292
  0.7 5.2 %copy-start.5 = (f32[1024]{0:T(1024)S(1)}, f32[1024]{0:T(1024)}, u32[]{:S(2)}) copy-start(f32[1024]{0:T(1024)} %param.14) | copy-start | bytes 12292
  0.7 5.2 %copy-start.8 = (f32[40]{0:T(128)S(1)}, f32[40]{0:T(128)}, u32[]{:S(2)}) copy-start(f32[40]{0:T(128)} %profile.1) | copy-start | bytes 484
  3.3 2.5 %copy-start.3 = (s32[1024]{0:T(1024)S(1)}, s32[1024]{0:T(1024)}, u32[]{:S(2)}) copy-start(s32[1024]{0:T(1024)} %param.10) | copy-start | bytes 12292
  3.4 7.1 %collective-permute-start = (f32[208,128]{1,0:T(8,128)}, f32[208,128]{1,0:T(8,128)S(1)}, u32[]{:S(2)}, u32[]{:S(2)}) collective-permute-start(f32[208,128]{1,0:T(8,128)} %get-tuple-element.33), channel_id=1, source_target_pairs={{0,1},{1,0},{2,3},{3,2},{4,5},{5,4},{6,7},{7,6},{8,9},{9,8},{10,11... | collective-permute-start | bytes 319496 | tf_op jit(solution)/shard_map/ppermute | solution.py:597
  4.1 1.8 %copy-start.6 = (s32[1,4,2]{1,2,0:T(2,128)S(1)}, s32[1,4,2]{1,2,0:T(2,128)}, u32[]{:S(2)}) copy-start(s32[1,4,2]{1,2,0:T(2,128)} %param.15) | copy-start | bytes 100
  4.1 1.8 %copy-start.7 = (f32[40]{0:T(128)S(1)}, f32[40]{0:T(128)}, u32[]{:S(2)}) copy-start(f32[40]{0:T(128)} %thick.3) | copy-start | bytes 484
  4.1 6.3 %collective-permute-start.1 = (f32[208,128]{1,0:T(8,128)}, f32[208,128]{1,0:T(8,128)S(1)}, u32[]{:S(2)}, u32[]{:S(2)}) collective-permute-start(f32[208,128]{1,0:T(8,128)} %get-tuple-element.34), channel_id=1, source_target_pairs={{0,2},{1,3},{2,0},{3,1},{4,6},{5,7},{6,4},{7,5},{8,10},{9,11},{10,... | collective-permute-start | bytes 319496 | tf_op jit(solution)/shard_map/ppermute | solution.py:595
  5.3 5.1 %collective-permute-start.2 = (f32[128,128]{1,0:T(8,128)}, f32[128,128]{1,0:T(8,128)S(1)}, u32[]{:S(2)}, u32[]{:S(2)}) collective-permute-start(f32[128,128]{1,0:T(8,128)} %get-tuple-element.35), channel_id=1, source_target_pairs={{0,3},{1,2},{2,1},{3,0},{4,7},{5,6},{6,5},{7,4},{8,11},{9,10},{10,... | collective-permute-start | bytes 196616 | tf_op jit(solution)/shard_map/ppermute | solution.py:596
  10.5 3.8 %collective-permute-start.3 = (f32[152,128]{1,0:T(8,128)S(1)}, f32[152,128]{1,0:T(8,128)S(1)}, u32[]{:S(2)}, u32[]{:S(2)}) collective-permute-start(f32[152,128]{1,0:T(8,128)S(1)} %get-tuple-element.42), channel_id=1, source_target_pairs={{0,4},{1,5},{2,6},{3,7},{4,0},{5,1},{6,2},{7,3},{8,12},{9,13},{10,... | collective-permute-start | bytes 233480 | tf_op jit(solution)/shard_map/ppermute | solution.py:603
  11.8 4.1 %collective-permute-start.4 = (f32[152,128]{1,0:T(8,128)S(1)}, f32[152,128]{1,0:T(8,128)S(1)}, u32[]{:S(2)}, u32[]{:S(2)}) collective-permute-start(f32[152,128]{1,0:T(8,128)S(1)} %get-tuple-element.43), channel_id=1, source_target_pairs={{4,8},{5,9},{6,10},{7,11},{12,16},{13,17},{14,18},{15,19},{20,24},... | collective-permute-start | bytes 233480 | tf_op jit(solution)/shard_map/ppermute | solution.py:604
  15.9 1.7 %copy-start.10 = (f32[80,128]{1,0:T(8,128)S(1)}, f32[80,128]{1,0:T(8,128)}, u32[]{:S(2)}) copy-start(f32[80,128]{1,0:T(8,128)} %get-tuple-element.55) | copy-start | bytes 122884
  15.9 5.0 %copy-start.9 = (f32[80,128]{1,0:T(8,128)S(1)}, f32[80,128]{1,0:T(8,128)}, u32[]{:S(2)}) copy-start(f32[80,128]{1,0:T(8,128)} %get-tuple-element.56) | copy-start | bytes 122884
  17.2 5.8 %collective-permute-start.5 = (f32[48,128]{1,0:T(8,128)S(1)}, f32[48,128]{1,0:T(8,128)S(1)}, u32[]{:S(2)}, u32[]{:S(2)}) collective-permute-start(f32[48,128]{1,0:T(8,128)S(1)} %get-tuple-element.47), channel_id=1, source_target_pairs={{0,4},{1,5},{2,6},{3,7},{4,0},{5,1},{6,2},{7,3},{8,12},{9,13},{10,... | collective-permute-start | bytes 73736 | tf_op jit(solution)/shard_map/ppermute | solution.py:603
  17.6 5.4 %collective-permute-start.6 = (f32[48,128]{1,0:T(8,128)S(1)}, f32[48,128]{1,0:T(8,128)S(1)}, u32[]{:S(2)}, u32[]{:S(2)}) collective-permute-start(f32[48,128]{1,0:T(8,128)S(1)} %get-tuple-element.48), channel_id=1, source_target_pairs={{4,8},{5,9},{6,10},{7,11},{12,16},{13,17},{14,18},{15,19},{20,24},... | collective-permute-start | bytes 73736 | tf_op jit(solution)/shard_map/ppermute | solution.py:604
  17.6 10.1 %collective-permute-start.9 = (f32[80,128]{1,0:T(8,128)S(1)}, f32[80,128]{1,0:T(8,128)S(1)}, u32[]{:S(2)}, u32[]{:S(2)}) collective-permute-start(f32[80,128]{1,0:T(8,128)S(1)} %copy-done.10), channel_id=1, source_target_pairs={{1,2},{3,4},{5,6},{7,8},{9,10},{11,12},{13,14},{15,16},{17,18},{19... | collective-permute-start | bytes 122888 | tf_op jit(solution)/shard_map/ppermute | solution.py:598
  21.0 6.7 %collective-permute-start.10 = (f32[80,128]{1,0:T(8,128)S(1)}, f32[80,128]{1,0:T(8,128)S(1)}, u32[]{:S(2)}, u32[]{:S(2)}) collective-permute-start(f32[80,128]{1,0:T(8,128)S(1)} %copy-done.9), channel_id=1, source_target_pairs={{2,4},{3,5},{6,8},{7,9},{10,12},{11,13},{14,16},{15,17},{18,20},{1... | collective-permute-start | bytes 122888 | tf_op jit(solution)/shard_map/ppermute | solution.py:599
  24.4 6.3 %collective-permute-start.7 = (f32[48,128]{1,0:T(8,128)S(1)}, f32[48,128]{1,0:T(8,128)S(1)}, u32[]{:S(2)}, u32[]{:S(2)}) collective-permute-start(f32[48,128]{1,0:T(8,128)S(1)} %get-tuple-element.52), channel_id=1, source_target_pairs={{0,4},{1,5},{2,6},{3,7},{4,0},{5,1},{6,2},{7,3},{8,12},{9,13},{10,... | collective-permute-start | bytes 73736 | tf_op jit(solution)/shard_map/ppermute | solution.py:603
  26.3 4.4 %collective-permute-start.8 = (f32[48,128]{1,0:T(8,128)S(1)}, f32[48,128]{1,0:T(8,128)S(1)}, u32[]{:S(2)}, u32[]{:S(2)}) collective-permute-start(f32[48,128]{1,0:T(8,128)S(1)} %get-tuple-element.53), channel_id=1, source_target_pairs={{4,8},{5,9},{6,10},{7,11},{12,16},{13,17},{14,18},{15,19},{20,24},... | collective-permute-start | bytes 73736 | tf_op jit(solution)/shard_map/ppermute | solution.py:604

commit v5 on v4

--- a/solution.py
+++ b/solution.py
@@ -6,6 +6,7 @@
 from jax.experimental import pallas as pl
 from jax.experimental.pallas import tpu as pltpu
 from jax.sharding import PartitionSpec as P
+
 
 LANES = 128
 SUBS = 8
@@ -19,6 +20,7 @@
 friction = 0.05
 ABSENT = 3e38
 PRESENT = 1e38
+
 
 SMEM = pl.BlockSpec(memory_space=pltpu.SMEM)
 VMEM = pl.BlockSpec(memory_space=pltpu.VMEM)
@@ -77,28 +79,11 @@
     return jnp.where(slots >= 0, taken, 0.0)
 
 
-def prepare(
-    place_ref, slots, thick, tracer_hbm, bottom_hbm, index_hbm, weight_hbm, ssh_hbm, velocity_hbm,
-    near, side, far, odd, odd_side, tracer, bottom, index, weight, ssh, velocity, sems,
-    *, count, send,
-):
-    sources = (bottom_hbm, tracer_hbm, index_hbm, weight_hbm, ssh_hbm, velocity_hbm)
-    targets = (bottom, tracer, index, weight, ssh, velocity)
-    copies = [
-        pltpu.make_async_copy(source, target, sems.at[n])
-        for n, (source, target) in enumerate(zip(sources, targets))
-    ]
-    for copy in copies:
-        copy.start()
-    levels, cells = tracer.shape
+def tracer_blocks(place, slots, tracer, bottom, outs, send):
+    levels = tracer.shape[0]
     tiles = levels // SUBS
-    blocks = cells // LANES
-    edges = index.shape[0]
-    rows = lax.broadcasted_iota(jnp.int32, (SUBS, LANES), 0)
-    place = place_ref[0]
-    copies[0].wait()
-    copies[1].wait()
-    for way, out in enumerate((near, odd, side, odd_side)):
+    rows = lax.broadcasted_iota(jnp.int32, (SUBS, LANES), 0)
+    for way, out in outs:
         offset = 1 if way < 2 else 2
         first = (place // offset) % 2 == 0
         base = 0 if way < 2 else 2
@@ -114,8 +99,14 @@
                 value = tracer[k * SUBS : (k + 1) * SUBS, pl.ds(at, LANES)]
                 row = start + slot * levels + k * SUBS
                 out[row : row + SUBS, :] = jnp.where(rows + k * SUBS < depth, value, ABSENT)
-    for copy in copies[2:]:
-        copy.wait()
+
+
+def prepare(
+    place_ref, slots, thick, tracer, bottom, index, weight, ssh, velocity, near, side, far, *,
+    count, send,
+):
+    place = place_ref[0]
+    tracer_blocks(place, slots, tracer, bottom, ((0, near), (2, side)), send)
     own_tables(place, slots, thick, tracer, bottom, index, weight, ssh, velocity, far, count, send)
     for k in range(far.shape[0] // SUBS):
         at = slice(k * SUBS, (k + 1) * SUBS)
@@ -389,7 +380,7 @@
 
 def last_pair(
     place_ref, index, weight, force, slots, height_in, speed_in, total_in, even_in, odd_in,
-    first_even, first_odd, bottom, base, shape, new_height, new_speed, out_hbm, out, height, speed,
+    first_even, first_odd, bottom, base, shape, height_hbm, speed_hbm, out_hbm, out, height, speed,
     total, ext, virtual, sems, *, send,
 ):
     position = place_ref[0] % TEAM
@@ -397,11 +388,15 @@
         place_ref[0], index, weight, force, slots, height_in, speed_in, total_in, even_in, odd_in,
         first_even, first_odd, height, speed, total, ext, virtual, position, send=send,
     )
-    new_height[...] = height[position]
-    new_speed[...] = speed[position]
     ext[0, 0:SUBS, :] = total[position] / SUBSTEPS
     rows = lax.broadcasted_iota(jnp.int32, (SUBS, LANES), 0)
-    copies = []
+    tiles = out.shape[0] // SUBS
+    copies = [
+        pltpu.make_async_copy(height.at[position], height_hbm, sems.at[tiles]),
+        pltpu.make_async_copy(speed.at[position], speed_hbm, sems.at[tiles + 1]),
+    ]
+    for copy in copies:
+        copy.start()
     for k in range(out.shape[0] // SUBS):
         levels = slice(k * SUBS, (k + 1) * SUBS)
         for i in range(out.shape[1] // LANES):
@@ -435,11 +430,15 @@
 
 def tracer_own(
     place_ref, slots, thick, profile, tracer, bottom, index, weight, ssh, velocity, out, shape, mine_out,
-    held, *, count, send,
+    odd, odd_side, local, held, *, count, send,
 ):
     own_tables(
         place_ref[0], slots, thick, tracer, bottom, index, weight, ssh, velocity, mine_out, count, send
     )
+    tracer_blocks(place_ref[0], slots, tracer, bottom, ((1, odd), (3, odd_side)), send)
+    for i in range(index.shape[1] // LANES):
+        at = slice(i * LANES, (i + 1) * LANES)
+        local[:, at] = localize(index[:, at], place_ref[0], count, index.shape[1], send)
     levels, cells = tracer.shape
     tiles = levels // SUBS
     blocks = cells // LANES
@@ -487,34 +486,30 @@
     lax.fori_loop(0, blocks, cell_block, 0)
 
 
-def tracer_halo(place_ref, tracer, bottom, index, weight, part, a, b, c, d, out, *, count, send):
+def tracer_halo(tracer, bottom, local, weight, part, a, b, out, *, send, ways):
     levels, cells = tracer.shape
     tiles = levels // SUBS
     blocks = cells // LANES
-    edges = index.shape[0]
-    arrived = (a, b, c, d)
-    rows = lax.broadcasted_iota(jnp.int32, (SUBS, LANES), 0)
-    place = place_ref[0]
-
-    def source(r):
-        ref = arrived[r // send]
-        start = ref.shape[0] - send * levels + r % send * levels
+    edges = local.shape[0]
+    rows = lax.broadcasted_iota(jnp.int32, (SUBS, LANES), 0)
+
+    def source(ref, slot):
+        start = ref.shape[0] - send * levels + slot * levels
         return lambda k: ref[start + k * SUBS : start + (k + 1) * SUBS, :]
+
+    sources = [
+        (blocks + way * send + slot, source(ref, slot))
+        for way, ref in zip(ways, (a, b))
+        for slot in range(send)
+    ]
 
     def cell_block(i, carry):
         lanes = pl.ds(pl.multiple_of(i * LANES, LANES), LANES)
         depth = bottom[pl.ds(i, 1), :]
         mine = [tracer[k * SUBS : (k + 1) * SUBS, lanes] for k in range(tiles)]
-        flat = collected(
-            [(blocks + r, source(r)) for r in range(4 * send)],
-            [
-                localize(index[j : j + 1, lanes], place, count, cells, send)
-                for j in range(edges)
-            ],
-            [weight[j : j + 1, lanes] for j in range(edges)],
-            mine,
-            tiles,
-        )
+        near = [local[j : j + 1, lanes] for j in range(edges)]
+        factors = [weight[j : j + 1, lanes] for j in range(edges)]
+        flat = collected(sources, near, factors, mine, tiles)
         for k in range(tiles):
             at = (slice(k * SUBS, (k + 1) * SUBS), lanes)
             added = jnp.where(rows + k * SUBS < depth, horizontal_rate * flat[k], 0.0)
@@ -542,7 +537,7 @@
     def shape(rows, kind=jnp.float32):
         return jax.ShapeDtypeStruct(rows, kind)
 
-    def call(body, name, outs, ins, scratch, flops, limit=4):
+    def call(body, outs, ins, scratch, flops, limit=4):
         return pl.pallas_call(
             functools.partial(body, send=send),
             out_shape=outs,
@@ -550,41 +545,35 @@
             scratch_shapes=scratch,
             compiler_params=pltpu.CompilerParams(vmem_limit_bytes=limit << 20),
             cost_estimate=pl.CostEstimate(flops=flops, bytes_accessed=1000, transcendentals=0),
-            name=name,
         )
 
     own = (2 * edges + 4) * SUBS
     halo = send * levels
-    near, side, far, odd, odd_side = call(
+    near, side, far = call(
         functools.partial(prepare, count=count),
-        "prepare",
         [
             shape((own + halo, LANES)),
             shape((own + halo, LANES)),
             shape((own, LANES)),
-            shape((halo, LANES)),
-            shape((halo, LANES)),
         ],
-        [SMEM, SMEM, SMEM] + [HBM] * 6,
-        [
-            pltpu.VMEM(tracer.shape, jnp.float32),
-            pltpu.VMEM(tile, jnp.int32),
-            pltpu.VMEM(neighbours.shape, jnp.int32),
-            pltpu.VMEM(edge_weight.shape, jnp.float32),
-            pltpu.VMEM(tile, jnp.float32),
-            pltpu.VMEM(tile, jnp.float32),
-            pltpu.SemaphoreType.DMA((6,)),
-        ],
+        [SMEM, SMEM, SMEM] + [VMEM] * 6,
+        [],
         4000000,
         60,
     )(
         place, slots, thickness, tracer, bottom, neighbours, edge_weight, ssh.reshape(tile),
         velocity.reshape(tile),
     )
-    part, columns, mine = call(
+    part, columns, mine, odd, odd_side, local = call(
         functools.partial(tracer_own, count=count),
-        "tracer_own",
-        [shape(tracer.shape), shape((levels, LANES)), shape((own, LANES))],
+        [
+            shape(tracer.shape),
+            shape((levels, LANES)),
+            shape((own, LANES)),
+            shape((halo, LANES)),
+            shape((halo, LANES)),
+            shape(neighbours.shape, jnp.int32),
+        ],
         [SMEM] * 4 + [VMEM] * 6,
         [pltpu.VMEM(tracer.shape, jnp.float32)],
         10000000,
@@ -592,23 +581,23 @@
         place, slots, thickness, profile, tracer, bottom, neighbours, edge_weight,
         ssh.reshape(tile), velocity.reshape(tile),
     )
-    side = lax.ppermute(side, "dom", even_swap(count, 2))
-    far = lax.ppermute(far, "dom", even_swap(count, 3))
-    near = lax.ppermute(near, "dom", even_swap(count, 1))
-    odd = lax.ppermute(odd, "dom", odd_swap(count, 1))
-    odd_side = lax.ppermute(odd_side, "dom", odd_swap(count, 2))
+
+    def send_on(value, way):
+        return lax.ppermute(value, "dom", way)
+
+    side = send_on(side, even_swap(count, 2))
+    far = send_on(far, even_swap(count, 3))
+    near = send_on(near, even_swap(count, 1))
+    odd = send_on(odd, odd_swap(count, 1))
+    odd_side = send_on(odd_side, odd_swap(count, 2))
 
     def swap(pair):
-        return (
-            lax.ppermute(pair[0], "dom", even_swap(count, TEAM)),
-            lax.ppermute(pair[1], "dom", odd_swap(count, TEAM)),
-        )
+        return (send_on(pair[0], even_swap(count, TEAM)), send_on(pair[1], odd_swap(count, TEAM)))
 
     state = [shape((TEAM,) + tile)] * 2
     entire = (6 + 2 * edges + 1) * SUBS
     *tables, height, speed, way_even, way_odd = call(
         gather_team,
-        "gather_team",
         [
             shape((TEAM, edges) + tile, jnp.int32),
             shape((TEAM, edges) + tile),
@@ -622,22 +611,19 @@
         500000,
     )(place, mine, near, side, far)
     constant = swap((way_even, way_odd))
-    base = call(
-        functools.partial(tracer_halo, count=count),
-        "tracer_halo",
-        shape(tracer.shape),
-        [SMEM] + [VMEM] * 9,
-        [],
-        10000000,
-    )(place, tracer, bottom, neighbours, edge_weight, part, near, odd, side, odd_side)
+    base = part
+    for ways, pair in (((0, 2), (near, side)), ((1, 3), (odd, odd_side))):
+        base = call(
+            functools.partial(tracer_halo, ways=ways), shape(tracer.shape), [VMEM] * 7, [], 5000000
+        )(tracer, bottom, local, edge_weight, base, *pair)
     scratch = [pltpu.VMEM((TEAM, 2 * SUBS, LANES), jnp.float32)] * 2
     light = [shape((6 * SUBS, LANES))] * 2
     height, speed, total, *ways = call(
-        first_pair, "first_pair", state + state[:1] + light, [SMEM] + [VMEM] * 8, scratch, 2000000
+        first_pair, state + state[:1] + light, [SMEM] + [VMEM] * 8, scratch, 2000000
     )(place, *tables, height, speed, *constant)
     arrived = swap(ways)
     height, speed, total, *ways = call(
-        middle_pair, "middle_pair", state + state[:1] + light, [SMEM] + [VMEM] * 11, scratch, 2000000
+        middle_pair, state + state[:1] + light, [SMEM] + [VMEM] * 11, scratch, 2000000
     )(place, *tables, height, speed, total, *arrived, *constant)
     arrived = swap(ways)
     team_scratch = [pltpu.VMEM((TEAM,) + tile, jnp.float32)] * 3
@@ -645,11 +631,11 @@
         functools.partial(last_pair, send=send),
         out_shape=[shape(tile), shape(tile), shape(tracer.shape)],
         in_specs=[SMEM] + [VMEM] * 14,
-        out_specs=[VMEM, VMEM, HBM],
+        out_specs=[HBM, HBM, HBM],
         scratch_shapes=[pltpu.VMEM(tracer.shape, jnp.float32)]
         + team_scratch
         + scratch
-        + [pltpu.SemaphoreType.DMA((levels // SUBS,))],
+        + [pltpu.SemaphoreType.DMA((levels // SUBS + 2,))],
         compiler_params=pltpu.CompilerParams(vmem_limit_bytes=4 << 20),
         cost_estimate=pl.CostEstimate(flops=2500000, bytes_accessed=1000, transcendentals=0),
         name="last_pair",
@@ -669,6 +655,7 @@
         P(),
         P(),
     )
+
     return jax.shard_map(
         shards,
         mesh=mesh,

time: 33.6 us -> 32.5 us (0.967)
  Pallas kernels: 14.1 us -> 13.4 us
    pallas_call x1, Pallas kernels: 2.34 us -> 1.76 us  [shards(): pl.pallas_call(functools.partial(last_pair, send=send), out_shape=[shape(...]
    pallas_call x6 -> x7, Pallas kernels: 11.7 us -> 11.6 us  [the longest x2 3.57 us: shards(): call(functools.partial(tracer_halo, ways=ways), shape(tracer.shape), [VME...]
  transfers between devices with their start and end apart: 11 -> 11, of which waited for: 3 -> 3; matrix products, arithmetic and copies ran while one was open for 0% -> 0% of each run, Pallas kernels for 23% -> 26%
where the time goes in v5:
time: 32.5 us; the launch traced here: 32.2 us
  Pallas kernels  13.4 us (41%)
  starting transfers between devices  12.9 us (40%)
  waiting for transfers between devices  5.16 us (16%)
  between operations  0.81 us (2%)
    ppermute x11, starting transfers between devices, send_on(): return lax.ppermute(value, 'dom', way)  12.9 us
    ppermute x11, waiting for transfers between devices, send_on(): return lax.ppermute(value, 'dom', way)  5.16 us
    pallas_call x2, Pallas kernels, shards(): call(functools.partial(tracer_halo, ways=ways), shape(tracer.shape), [VME...  3.57 us
    pallas_call x1, Pallas kernels, shards(): call(functools.partial(tracer_own, count=count), [shape(tracer.shape), sh...  3.53 us
    pallas_call x1, Pallas kernels, shards(): call(functools.partial(prepare, count=count), [shape((own + halo, LANES))...  1.87 us
    pallas_call x1, Pallas kernels, shards(): pl.pallas_call(functools.partial(last_pair, send=send), out_shape=[shape(...  1.76 us
    pallas_call x1, Pallas kernels, shards(): call(middle_pair, state + state[:1] + light, [SMEM] + [VMEM] * 11, scratc...  1.3 us
    pallas_call x1, Pallas kernels, shards(): call(first_pair, state + state[:1] + light, [SMEM] + [VMEM] * 8, scratch,...  1.3 us
  transfers between devices with their start and end apart: 11, of which 3 were waited for; matrix products, arithmetic and copies ran while one was open for 0% of the time, Pallas kernels for 26%

profile of v5, /device:TPU:9, one launch (start us, length us, event | category | flops | bytes accessed | tf_op | source)
XLA Modules:
  0.0 32.2 jit_solution(8565018358536137712)
XLA Ops:
  0.6 0.0 copy-start
  0.6 0.0 copy-start.1
  0.7 0.0 copy-start.2
  0.7 0.0 copy-start.4
  0.7 0.0 copy-start.5
  0.7 0.0 copy-start.8
  0.7 1.9 %shard_map.113 = (f32[208,128]{1,0:T(8,128)}, f32[208,128]{1,0:T(8,128)}, f32[128,128]{1,0:T(8,128)}) custom-call(s32[1]{0:T(128)} %bitcast.place_ref.place, s32[1,2,4]{2,1,0:T(2,128)} %bitcast.16, f32[40]{0:T(128)} %thick.3, f32[40,1024]{1,0:T(8,128)} %tracer.7, s32[8,128]{1,0:T(8,128)} %bitcast.7, s32[6,1024]{1,0:T(8,128)} %index.3, f32[6,1024]{1,0:T(8,128)} %weight.7, ...), custom_call_target="tpu_custom_call" | custom-call | flops 4000000 | bytes 1000 | tf_op jit(solution)/shard_map/pallas_call | solution.py:552
  2.6 0.0 copy-start.3
  2.6 0.7 %collective-permute-start = (f32[208,128]{1,0:T(8,128)}, f32[208,128]{1,0:T(8,128)S(1)}, u32[]{:S(2)}, u32[]{:S(2)}) collective-permute-start(f32[208,128]{1,0:T(8,128)} %get-tuple-element.34), channel_id=1, source_target_pairs={{0,1},{1,0},{2,3},{3,2},{4,5},{5,4},{6,7},{7,6},{8,9},{9,8},{10,11... | collective-permute-start | bytes 319496 | tf_op jit(solution)/shard_map/ppermute | solution.py:586
  3.2 0.0 copy-start.6
  3.2 0.0 copy-start.7
  3.2 1.2 %collective-permute-start.1 = (f32[208,128]{1,0:T(8,128)}, f32[208,128]{1,0:T(8,128)S(1)}, u32[]{:S(2)}, u32[]{:S(2)}) collective-permute-start(f32[208,128]{1,0:T(8,128)} %get-tuple-element.35), channel_id=1, source_target_pairs={{0,2},{1,3},{2,0},{3,1},{4,6},{5,7},{6,4},{7,5},{8,10},{9,11},{10,... | collective-permute-start | bytes 319496 | tf_op jit(solution)/shard_map/ppermute | solution.py:586
  4.5 0.5 %collective-permute-start.2 = (f32[128,128]{1,0:T(8,128)}, f32[128,128]{1,0:T(8,128)S(1)}, u32[]{:S(2)}, u32[]{:S(2)}) collective-permute-start(f32[128,128]{1,0:T(8,128)} %get-tuple-element.36), channel_id=1, source_target_pairs={{0,3},{1,2},{2,1},{3,0},{4,7},{5,6},{6,5},{7,4},{8,11},{9,10},{10,... | collective-permute-start | bytes 196616 | tf_op jit(solution)/shard_map/ppermute | solution.py:586
  5.0 0.0 copy-done
  5.0 0.0 copy-done.1
  5.0 0.0 copy-done.2
  5.0 0.0 copy-done.4
  5.0 0.0 copy-done.5
  5.0 0.0 copy-done.8
  5.0 0.0 copy-done.3
  5.0 0.0 copy-done.6
  5.0 0.0 copy-done.7
  5.0 3.5 %shard_map.112 = (f32[40,1024]{1,0:T(8,128)S(1)}, f32[40,128]{1,0:T(8,128)S(1)}, f32[128,128]{1,0:T(8,128)S(1)}, f32[80,128]{1,0:T(8,128)S(1)}, f32[80,128]{1,0:T(8,128)S(1)}, /*index=5*/s32[6,1024]{1,0:T(8,128)S(1)}) custom-call(s32[1]{0:T(128)} %bitcast.place_ref.place, s32[1,2,4]{2,1,0:T(2,128)S(1)} %bitcast.17, f32[40]{0:T(128)S(1)} %copy-done.7, ...), custom_call_target="tpu_custom_call" | custom-call | flops 10000000 | bytes 1000 | tf_op jit(solution)/shard_map/pallas_call | solution.py:567
  8.6 1.0 %collective-permute-done.2.far = f32[128,128]{1,0:T(8,128)S(1)} collective-permute-done((f32[128,128]{1,0:T(8,128)}, f32[128,128]{1,0:T(8,128)S(1)}, u32[]{:S(2)}, u32[]{:S(2)}) %collective-permute-start.2) | collective-permute-done | bytes 65568 | tf_op jit(solution)/shard_map/ppermute | solution.py:586
  9.6 0.0 collective-permute-done.near.a
  9.6 0.0 collective-permute-done.1.side.b
  9.6 0.1 shard_map.114
  9.6 1.3 %collective-permute-start.3 = (f32[152,128]{1,0:T(8,128)S(1)}, f32[152,128]{1,0:T(8,128)S(1)}, u32[]{:S(2)}, u32[]{:S(2)}) collective-permute-start(f32[152,128]{1,0:T(8,128)S(1)} %get-tuple-element.43), channel_id=1, source_target_pairs={{0,4},{1,5},{2,6},{3,7},{4,0},{5,1},{6,2},{7,3},{8,12},{9,13},{10,... | collective-permute-start | bytes 233480 | tf_op jit(solution)/shard_map/ppermute | solution.py:586
  10.9 0.0 collective-permute-start.4
  10.9 2.5 %collective-permute-done.3.even_in.first_even = f32[152,128]{1,0:T(8,128)S(1)} collective-permute-done((f32[152,128]{1,0:T(8,128)S(1)}, f32[152,128]{1,0:T(8,128)S(1)}, u32[]{:S(2)}, u32[]{:S(2)}) %collective-permute-start.3) | collective-permute-done | bytes 77856 | tf_op jit(solution)/shard_map/ppermute | solution.py:586
  13.5 1.6 %collective-permute-done.4.odd_in.first_odd = f32[152,128]{1,0:T(8,128)S(1)} collective-permute-done((f32[152,128]{1,0:T(8,128)S(1)}, f32[152,128]{1,0:T(8,128)S(1)}, u32[]{:S(2)}, u32[]{:S(2)}) %collective-permute-start.4) | collective-permute-done | bytes 77856 | tf_op jit(solution)/shard_map/ppermute | solution.py:586
  15.1 1.3 %shard_map.115 = (f32[4,8,128]{2,1,0:T(8,128)S(1)}, f32[4,8,128]{2,1,0:T(8,128)S(1)}, f32[4,8,128]{2,1,0:T(8,128)S(1)}, f32[48,128]{1,0:T(8,128)S(1)}, f32[48,128]{1,0:T(8,128)S(1)}) custom-call(s32[1]{0:T(128)} %bitcast.place_ref.place, s32[4,6,8,128]{3,2,1,0:T(8,128)S(1)} %get-tuple-element.37.index, f32[4,6,8,128]{3,2,1,0:T(8,128)S(1)} %get-tuple-element.38.weight, ...), custom_call_target="tpu_custom_call" | custom-call | flops 2000000 | bytes 1000 | tf_op jit(solution)/shard_map/pallas_call | solution.py:621
  16.4 0.4 %collective-permute-start.5 = (f32[48,128]{1,0:T(8,128)S(1)}, f32[48,128]{1,0:T(8,128)S(1)}, u32[]{:S(2)}, u32[]{:S(2)}) collective-permute-start(f32[48,128]{1,0:T(8,128)S(1)} %get-tuple-element.48), channel_id=1, source_target_pairs={{0,4},{1,5},{2,6},{3,7},{4,0},{5,1},{6,2},{7,3},{8,12},{9,13},{10,... | collective-permute-start | bytes 73736 | tf_op jit(solution)/shard_map/ppermute | solution.py:586
  16.8 0.0 collective-permute-start.6
  16.8 3.3 %collective-permute-start.9 = (f32[80,128]{1,0:T(8,128)S(1)}, f32[80,128]{1,0:T(8,128)S(1)}, u32[]{:S(2)}, u32[]{:S(2)}) collective-permute-start(f32[80,128]{1,0:T(8,128)S(1)} %get-tuple-element.57), channel_id=1, source_target_pairs={{1,2},{3,4},{5,6},{7,8},{9,10},{11,12},{13,14},{15,16},{17,18},{19... | collective-permute-start | bytes 122888 | tf_op jit(solution)/shard_map/ppermute | solution.py:586
  20.1 2.1 %collective-permute-start.10 = (f32[80,128]{1,0:T(8,128)S(1)}, f32[80,128]{1,0:T(8,128)S(1)}, u32[]{:S(2)}, u32[]{:S(2)}) collective-permute-start(f32[80,128]{1,0:T(8,128)S(1)} %get-tuple-element.58), channel_id=1, source_target_pairs={{2,4},{3,5},{6,8},{7,9},{10,12},{11,13},{14,16},{15,17},{18,20},{1... | collective-permute-start | bytes 122888 | tf_op jit(solution)/shard_map/ppermute | solution.py:586
  22.2 0.0 collective-permute-done.5.even_in
  22.2 0.0 collective-permute-done.6.odd_in
  22.2 1.3 %shard_map.116 = (f32[4,8,128]{2,1,0:T(8,128)S(1)}, f32[4,8,128]{2,1,0:T(8,128)S(1)}, f32[4,8,128]{2,1,0:T(8,128)S(1)}, f32[48,128]{1,0:T(8,128)S(1)}, f32[48,128]{1,0:T(8,128)S(1)}) custom-call(s32[1]{0:T(128)} %bitcast.place_ref.place, s32[4,6,8,128]{3,2,1,0:T(8,128)S(1)} %get-tuple-element.37.index, f32[4,6,8,128]{3,2,1,0:T(8,128)S(1)} %get-tuple-element.38.weight, ...), custom_call_target="tpu_custom_call" | custom-call | flops 2000000 | bytes 1000 | tf_op jit(solution)/shard_map/pallas_call | solution.py:625
  23.5 1.9 %collective-permute-start.7 = (f32[48,128]{1,0:T(8,128)S(1)}, f32[48,128]{1,0:T(8,128)S(1)}, u32[]{:S(2)}, u32[]{:S(2)}) collective-permute-start(f32[48,128]{1,0:T(8,128)S(1)} %get-tuple-element.53), channel_id=1, source_target_pairs={{0,4},{1,5},{2,6},{3,7},{4,0},{5,1},{6,2},{7,3},{8,12},{9,13},{10,... | collective-permute-start | bytes 73736 | tf_op jit(solution)/shard_map/ppermute | solution.py:586
  25.4 1.4 %collective-permute-start.8 = (f32[48,128]{1,0:T(8,128)S(1)}, f32[48,128]{1,0:T(8,128)S(1)}, u32[]{:S(2)}, u32[]{:S(2)}) collective-permute-start(f32[48,128]{1,0:T(8,128)S(1)} %get-tuple-element.54), channel_id=1, source_target_pairs={{4,8},{5,9},{6,10},{7,11},{12,16},{13,17},{14,18},{15,19},{20,24},... | collective-permute-start | bytes 73736 | tf_op jit(solution)/shard_map/ppermute | solution.py:586
  26.9 1.8 %shard_map.117.part = f32[40,1024]{1,0:T(8,128)S(1)} custom-call(f32[40,1024]{1,0:T(8,128)S(1)} %copy-done, s32[8,128]{1,0:T(8,128)S(1)} %bitcast.9, s32[6,1024]{1,0:T(8,128)S(1)} %get-tuple-element.55.local, f32[6,1024]{1,0:T(8,128)S(1)} %copy-done.1, f32[40,1024]{1,0:T(8,128)S(1)} %get-tuple-element.56.part, f32[208,128]{1,0:T(8,128)S(1)} %collective-permute-done.near.a, ...), custom_call_target="tpu_custom_call" | custom-call | flops 5000000 | bytes 1000 | tf_op jit(solution)/shard_map/pallas_call | solution.py:616
  28.7 0.0 collective-permute-done.9.a
  28.7 0.0 collective-permute-done.10.b
  28.7 1.8 %shard_map.118.base = f32[40,1024]{1,0:T(8,128)S(1)} custom-call(f32[40,1024]{1,0:T(8,128)S(1)} %copy-done, s32[8,128]{1,0:T(8,128)S(1)} %bitcast.10, s32[6,1024]{1,0:T(8,128)S(1)} %get-tuple-element.55.local, f32[6,1024]{1,0:T(8,128)S(1)} %copy-done.1, f32[40,1024]{1,0:T(8,128)S(1)} %shard_map.117.part, f32[80,128]{1,0:T(8,128)S(1)} %collective-permute-done.9.a, ...), custom_call_target="tpu_custom_call" | custom-call | flops 5000000 | bytes 1000 | tf_op jit(solution)/shard_map/pallas_call | solution.py:616
  30.5 0.0 collective-permute-done.7.even_in
  30.5 0.0 collective-permute-done.8.odd_in
  30.5 1.8 %last_pair.1 = (f32[8,128]{1,0:T(8,128)}, f32[8,128]{1,0:T(8,128)}, f32[40,1024]{1,0:T(8,128)}) custom-call(s32[1]{0:T(128)} %bitcast.place_ref.place, s32[4,6,8,128]{3,2,1,0:T(8,128)S(1)} %get-tuple-element.37.index, f32[4,6,8,128]{3,2,1,0:T(8,128)S(1)} %get-tuple-element.38.weight, f32[4,8,128]{2,1,0:T(8,128)S(1)} %get-tuple-element.39.force, ...), custom_call_target="tpu_custom_call" | custom-call | flops 2500000 | bytes 1000 | tf_op jit(solution)/shard_map/last_pair/pallas_call | solution.py:630
Async XLA Ops:
  0.6 4.3 %copy-start = (f32[40,1024]{1,0:T(8,128)S(1)}, f32[40,1024]{1,0:T(8,128)}, u32[]{:S(2)}) copy-start(f32[40,1024]{1,0:T(8,128)} %tracer.7) | copy-start | bytes 491524
  0.6 4.3 %copy-start.1 = (f32[6,1024]{1,0:T(8,128)S(1)}, f32[6,1024]{1,0:T(8,128)}, u32[]{:S(2)}) copy-start(f32[6,1024]{1,0:T(8,128)} %weight.7) | copy-start | bytes 73732
  0.7 4.3 %copy-start.2 = (s32[6,1024]{1,0:T(8,128)S(1)}, s32[6,1024]{1,0:T(8,128)}, u32[]{:S(2)}) copy-start(s32[6,1024]{1,0:T(8,128)} %index.3) | copy-start | bytes 73732
  0.7 4.3 %copy-start.4 = (f32[1024]{0:T(1024)S(1)}, f32[1024]{0:T(1024)}, u32[]{:S(2)}) copy-start(f32[1024]{0:T(1024)} %param.13) | copy-start | bytes 12292
  0.7 4.3 %copy-start.5 = (f32[1024]{0:T(1024)S(1)}, f32[1024]{0:T(1024)}, u32[]{:S(2)}) copy-start(f32[1024]{0:T(1024)} %param.14) | copy-start | bytes 12292
  0.7 4.3 %copy-start.8 = (f32[40]{0:T(128)S(1)}, f32[40]{0:T(128)}, u32[]{:S(2)}) copy-start(f32[40]{0:T(128)} %profile.1) | copy-start | bytes 484
  2.6 2.4 %copy-start.3 = (s32[1024]{0:T(1024)S(1)}, s32[1024]{0:T(1024)}, u32[]{:S(2)}) copy-start(s32[1024]{0:T(1024)} %param.10) | copy-start | bytes 12292
  2.6 7.0 %collective-permute-start = (f32[208,128]{1,0:T(8,128)}, f32[208,128]{1,0:T(8,128)S(1)}, u32[]{:S(2)}, u32[]{:S(2)}) collective-permute-start(f32[208,128]{1,0:T(8,128)} %get-tuple-element.34), channel_id=1, source_target_pairs={{0,1},{1,0},{2,3},{3,2},{4,5},{5,4},{6,7},{7,6},{8,9},{9,8},{10,11... | collective-permute-start | bytes 319496 | tf_op jit(solution)/shard_map/ppermute | solution.py:586
  3.2 1.8 %copy-start.6 = (s32[1,4,2]{1,2,0:T(2,128)S(1)}, s32[1,4,2]{1,2,0:T(2,128)}, u32[]{:S(2)}) copy-start(s32[1,4,2]{1,2,0:T(2,128)} %param.15) | copy-start | bytes 100
  3.2 1.8 %copy-start.7 = (f32[40]{0:T(128)S(1)}, f32[40]{0:T(128)}, u32[]{:S(2)}) copy-start(f32[40]{0:T(128)} %thick.3) | copy-start | bytes 484
  3.2 6.3 %collective-permute-start.1 = (f32[208,128]{1,0:T(8,128)}, f32[208,128]{1,0:T(8,128)S(1)}, u32[]{:S(2)}, u32[]{:S(2)}) collective-permute-start(f32[208,128]{1,0:T(8,128)} %get-tuple-element.35), channel_id=1, source_target_pairs={{0,2},{1,3},{2,0},{3,1},{4,6},{5,7},{6,4},{7,5},{8,10},{9,11},{10,... | collective-permute-start | bytes 319496 | tf_op jit(solution)/shard_map/ppermute | solution.py:586
  4.5 5.1 %collective-permute-start.2 = (f32[128,128]{1,0:T(8,128)}, f32[128,128]{1,0:T(8,128)S(1)}, u32[]{:S(2)}, u32[]{:S(2)}) collective-permute-start(f32[128,128]{1,0:T(8,128)} %get-tuple-element.36), channel_id=1, source_target_pairs={{0,3},{1,2},{2,1},{3,0},{4,7},{5,6},{6,5},{7,4},{8,11},{9,10},{10,... | collective-permute-start | bytes 196616 | tf_op jit(solution)/shard_map/ppermute | solution.py:586
  9.6 3.8 %collective-permute-start.3 = (f32[152,128]{1,0:T(8,128)S(1)}, f32[152,128]{1,0:T(8,128)S(1)}, u32[]{:S(2)}, u32[]{:S(2)}) collective-permute-start(f32[152,128]{1,0:T(8,128)S(1)} %get-tuple-element.43), channel_id=1, source_target_pairs={{0,4},{1,5},{2,6},{3,7},{4,0},{5,1},{6,2},{7,3},{8,12},{9,13},{10,... | collective-permute-start | bytes 233480 | tf_op jit(solution)/shard_map/ppermute | solution.py:586
  10.9 4.1 %collective-permute-start.4 = (f32[152,128]{1,0:T(8,128)S(1)}, f32[152,128]{1,0:T(8,128)S(1)}, u32[]{:S(2)}, u32[]{:S(2)}) collective-permute-start(f32[152,128]{1,0:T(8,128)S(1)} %get-tuple-element.44), channel_id=1, source_target_pairs={{4,8},{5,9},{6,10},{7,11},{12,16},{13,17},{14,18},{15,19},{20,24},... | collective-permute-start | bytes 233480 | tf_op jit(solution)/shard_map/ppermute | solution.py:586
  16.4 5.8 %collective-permute-start.5 = (f32[48,128]{1,0:T(8,128)S(1)}, f32[48,128]{1,0:T(8,128)S(1)}, u32[]{:S(2)}, u32[]{:S(2)}) collective-permute-start(f32[48,128]{1,0:T(8,128)S(1)} %get-tuple-element.48), channel_id=1, source_target_pairs={{0,4},{1,5},{2,6},{3,7},{4,0},{5,1},{6,2},{7,3},{8,12},{9,13},{10,... | collective-permute-start | bytes 73736 | tf_op jit(solution)/shard_map/ppermute | solution.py:586
  16.8 5.4 %collective-permute-start.6 = (f32[48,128]{1,0:T(8,128)S(1)}, f32[48,128]{1,0:T(8,128)S(1)}, u32[]{:S(2)}, u32[]{:S(2)}) collective-permute-start(f32[48,128]{1,0:T(8,128)S(1)} %get-tuple-element.49), channel_id=1, source_target_pairs={{4,8},{5,9},{6,10},{7,11},{12,16},{13,17},{14,18},{15,19},{20,24},... | collective-permute-start | bytes 73736 | tf_op jit(solution)/shard_map/ppermute | solution.py:586
  16.8 11.9 %collective-permute-start.9 = (f32[80,128]{1,0:T(8,128)S(1)}, f32[80,128]{1,0:T(8,128)S(1)}, u32[]{:S(2)}, u32[]{:S(2)}) collective-permute-start(f32[80,128]{1,0:T(8,128)S(1)} %get-tuple-element.57), channel_id=1, source_target_pairs={{1,2},{3,4},{5,6},{7,8},{9,10},{11,12},{13,14},{15,16},{17,18},{19... | collective-permute-start | bytes 122888 | tf_op jit(solution)/shard_map/ppermute | solution.py:586
  20.1 8.5 %collective-permute-start.10 = (f32[80,128]{1,0:T(8,128)S(1)}, f32[80,128]{1,0:T(8,128)S(1)}, u32[]{:S(2)}, u32[]{:S(2)}) collective-permute-start(f32[80,128]{1,0:T(8,128)S(1)} %get-tuple-element.58), channel_id=1, source_target_pairs={{2,4},{3,5},{6,8},{7,9},{10,12},{11,13},{14,16},{15,17},{18,20},{1... | collective-permute-start | bytes 122888 | tf_op jit(solution)/shard_map/ppermute | solution.py:586
  23.5 7.0 %collective-permute-start.7 = (f32[48,128]{1,0:T(8,128)S(1)}, f32[48,128]{1,0:T(8,128)S(1)}, u32[]{:S(2)}, u32[]{:S(2)}) collective-permute-start(f32[48,128]{1,0:T(8,128)S(1)} %get-tuple-element.53), channel_id=1, source_target_pairs={{0,4},{1,5},{2,6},{3,7},{4,0},{5,1},{6,2},{7,3},{8,12},{9,13},{10,... | collective-permute-start | bytes 73736 | tf_op jit(solution)/shard_map/ppermute | solution.py:586
  25.4 5.1 %collective-permute-start.8 = (f32[48,128]{1,0:T(8,128)S(1)}, f32[48,128]{1,0:T(8,128)S(1)}, u32[]{:S(2)}, u32[]{:S(2)}) collective-permute-start(f32[48,128]{1,0:T(8,128)S(1)} %get-tuple-element.54), channel_id=1, source_target_pairs={{4,8},{5,9},{6,10},{7,11},{12,16},{13,17},{14,18},{15,19},{20,24},... | collective-permute-start | bytes 73736 | tf_op jit(solution)/shard_map/ppermute | solution.py:586

commit v6 on v5

--- a/solution.py
+++ b/solution.py
@@ -102,16 +102,28 @@
 
 
 def prepare(
-    place_ref, slots, thick, tracer, bottom, index, weight, ssh, velocity, near, side, far, *,
-    count, send,
+    place_ref, slots, thick, tracer, bottom, index, weight, ssh, velocity, near, side, far, mine, by_one,
+    by_two, sems, *, count, send,
 ):
     place = place_ref[0]
-    tracer_blocks(place, slots, tracer, bottom, ((0, near), (2, side)), send)
-    own_tables(place, slots, thick, tracer, bottom, index, weight, ssh, velocity, far, count, send)
-    for k in range(far.shape[0] // SUBS):
-        at = slice(k * SUBS, (k + 1) * SUBS)
-        near[at, :] = far[at, :]
-        side[at, :] = far[at, :]
+    own = mine.shape[0]
+    tracer_blocks(place, slots, tracer, bottom, ((0, by_one), (2, by_two)), send)
+    copies = [
+        pltpu.make_async_copy(by_two, side.at[own:, :], sems.at[0]),
+        pltpu.make_async_copy(by_one, near.at[own:, :], sems.at[1]),
+    ]
+    for copy in copies:
+        copy.start()
+    own_tables(place, slots, thick, tracer, bottom, index, weight, ssh, velocity, mine, count, send)
+    late = [
+        pltpu.make_async_copy(mine, side.at[:own, :], sems.at[2]),
+        pltpu.make_async_copy(mine, far, sems.at[3]),
+        pltpu.make_async_copy(mine, near.at[:own, :], sems.at[4]),
+    ]
+    for copy in late:
+        copy.start()
+    for copy in copies + late:
+        copy.wait()
 
 
 def own_tables(
@@ -269,7 +281,7 @@
         ref_even, ref_odd = (first_even, first_odd) if constant else (even_in, odd_in)
         at = slice(k * SUBS, (k + 1) * SUBS)
         a, b = ref_even[at, :], ref_odd[at, :]
-        return jnp.where(even, a, b) if right else jnp.where(even, b, a)
+        return jnp.where(even == right, a, b)
 
     def fill(heights, left, right):
         out = [outgoing(h, s) for h, s in zip(heights, held)]
@@ -314,8 +326,15 @@
     virtual[3, 0:SUBS, :] = side_of(1, False, True)
     virtual[3, SUBS : 2 * SUBS, :] = side_of(3, False, True) + blend(rows, send, {2: out[3]})
     later, faster = advance_team(heights, speeds)
-    for number, right in enumerate((False, True)):
-        moved_group = 2 if right else 3
+    if only is None:
+        wanted = ((0, False), (1, True))
+    else:
+        right = only >= TEAM // 2
+        wanted = ((right.astype(jnp.int32), right),)
+    moved_edges = []
+    for number, right in wanted:
+        before = jnp.where(right, edge[1], edge[0])
+        moved_group = jnp.where(right, 2, 3)
         laplace = gathered(
             lambda r: jnp.where(
                 group_of(rows, send) == moved_group,
@@ -324,12 +343,12 @@
             ),
             [side_of(6 + j, True, right).astype(jnp.int32) for j in range(edges)],
             [side_of(6 + edges + j, True, right) for j in range(edges)],
-            edge[number],
+            before,
             2 * SUBS,
         )
-        edge[number] = stepped(
-            laplace, side_of(6 + 2 * edges, True, right), edge[number], side_of(5, False, right)
-        )[0]
+        force_here = side_of(6 + 2 * edges, True, right)
+        moved_edges.append(stepped(laplace, force_here, before, side_of(5, False, right))[0])
+    edge = [moved_edges[0], moved_edges[-1]]
     fill(later, edge[0], edge[1])
     if only is not None:
         for q in range(TEAM):
@@ -537,11 +556,14 @@
     def shape(rows, kind=jnp.float32):
         return jax.ShapeDtypeStruct(rows, kind)
 
-    def call(body, outs, ins, scratch, flops, limit=4):
+    def call(body, outs, ins, scratch, flops, limit=4, placed=None):
+        if placed is None:
+            placed = jax.tree.map(lambda _: VMEM, outs)
         return pl.pallas_call(
             functools.partial(body, send=send),
             out_shape=outs,
             in_specs=ins,
+            out_specs=placed,
             scratch_shapes=scratch,
             compiler_params=pltpu.CompilerParams(vmem_limit_bytes=limit << 20),
             cost_estimate=pl.CostEstimate(flops=flops, bytes_accessed=1000, transcendentals=0),
@@ -557,9 +579,15 @@
             shape((own, LANES)),
         ],
         [SMEM, SMEM, SMEM] + [VMEM] * 6,
-        [],
+        [
+            pltpu.VMEM((own, LANES), jnp.float32),
+            pltpu.VMEM((halo, LANES), jnp.float32),
+            pltpu.VMEM((halo, LANES), jnp.float32),
+            pltpu.SemaphoreType.DMA((5,)),
+        ],
         4000000,
         60,
+        [HBM] * 3,
     )(
         place, slots, thickness, tracer, bottom, neighbours, edge_weight, ssh.reshape(tile),
         velocity.reshape(tile),

time: 32.5 us -> 32.5 us (level)
  no operation moved by 1% of the time
where the time goes in v6:
time: 32.5 us; the launch traced here: 32.2 us
  Pallas kernels  13.3 us (41%)
  starting transfers between devices  12.9 us (40%)
  waiting for transfers between devices  5.15 us (16%)
  between operations  0.83 us (3%)
    ppermute x11, starting transfers between devices, send_on(): return lax.ppermute(value, 'dom', way)  12.9 us
    ppermute x11, waiting for transfers between devices, send_on(): return lax.ppermute(value, 'dom', way)  5.15 us
    pallas_call x2, Pallas kernels, shards(): call(functools.partial(tracer_halo, ways=ways), shape(tracer.shape), [VME...  3.57 us
    pallas_call x1, Pallas kernels, shards(): call(functools.partial(tracer_own, count=count), [shape(tracer.shape), sh...  3.53 us
    pallas_call x1, Pallas kernels, shards(): call(functools.partial(prepare, count=count), [shape((own + halo, LANES))...  1.88 us
    pallas_call x1, Pallas kernels, shards(): pl.pallas_call(functools.partial(last_pair, send=send), out_shape=[shape(...  1.64 us
    pallas_call x1, Pallas kernels, shards(): call(middle_pair, state + state[:1] + light, [SMEM] + [VMEM] * 11, scratc...  1.3 us
    pallas_call x1, Pallas kernels, shards(): call(first_pair, state + state[:1] + light, [SMEM] + [VMEM] * 8, scratch,...  1.3 us
  transfers between devices with their start and end apart: 11, of which 3 were waited for; matrix products, arithmetic and copies ran while one was open for 0% of the time, Pallas kernels for 26%

profile of v6, /device:TPU:9, one launch (start us, length us, event | category | flops | bytes accessed | tf_op | source)
XLA Modules:
  0.0 32.2 jit_solution(6546318063628324270)
XLA Ops:
  0.6 0.0 copy-start
  0.6 0.0 copy-start.1
  0.7 0.0 copy-start.2
  0.7 0.0 copy-start.4
  0.7 0.0 copy-start.5
  0.7 0.0 copy-start.8
  0.7 1.9 %shard_map.113 = (f32[208,128]{1,0:T(8,128)}, f32[208,128]{1,0:T(8,128)}, f32[128,128]{1,0:T(8,128)}) custom-call(s32[1]{0:T(128)} %bitcast.place_ref.place, s32[1,2,4]{2,1,0:T(2,128)} %bitcast.16, f32[40]{0:T(128)} %thick.3, f32[40,1024]{1,0:T(8,128)} %tracer.7, s32[8,128]{1,0:T(8,128)} %bitcast.7, s32[6,1024]{1,0:T(8,128)} %index.3, f32[6,1024]{1,0:T(8,128)} %weight.7, ...), custom_call_target="tpu_custom_call" | custom-call | flops 4000000 | bytes 1000 | tf_op jit(solution)/shard_map/pallas_call | solution.py:574
  2.6 0.0 copy-start.3
  2.6 0.7 %collective-permute-start = (f32[208,128]{1,0:T(8,128)}, f32[208,128]{1,0:T(8,128)S(1)}, u32[]{:S(2)}, u32[]{:S(2)}) collective-permute-start(f32[208,128]{1,0:T(8,128)} %get-tuple-element.34), channel_id=1, source_target_pairs={{0,1},{1,0},{2,3},{3,2},{4,5},{5,4},{6,7},{7,6},{8,9},{9,8},{10,11... | collective-permute-start | bytes 319496 | tf_op jit(solution)/shard_map/ppermute | solution.py:614
  3.3 0.0 copy-start.6
  3.3 0.0 copy-start.7
  3.3 1.2 %collective-permute-start.1 = (f32[208,128]{1,0:T(8,128)}, f32[208,128]{1,0:T(8,128)S(1)}, u32[]{:S(2)}, u32[]{:S(2)}) collective-permute-start(f32[208,128]{1,0:T(8,128)} %get-tuple-element.35), channel_id=1, source_target_pairs={{0,2},{1,3},{2,0},{3,1},{4,6},{5,7},{6,4},{7,5},{8,10},{9,11},{10,... | collective-permute-start | bytes 319496 | tf_op jit(solution)/shard_map/ppermute | solution.py:614
  4.5 0.5 %collective-permute-start.2 = (f32[128,128]{1,0:T(8,128)}, f32[128,128]{1,0:T(8,128)S(1)}, u32[]{:S(2)}, u32[]{:S(2)}) collective-permute-start(f32[128,128]{1,0:T(8,128)} %get-tuple-element.36), channel_id=1, source_target_pairs={{0,3},{1,2},{2,1},{3,0},{4,7},{5,6},{6,5},{7,4},{8,11},{9,10},{10,... | collective-permute-start | bytes 196616 | tf_op jit(solution)/shard_map/ppermute | solution.py:614
  5.1 0.0 copy-done
  5.1 0.0 copy-done.1
  5.1 0.0 copy-done.2
  5.1 0.0 copy-done.4
  5.1 0.0 copy-done.5
  5.1 0.0 copy-done.8
  5.1 0.0 copy-done.3
  5.1 0.0 copy-done.6
  5.1 0.0 copy-done.7
  5.1 3.5 %shard_map.112 = (f32[40,1024]{1,0:T(8,128)S(1)}, f32[40,128]{1,0:T(8,128)S(1)}, f32[128,128]{1,0:T(8,128)S(1)}, f32[80,128]{1,0:T(8,128)S(1)}, f32[80,128]{1,0:T(8,128)S(1)}, /*index=5*/s32[6,1024]{1,0:T(8,128)S(1)}) custom-call(s32[1]{0:T(128)} %bitcast.place_ref.place, s32[1,2,4]{2,1,0:T(2,128)S(1)} %bitcast.17, f32[40]{0:T(128)S(1)} %copy-done.7, ...), custom_call_target="tpu_custom_call" | custom-call | flops 10000000 | bytes 1000 | tf_op jit(solution)/shard_map/pallas_call | solution.py:595
  8.7 1.0 %collective-permute-done.2.far = f32[128,128]{1,0:T(8,128)S(1)} collective-permute-done((f32[128,128]{1,0:T(8,128)}, f32[128,128]{1,0:T(8,128)S(1)}, u32[]{:S(2)}, u32[]{:S(2)}) %collective-permute-start.2) | collective-permute-done | bytes 65568 | tf_op jit(solution)/shard_map/ppermute | solution.py:614
  9.6 0.0 collective-permute-done.near.a
  9.7 0.0 collective-permute-done.1.side.b
  9.7 0.1 shard_map.114
  9.7 1.3 %collective-permute-start.3 = (f32[152,128]{1,0:T(8,128)S(1)}, f32[152,128]{1,0:T(8,128)S(1)}, u32[]{:S(2)}, u32[]{:S(2)}) collective-permute-start(f32[152,128]{1,0:T(8,128)S(1)} %get-tuple-element.43), channel_id=1, source_target_pairs={{0,4},{1,5},{2,6},{3,7},{4,0},{5,1},{6,2},{7,3},{8,12},{9,13},{10,... | collective-permute-start | bytes 233480 | tf_op jit(solution)/shard_map/ppermute | solution.py:614
  11.0 0.0 collective-permute-start.4
  11.0 2.5 %collective-permute-done.3.even_in.first_even = f32[152,128]{1,0:T(8,128)S(1)} collective-permute-done((f32[152,128]{1,0:T(8,128)S(1)}, f32[152,128]{1,0:T(8,128)S(1)}, u32[]{:S(2)}, u32[]{:S(2)}) %collective-permute-start.3) | collective-permute-done | bytes 77856 | tf_op jit(solution)/shard_map/ppermute | solution.py:614
  13.6 1.6 %collective-permute-done.4.odd_in.first_odd = f32[152,128]{1,0:T(8,128)S(1)} collective-permute-done((f32[152,128]{1,0:T(8,128)S(1)}, f32[152,128]{1,0:T(8,128)S(1)}, u32[]{:S(2)}, u32[]{:S(2)}) %collective-permute-start.4) | collective-permute-done | bytes 77856 | tf_op jit(solution)/shard_map/ppermute | solution.py:614
  15.2 1.3 %shard_map.115 = (f32[4,8,128]{2,1,0:T(8,128)S(1)}, f32[4,8,128]{2,1,0:T(8,128)S(1)}, f32[4,8,128]{2,1,0:T(8,128)S(1)}, f32[48,128]{1,0:T(8,128)S(1)}, f32[48,128]{1,0:T(8,128)S(1)}) custom-call(s32[1]{0:T(128)} %bitcast.place_ref.place, s32[4,6,8,128]{3,2,1,0:T(8,128)S(1)} %get-tuple-element.37.index, f32[4,6,8,128]{3,2,1,0:T(8,128)S(1)} %get-tuple-element.38.weight, ...), custom_call_target="tpu_custom_call" | custom-call | flops 2000000 | bytes 1000 | tf_op jit(solution)/shard_map/pallas_call | solution.py:649
  16.5 0.4 %collective-permute-start.5 = (f32[48,128]{1,0:T(8,128)S(1)}, f32[48,128]{1,0:T(8,128)S(1)}, u32[]{:S(2)}, u32[]{:S(2)}) collective-permute-start(f32[48,128]{1,0:T(8,128)S(1)} %get-tuple-element.48), channel_id=1, source_target_pairs={{0,4},{1,5},{2,6},{3,7},{4,0},{5,1},{6,2},{7,3},{8,12},{9,13},{10,... | collective-permute-start | bytes 73736 | tf_op jit(solution)/shard_map/ppermute | solution.py:614
  16.9 0.0 collective-permute-start.6
  16.9 3.3 %collective-permute-start.9 = (f32[80,128]{1,0:T(8,128)S(1)}, f32[80,128]{1,0:T(8,128)S(1)}, u32[]{:S(2)}, u32[]{:S(2)}) collective-permute-start(f32[80,128]{1,0:T(8,128)S(1)} %get-tuple-element.57), channel_id=1, source_target_pairs={{1,2},{3,4},{5,6},{7,8},{9,10},{11,12},{13,14},{15,16},{17,18},{19... | collective-permute-start | bytes 122888 | tf_op jit(solution)/shard_map/ppermute | solution.py:614
  20.2 2.1 %collective-permute-start.10 = (f32[80,128]{1,0:T(8,128)S(1)}, f32[80,128]{1,0:T(8,128)S(1)}, u32[]{:S(2)}, u32[]{:S(2)}) collective-permute-start(f32[80,128]{1,0:T(8,128)S(1)} %get-tuple-element.58), channel_id=1, source_target_pairs={{2,4},{3,5},{6,8},{7,9},{10,12},{11,13},{14,16},{15,17},{18,20},{1... | collective-permute-start | bytes 122888 | tf_op jit(solution)/shard_map/ppermute | solution.py:614
  22.3 0.0 collective-permute-done.5.even_in
  22.3 0.0 collective-permute-done.6.odd_in
  22.3 1.3 %shard_map.116 = (f32[4,8,128]{2,1,0:T(8,128)S(1)}, f32[4,8,128]{2,1,0:T(8,128)S(1)}, f32[4,8,128]{2,1,0:T(8,128)S(1)}, f32[48,128]{1,0:T(8,128)S(1)}, f32[48,128]{1,0:T(8,128)S(1)}) custom-call(s32[1]{0:T(128)} %bitcast.place_ref.place, s32[4,6,8,128]{3,2,1,0:T(8,128)S(1)} %get-tuple-element.37.index, f32[4,6,8,128]{3,2,1,0:T(8,128)S(1)} %get-tuple-element.38.weight, ...), custom_call_target="tpu_custom_call" | custom-call | flops 2000000 | bytes 1000 | tf_op jit(solution)/shard_map/pallas_call | solution.py:653
  23.6 1.9 %collective-permute-start.7 = (f32[48,128]{1,0:T(8,128)S(1)}, f32[48,128]{1,0:T(8,128)S(1)}, u32[]{:S(2)}, u32[]{:S(2)}) collective-permute-start(f32[48,128]{1,0:T(8,128)S(1)} %get-tuple-element.53), channel_id=1, source_target_pairs={{0,4},{1,5},{2,6},{3,7},{4,0},{5,1},{6,2},{7,3},{8,12},{9,13},{10,... | collective-permute-start | bytes 73736 | tf_op jit(solution)/shard_map/ppermute | solution.py:614
  25.5 1.4 %collective-permute-start.8 = (f32[48,128]{1,0:T(8,128)S(1)}, f32[48,128]{1,0:T(8,128)S(1)}, u32[]{:S(2)}, u32[]{:S(2)}) collective-permute-start(f32[48,128]{1,0:T(8,128)S(1)} %get-tuple-element.54), channel_id=1, source_target_pairs={{4,8},{5,9},{6,10},{7,11},{12,16},{13,17},{14,18},{15,19},{20,24},... | collective-permute-start | bytes 73736 | tf_op jit(solution)/shard_map/ppermute | solution.py:614
  26.9 1.8 %shard_map.117.part = f32[40,1024]{1,0:T(8,128)S(1)} custom-call(f32[40,1024]{1,0:T(8,128)S(1)} %copy-done, s32[8,128]{1,0:T(8,128)S(1)} %bitcast.9, s32[6,1024]{1,0:T(8,128)S(1)} %get-tuple-element.55.local, f32[6,1024]{1,0:T(8,128)S(1)} %copy-done.1, f32[40,1024]{1,0:T(8,128)S(1)} %get-tuple-element.56.part, f32[208,128]{1,0:T(8,128)S(1)} %collective-permute-done.near.a, ...), custom_call_target="tpu_custom_call" | custom-call | flops 5000000 | bytes 1000 | tf_op jit(solution)/shard_map/pallas_call | solution.py:644
  28.7 0.0 collective-permute-done.9.a
  28.8 0.0 collective-permute-done.10.b
  28.8 1.8 %shard_map.118.base = f32[40,1024]{1,0:T(8,128)S(1)} custom-call(f32[40,1024]{1,0:T(8,128)S(1)} %copy-done, s32[8,128]{1,0:T(8,128)S(1)} %bitcast.10, s32[6,1024]{1,0:T(8,128)S(1)} %get-tuple-element.55.local, f32[6,1024]{1,0:T(8,128)S(1)} %copy-done.1, f32[40,1024]{1,0:T(8,128)S(1)} %shard_map.117.part, f32[80,128]{1,0:T(8,128)S(1)} %collective-permute-done.9.a, ...), custom_call_target="tpu_custom_call" | custom-call | flops 5000000 | bytes 1000 | tf_op jit(solution)/shard_map/pallas_call | solution.py:644
  30.6 0.0 collective-permute-done.7.even_in
  30.6 0.0 collective-permute-done.8.odd_in
  30.6 1.6 %last_pair.1 = (f32[8,128]{1,0:T(8,128)}, f32[8,128]{1,0:T(8,128)}, f32[40,1024]{1,0:T(8,128)}) custom-call(s32[1]{0:T(128)} %bitcast.place_ref.place, s32[4,6,8,128]{3,2,1,0:T(8,128)S(1)} %get-tuple-element.37.index, f32[4,6,8,128]{3,2,1,0:T(8,128)S(1)} %get-tuple-element.38.weight, f32[4,8,128]{2,1,0:T(8,128)S(1)} %get-tuple-element.39.force, ...), custom_call_target="tpu_custom_call" | custom-call | flops 2500000 | bytes 1000 | tf_op jit(solution)/shard_map/last_pair/pallas_call | solution.py:658
Async XLA Ops:
  0.6 4.4 %copy-start = (f32[40,1024]{1,0:T(8,128)S(1)}, f32[40,1024]{1,0:T(8,128)}, u32[]{:S(2)}) copy-start(f32[40,1024]{1,0:T(8,128)} %tracer.7) | copy-start | bytes 491524
  0.6 4.4 %copy-start.1 = (f32[6,1024]{1,0:T(8,128)S(1)}, f32[6,1024]{1,0:T(8,128)}, u32[]{:S(2)}) copy-start(f32[6,1024]{1,0:T(8,128)} %weight.7) | copy-start | bytes 73732
  0.7 4.4 %copy-start.2 = (s32[6,1024]{1,0:T(8,128)S(1)}, s32[6,1024]{1,0:T(8,128)}, u32[]{:S(2)}) copy-start(s32[6,1024]{1,0:T(8,128)} %index.3) | copy-start | bytes 73732
  0.7 4.4 %copy-start.4 = (f32[1024]{0:T(1024)S(1)}, f32[1024]{0:T(1024)}, u32[]{:S(2)}) copy-start(f32[1024]{0:T(1024)} %param.13) | copy-start | bytes 12292
  0.7 4.4 %copy-start.5 = (f32[1024]{0:T(1024)S(1)}, f32[1024]{0:T(1024)}, u32[]{:S(2)}) copy-start(f32[1024]{0:T(1024)} %param.14) | copy-start | bytes 12292
  0.7 4.4 %copy-start.8 = (f32[40]{0:T(128)S(1)}, f32[40]{0:T(128)}, u32[]{:S(2)}) copy-start(f32[40]{0:T(128)} %profile.1) | copy-start | bytes 484
  2.6 2.5 %copy-start.3 = (s32[1024]{0:T(1024)S(1)}, s32[1024]{0:T(1024)}, u32[]{:S(2)}) copy-start(s32[1024]{0:T(1024)} %param.10) | copy-start | bytes 12292
  2.6 7.1 %collective-permute-start = (f32[208,128]{1,0:T(8,128)}, f32[208,128]{1,0:T(8,128)S(1)}, u32[]{:S(2)}, u32[]{:S(2)}) collective-permute-start(f32[208,128]{1,0:T(8,128)} %get-tuple-element.34), channel_id=1, source_target_pairs={{0,1},{1,0},{2,3},{3,2},{4,5},{5,4},{6,7},{7,6},{8,9},{9,8},{10,11... | collective-permute-start | bytes 319496 | tf_op jit(solution)/shard_map/ppermute | solution.py:614
  3.3 1.8 %copy-start.6 = (s32[1,4,2]{1,2,0:T(2,128)S(1)}, s32[1,4,2]{1,2,0:T(2,128)}, u32[]{:S(2)}) copy-start(s32[1,4,2]{1,2,0:T(2,128)} %param.15) | copy-start | bytes 100
  3.3 1.8 %copy-start.7 = (f32[40]{0:T(128)S(1)}, f32[40]{0:T(128)}, u32[]{:S(2)}) copy-start(f32[40]{0:T(128)} %thick.3) | copy-start | bytes 484
  3.3 6.3 %collective-permute-start.1 = (f32[208,128]{1,0:T(8,128)}, f32[208,128]{1,0:T(8,128)S(1)}, u32[]{:S(2)}, u32[]{:S(2)}) collective-permute-start(f32[208,128]{1,0:T(8,128)} %get-tuple-element.35), channel_id=1, source_target_pairs={{0,2},{1,3},{2,0},{3,1},{4,6},{5,7},{6,4},{7,5},{8,10},{9,11},{10,... | collective-permute-start | bytes 319496 | tf_op jit(solution)/shard_map/ppermute | solution.py:614
  4.5 5.1 %collective-permute-start.2 = (f32[128,128]{1,0:T(8,128)}, f32[128,128]{1,0:T(8,128)S(1)}, u32[]{:S(2)}, u32[]{:S(2)}) collective-permute-start(f32[128,128]{1,0:T(8,128)} %get-tuple-element.36), channel_id=1, source_target_pairs={{0,3},{1,2},{2,1},{3,0},{4,7},{5,6},{6,5},{7,4},{8,11},{9,10},{10,... | collective-permute-start | bytes 196616 | tf_op jit(solution)/shard_map/ppermute | solution.py:614
  9.7 3.8 %collective-permute-start.3 = (f32[152,128]{1,0:T(8,128)S(1)}, f32[152,128]{1,0:T(8,128)S(1)}, u32[]{:S(2)}, u32[]{:S(2)}) collective-permute-start(f32[152,128]{1,0:T(8,128)S(1)} %get-tuple-element.43), channel_id=1, source_target_pairs={{0,4},{1,5},{2,6},{3,7},{4,0},{5,1},{6,2},{7,3},{8,12},{9,13},{10,... | collective-permute-start | bytes 233480 | tf_op jit(solution)/shard_map/ppermute | solution.py:614
  11.0 4.1 %collective-permute-start.4 = (f32[152,128]{1,0:T(8,128)S(1)}, f32[152,128]{1,0:T(8,128)S(1)}, u32[]{:S(2)}, u32[]{:S(2)}) collective-permute-start(f32[152,128]{1,0:T(8,128)S(1)} %get-tuple-element.44), channel_id=1, source_target_pairs={{4,8},{5,9},{6,10},{7,11},{12,16},{13,17},{14,18},{15,19},{20,24},... | collective-permute-start | bytes 233480 | tf_op jit(solution)/shard_map/ppermute | solution.py:614
  16.5 5.8 %collective-permute-start.5 = (f32[48,128]{1,0:T(8,128)S(1)}, f32[48,128]{1,0:T(8,128)S(1)}, u32[]{:S(2)}, u32[]{:S(2)}) collective-permute-start(f32[48,128]{1,0:T(8,128)S(1)} %get-tuple-element.48), channel_id=1, source_target_pairs={{0,4},{1,5},{2,6},{3,7},{4,0},{5,1},{6,2},{7,3},{8,12},{9,13},{10,... | collective-permute-start | bytes 73736 | tf_op jit(solution)/shard_map/ppermute | solution.py:614
  16.9 5.4 %collective-permute-start.6 = (f32[48,128]{1,0:T(8,128)S(1)}, f32[48,128]{1,0:T(8,128)S(1)}, u32[]{:S(2)}, u32[]{:S(2)}) collective-permute-start(f32[48,128]{1,0:T(8,128)S(1)} %get-tuple-element.49), channel_id=1, source_target_pairs={{4,8},{5,9},{6,10},{7,11},{12,16},{13,17},{14,18},{15,19},{20,24},... | collective-permute-start | bytes 73736 | tf_op jit(solution)/shard_map/ppermute | solution.py:614
  16.9 11.9 %collective-permute-start.9 = (f32[80,128]{1,0:T(8,128)S(1)}, f32[80,128]{1,0:T(8,128)S(1)}, u32[]{:S(2)}, u32[]{:S(2)}) collective-permute-start(f32[80,128]{1,0:T(8,128)S(1)} %get-tuple-element.57), channel_id=1, source_target_pairs={{1,2},{3,4},{5,6},{7,8},{9,10},{11,12},{13,14},{15,16},{17,18},{19... | collective-permute-start | bytes 122888 | tf_op jit(solution)/shard_map/ppermute | solution.py:614
  20.2 8.5 %collective-permute-start.10 = (f32[80,128]{1,0:T(8,128)S(1)}, f32[80,128]{1,0:T(8,128)S(1)}, u32[]{:S(2)}, u32[]{:S(2)}) collective-permute-start(f32[80,128]{1,0:T(8,128)S(1)} %get-tuple-element.58), channel_id=1, source_target_pairs={{2,4},{3,5},{6,8},{7,9},{10,12},{11,13},{14,16},{15,17},{18,20},{1... | collective-permute-start | bytes 122888 | tf_op jit(solution)/shard_map/ppermute | solution.py:614
  23.6 7.0 %collective-permute-start.7 = (f32[48,128]{1,0:T(8,128)S(1)}, f32[48,128]{1,0:T(8,128)S(1)}, u32[]{:S(2)}, u32[]{:S(2)}) collective-permute-start(f32[48,128]{1,0:T(8,128)S(1)} %get-tuple-element.53), channel_id=1, source_target_pairs={{0,4},{1,5},{2,6},{3,7},{4,0},{5,1},{6,2},{7,3},{8,12},{9,13},{10,... | collective-permute-start | bytes 73736 | tf_op jit(solution)/shard_map/ppermute | solution.py:614
  25.5 5.1 %collective-permute-start.8 = (f32[48,128]{1,0:T(8,128)S(1)}, f32[48,128]{1,0:T(8,128)S(1)}, u32[]{:S(2)}, u32[]{:S(2)}) collective-permute-start(f32[48,128]{1,0:T(8,128)S(1)} %get-tuple-element.54), channel_id=1, source_target_pairs={{4,8},{5,9},{6,10},{7,11},{12,16},{13,17},{14,18},{15,19},{20,24},... | collective-permute-start | bytes 73736 | tf_op jit(solution)/shard_map/ppermute | solution.py:614
